TPU v7x, 128 devices: a whole 4x4x4 slice. The times are simulated.
128 devices in a mesh: inner: 4 (over x), fsdp: 32 (over z, y, core).
Axes of the slice: x: 4, y: 4, z: 4, core: 2. Of those that a mesh axis runs over, the one named last changes fastest.
Arguments:
- x_in: bfloat16 [16384, 2048], P(('inner', 'fsdp'))
- w_up: bfloat16 [2, 2048, 8192], P(None, ('inner', 'fsdp'))
- w_down: bfloat16 [2, 8192, 2048], P(None, ('inner', 'fsdp'))
- grad_out: bfloat16 [16384, 2048], P(('inner', 'fsdp'))
Outputs:
- output 1: bfloat16 [16384, 2048], P(('inner', 'fsdp'))
- output 2: bfloat16 [16384, 2048], P(('inner', 'fsdp'))
- output 3: float32 [2, 2048, 8192], P(None, ('inner', 'fsdp'))
- output 4: float32 [2, 8192, 2048], P(None, ('inner', 'fsdp'))
All inputs are finite; a program needn't handle non-finite values.
Results may differ from a plain program's by a relative error of at most 0.00497.
Values are sent between devices in bfloat16 or wider.
A program may use at most 1 GiB of HBM per device.

v0:
```python
import jax
import jax.numpy as jnp
from jax import lax
from jax.sharding import PartitionSpec as P


def gelu_parts(pre_act):
    norm_cdf = 0.5 * (1.0 + lax.erf(pre_act * (2.0 ** -0.5)))
    norm_pdf = jnp.exp(-0.5 * pre_act * pre_act) * ((2.0 * jnp.pi) ** -0.5)
    return pre_act * norm_cdf, norm_cdf + pre_act * norm_pdf


def contract(left, right, left_dim, right_dim):
    return lax.dot_general(left, right, (((left_dim,), (right_dim,)), ((), ())), preferred_element_type=jnp.float32)


def layer_forward(x_cur, up_mat, down_mat):
    pre_act = contract(x_cur, up_mat, 1, 0)
    post_act = gelu_parts(pre_act)[0].astype(jnp.bfloat16)
    return (x_cur.astype(jnp.float32) + contract(post_act, down_mat, 1, 0)).astype(jnp.bfloat16)


def layer_backward(x_cur, g_cur, up_mat, down_mat):
    pre_act = contract(x_cur, up_mat, 1, 0)
    post_full, gelu_slope = gelu_parts(pre_act)
    post_act = post_full.astype(jnp.bfloat16)
    d_pre = (contract(g_cur, down_mat, 1, 1) * gelu_slope).astype(jnp.bfloat16)
    g_next = (g_cur.astype(jnp.float32) + contract(d_pre, up_mat, 1, 1)).astype(jnp.bfloat16)
    grad_up = contract(x_cur, d_pre, 0, 0)
    grad_down = contract(post_act, g_cur, 0, 0)
    return g_next, grad_up, grad_down


def solution(mesh):
    fsdp_size = mesh.shape["fsdp"]
    all_axes = ("inner", "fsdp")
    tok_spec = P(all_axes, None)
    weight_spec = P(None, all_axes, None)

    def device_step(x_loc, up_loc, down_loc, g_loc):
        layers = up_loc.shape[0]
        kept_layers = layers // 2
        copy_up_rows = up_loc.shape[1] * fsdp_size
        copy_down_rows = down_loc.shape[1] * fsdp_size
        inner_idx = lax.axis_index("inner")
        x_cur = x_loc
        layer_inputs = []
        copies = {}
        for layer in range(layers):
            full_up = lax.all_gather(up_loc[layer], all_axes, axis=0, tiled=True)
            full_down = lax.all_gather(down_loc[layer], all_axes, axis=0, tiled=True)
            layer_inputs.append(x_cur)
            x_cur = layer_forward(x_cur, full_up, full_down)
            if layer >= layers - kept_layers:
                copies[layer] = (
                    lax.dynamic_slice_in_dim(full_up, inner_idx * copy_up_rows, copy_up_rows, axis=0),
                    lax.dynamic_slice_in_dim(full_down, inner_idx * copy_down_rows, copy_down_rows, axis=0))
        g_cur = g_loc
        grads_up = [None] * layers
        grads_down = [None] * layers
        for layer in reversed(range(layers)):
            if layer in copies:
                full_up = lax.all_gather(copies[layer][0], "inner", axis=0, tiled=True)
                full_down = lax.all_gather(copies[layer][1], "inner", axis=0, tiled=True)
            else:
                full_up = lax.all_gather(up_loc[layer], all_axes, axis=0, tiled=True)
                full_down = lax.all_gather(down_loc[layer], all_axes, axis=0, tiled=True)
            g_cur, grad_up, grad_down = layer_backward(layer_inputs[layer], g_cur, full_up, full_down)
            grads_up[layer] = lax.psum_scatter(grad_up, all_axes, scatter_dimension=0, tiled=True)
            grads_down[layer] = lax.psum_scatter(grad_down, all_axes, scatter_dimension=0, tiled=True)
        return x_cur, g_cur, jnp.stack(grads_up), jnp.stack(grads_down)

    return jax.shard_map(device_step, mesh=mesh, in_specs=(tok_spec, weight_spec, weight_spec, tok_spec), out_specs=(tok_spec, tok_spec, weight_spec, weight_spec), check_vma=False)
```

profile of v0, /device:TPU:1, one launch (start us, length us, event | category | flops | bytes accessed | tf_op | source)
XLA Modules:
  0.0 4087.4 jit_solution(12071790241140621998)
XLA Ops:
  7.2 0.0 all-gather.17.cloned.1.call-start
  7.2 1.9 fusion.81
  9.1 0.0 all-gather.17.cloned.1.call-update
  9.1 0.0 all-gather.19.cloned.1.call-start
  9.1 1.9 fusion.82
  11.0 0.0 all-gather.19.cloned.1.call-update
  11.0 0.0 all-gather.13.cloned.1.call-start
  11.1 0.7 all-gather.13.cloned.1.call-update
  11.8 0.0 all-gather.15.cloned.1.call-start
  11.8 0.5 all-gather.15.cloned.1.call-update
  12.3 0.0 all-gather.23.cloned.1.call-start
  12.4 109.1 %all-gather.17.cloned.1.call-done = bf16[1,2048,8192]{2,1,0:T(8,128)(2,1)} async-done(((bf16[1,16,8192]{2,1,0:T(8,128)(2,1)}), bf16[1,2048,8192]{2,1,0:T(8,128)(2,1)}) %all-gather.17.cloned.1.call-update) | async-done | bytes 33554448 | tf_op jit(solution)/shard_map/all_gather | solution.py:50
  121.5 7.6 constant_dynamic-slice_fusion
  129.1 0.0 all-gather.23.cloned.1.call-update
  129.1 0.0 all-gather.21.cloned.1.call-start
  129.1 101.6 %all-gather.19.cloned.1.call-done = bf16[1,8192,2048]{2,1,0:T(8,128)(2,1)} async-done(((bf16[1,64,2048]{2,1,0:T(8,128)(2,1)}), bf16[1,8192,2048]{2,1,0:T(8,128)(2,1)}) %all-gather.19.cloned.1.call-update) | async-done | bytes 33554448 | tf_op jit(solution)/shard_map/all_gather | solution.py:51
  230.7 8.3 constant_dynamic-slice_fusion.1
  239.0 0.0 copy-start.4
  239.0 0.0 all-gather.21.cloned.1.call-update
  239.0 0.0 reduce-scatter.15.cloned.1.call-start
  239.1 100.8 %all-gather.13.cloned.1.call-done = bf16[1,2048,8192]{2,1,0:T(8,128)(2,1)} async-done(((bf16[1,16,8192]{2,1,0:T(8,128)(2,1)}), bf16[1,2048,8192]{2,1,0:T(8,128)(2,1)}) %all-gather.13.cloned.1.call-update) | async-done | bytes 33554448 | tf_op jit(solution)/shard_map/all_gather | solution.py:50
  339.9 0.0 copy-done.4
  339.9 17.1 fusion.16
  357.0 92.0 %all-gather.15.cloned.1.call-done = bf16[1,8192,2048]{2,1,0:T(8,128)(2,1)} async-done(((bf16[1,64,2048]{2,1,0:T(8,128)(2,1)}), bf16[1,8192,2048]{2,1,0:T(8,128)(2,1)}) %all-gather.15.cloned.1.call-update) | async-done | bytes 33554448 | tf_op jit(solution)/shard_map/all_gather | solution.py:51
  449.0 16.5 fusion.70
  465.5 0.0 copy-start
  465.5 277.9 %all-gather.23.cloned.1.call-done = bf16[1,2048,8192]{2,1,0:T(8,128)(2,1)} async-done(((bf16[1,512,8192]{2,1,0:T(8,128)(2,1)}), bf16[1,2048,8192]{2,1,0:T(8,128)(2,1)}) %all-gather.23.cloned.1.call-update) | async-done | bytes 33554448 | tf_op jit(solution)/shard_map/all_gather | solution.py:63
  743.4 17.2 fusion.2
  760.7 279.5 %all-gather.21.cloned.1.call-done = bf16[1,8192,2048]{2,1,0:T(8,128)(2,1)} async-done(((bf16[1,2048,2048]{2,1,0:T(8,128)(2,1)}), bf16[1,8192,2048]{2,1,0:T(8,128)(2,1)}) %all-gather.21.cloned.1.call-update) | async-done | bytes 33554448 | tf_op jit(solution)/shard_map/all_gather | solution.py:64
  1040.2 18.0 fusion.27
  1058.2 0.0 copy-done
  1058.2 23.1 fusion.83
  1081.3 0.0 reduce-scatter.15.cloned.1.call-update
  1081.3 0.3 reduce-scatter.13.cloned.1.call-start
  1081.6 0.8 copy-done.6
  1082.4 16.8 fusion.59
  1099.1 17.1 fusion.30
  1116.2 0.0 copy-start.2
  1116.2 23.1 convolution_bitcast_fusion
  1139.4 0.0 copy-done.2
  1139.4 61.2 %copy.17 = f32[2048,8192]{1,0:T(8,128)} copy(f32[2048,8192]{0,1:T(8,128)} %convolution_bitcast_fusion) | data formatting | bytes 134217728
  1200.6 0.0 reduce-scatter.13.cloned.1.call-update
  1200.6 0.0 reduce-scatter.9.cloned.1.call-start
  1200.6 1.0 copy-done.5
  1201.6 25.4 fusion.80
  1227.0 0.0 reduce-scatter.9.cloned.1.call-update
  1227.0 0.3 reduce-scatter.11.cloned.1.call-start
  1227.3 0.7 copy-done.7
  1228.0 25.5 fusion.73
  1253.5 0.0 reduce-scatter.11.cloned.1.call-update
  1253.5 1.0 copy-done.1
  1254.5 24.7 fusion.65
  1279.3 0.0 copy-done.3
  1279.3 16.7 fusion.62
  1296.0 532.7 %reduce-scatter.15.cloned.1.call-done = f32[16,8192]{1,0:T(8,128)} async-done(((f32[2048,8192]{1,0:T(8,128)}), f32[16,8192]{1,0:T(8,128)}) %reduce-scatter.15.cloned.1.call-update) | async-done | bytes 524304
  1828.8 3.5 copy.20
  1832.3 2.8 copy.14
  1835.1 743.1 %reduce-scatter.13.cloned.1.call-done = f32[16,8192]{1,0:T(8,128)} async-done(((f32[2048,8192]{1,0:T(8,128)}), f32[16,8192]{1,0:T(8,128)}) %reduce-scatter.13.cloned.1.call-update) | async-done | bytes 524304
  2578.2 3.5 copy.18
  2581.7 2.8 copy.13
  2584.5 743.1 %reduce-scatter.9.cloned.1.call-done = f32[64,2048]{1,0:T(8,128)} async-done(((f32[8192,2048]{1,0:T(8,128)}), f32[64,2048]{1,0:T(8,128)}) %reduce-scatter.9.cloned.1.call-update) | async-done | bytes 524304 | tf_op jit(solution)/shard_map/reduce_scatter | solution.py:70
  3327.6 749.2 %reduce-scatter.11.cloned.1.call-done = f32[64,2048]{1,0:T(8,128)} async-done(((f32[8192,2048]{1,0:T(8,128)}), f32[64,2048]{1,0:T(8,128)}) %reduce-scatter.11.cloned.1.call-update) | async-done | bytes 524304 | tf_op jit(solution)/shard_map/reduce_scatter | solution.py:70
  4076.8 2.3 pad_maximum_fusion.1
  4079.1 1.0 pad_maximum_fusion
  (5 shorter events, 0.0 us)
Async XLA Ops:
  7.2 114.3 %all-gather.17.cloned.1.call-start = ((), (), s32[]{:S(2)}) async-start(), calls=%async_computation.8 | async-start | bytes 33816576 | tf_op jit(solution)/shard_map/all_gather | solution.py:50
  9.1 221.6 %all-gather.19.cloned.1.call-start = ((), (), s32[]{:S(2)}) async-start(), calls=%async_computation.9 | async-start | bytes 33816576 | tf_op jit(solution)/shard_map/all_gather | solution.py:51
  11.0 328.9 %all-gather.13.cloned.1.call-start = ((), (), s32[]{:S(2)}) async-start(), calls=%async_computation.6 | async-start | bytes 33816576 | tf_op jit(solution)/shard_map/all_gather | solution.py:50
  11.8 437.2 %all-gather.15.cloned.1.call-start = ((), (), s32[]{:S(2)}) async-start(), calls=%async_computation.7 | async-start | bytes 33816576 | tf_op jit(solution)/shard_map/all_gather | solution.py:51
  12.3 731.1 %all-gather.23.cloned.1.call-start = ((), (), s32[]{:S(2)}) async-start(), calls=%async_computation.11 | async-start | bytes 41943040 | tf_op jit(solution)/shard_map/all_gather | solution.py:63
  129.1 911.1 %all-gather.21.cloned.1.call-start = ((), (), s32[]{:S(2)}) async-start(), calls=%async_computation.10 | async-start | bytes 41943040 | tf_op jit(solution)/shard_map/all_gather | solution.py:64
  239.0 100.9 %copy-start.4 = (bf16[128,2048]{1,0:T(8,128)(2,1)S(1)}, bf16[128,2048]{1,0:T(8,128)(2,1)}, u32[]{:S(2)}) copy-start(bf16[128,2048]{1,0:T(8,128)(2,1)} %param.4) | copy-start | bytes 1572868
  239.0 1589.7 %reduce-scatter.15.cloned.1.call-start = ((), (), s32[]{:S(2)}) async-start(), calls=%async_computation.13 | async-start | bytes 67633152
  465.5 592.7 %copy-start = (bf16[128,2048]{1,0:T(8,128)(2,1)}, bf16[128,2048]{1,0:T(8,128)(2,1)S(1)}, u32[]{:S(2)}) copy-start(bf16[128,2048]{1,0:T(8,128)(2,1)S(1)} %fusion.70) | copy-start | bytes 1572868
  1081.3 1.0 copy-start.6
  1081.3 1496.8 %reduce-scatter.13.cloned.1.call-start = ((), (), s32[]{:S(2)}) async-start(), calls=%async_computation.12 | async-start | bytes 67633152
  1116.2 23.1 copy-start.2
  1200.6 1.0 copy-start.5
  1200.6 2127.0 %reduce-scatter.9.cloned.1.call-start = ((), (), s32[]{:S(2)}) async-start(), calls=%async_computation.4 | async-start | bytes 67633152 | tf_op jit(solution)/shard_map/reduce_scatter | solution.py:70
  1227.0 1.0 copy-start.7
  1227.0 2849.8 %reduce-scatter.11.cloned.1.call-start = ((), (), s32[]{:S(2)}) async-start(), calls=%async_computation.5 | async-start | bytes 67633152 | tf_op jit(solution)/shard_map/reduce_scatter | solution.py:70
  1253.5 1.0 copy-start.1
  1254.5 24.7 copy-start.3
Sparse Core Ops, SparseCore 0:
  11.5 109.8 all-gather.16
  125.0 105.6 all-gather.18
  234.3 105.6 all-gather.12
  343.3 105.6 all-gather.14
  450.5 292.8 all-gather.22
  744.9 295.1 all-gather.20
  1081.5 747.2 reduce-scatter.14
  1831.2 746.9 reduce-scatter.12
  2580.6 746.9 reduce-scatter.8
  3329.8 746.9 reduce-scatter.10
where the time goes:
time: 4100 us; the launch traced here: 4090 us
  waiting for transfers between devices  3730 us (91%)
  matrix products  241 us (6%)
  local copies, waits for them, and re-layouts  96.9 us (2%)
    reduce_scatter x2, waiting for transfers between devices, device_step(): lax.psum_scatter(grad_down, all_axes, scatter_dimension=0, tiled=True)  1490 us
    unnamed x12, waiting for transfers between devices  1280 us
    all_gather x1, waiting for transfers between devices, device_step(): full_down = lax.all_gather(copies[layer][1], 'inner', axis=0, tiled=True)  280 us
    all_gather x1, waiting for transfers between devices, device_step(): full_up = lax.all_gather(copies[layer][0], 'inner', axis=0, tiled=True)  278 us
    dot_general x11, matrix products, contract(): lax.dot_general(left, right, (((left_dim,), (right_dim,)), ((), ())), pre...  218 us
    all_gather x2, waiting for transfers between devices, device_step(): full_up = lax.all_gather(up_loc[layer], all_axes, axis=0, tiled=True)  210 us
    all_gather x2, waiting for transfers between devices, device_step(): full_down = lax.all_gather(down_loc[layer], all_axes, axis=0, tiled=True)  194 us
  transfers between devices with their start and end apart: 10, of which 10 were waited for; matrix products, arithmetic and copies ran while one was open for 7% of the time, Pallas kernels for 0%

commit v1 on v0

v1 whole, which is shorter than its diff:
```python
import functools

import jax
import jax.numpy as jnp
import numpy as np
from jax import lax
from jax.experimental import pallas as pl
from jax.experimental.pallas import tpu as pltpu
from jax.sharding import Mesh, PartitionSpec as P

MESH_ID = pl.DeviceIdType.MESH
ALL = ("x", "z", "y", "c")
F32, BF16 = jnp.float32, jnp.bfloat16
RING, CORES, ARRIVALS = 4, 2, 6
OWN, NXT, OPP, PRV = range(RING)
X0, X1, G1, G0 = range(RING)
HALVES = (0, 1)
N_SEM = 224
N_LOCAL = 112


def gelu_parts(pre_act):
    norm_cdf = 0.5 * (1.0 + lax.erf(pre_act * (2.0 ** -0.5)))
    norm_pdf = jnp.exp(-0.5 * pre_act * pre_act) * ((2.0 * jnp.pi) ** -0.5)
    return pre_act * norm_cdf, norm_cdf + pre_act * norm_pdf


def loop(n, body, init):
    return lax.fori_loop(0, n, body, init)


def dot_nn(left, right):
    return lax.dot_general(left, right, (((1,), (0,)), ((), ())), preferred_element_type=F32)


def dot_nt(left, right):
    return lax.dot_general(left, right, (((1,), (1,)), ((), ())), preferred_element_type=F32)


def dot_tn(left, right):
    return lax.dot_general(left, right, (((0,), (0,)), ((), ())), preferred_element_type=F32)


def kernel(dims, x_in, wu_in, wd_in, g_in,
           y_out, gi_out, gu_out, gd_out,
           xh0, gh1, wuh, wdh, sh0, ah, ra1, rb1, ra2, rb2, uh,
           U, W, XV, GV1, GV0, SV, AV, DV, GPA, GPB, PP, DR, XR, RES, STA, STB,
           ss, rs, ls, credit):
    D, K, TB, UR, DR_ROWS = dims
    HB = TB // 2
    x, z, y, c = (lax.axis_index(a) for a in ALL)
    cp = 1 - c
    S2 = 2 * DR_ROWS
    XD = D // 4
    ZD = D // 16

    def dev(dx=0, dz=0, dy=0, dc=0):
        wrap = lambda v, d, n: v if d == 0 else lax.rem(v + (d % n), n)
        return (wrap(x, dx, 4), wrap(z, dz, 4), wrap(y, dy, 4), wrap(c, dc, 2))

    partner = dev(dc=1)
    rings = {"x": (x, dev(dx=1), dev(dx=-1)), "z": (z, dev(dz=1), dev(dz=-1)), "y": (y, dev(dy=1), dev(dy=-1))}
    off = lambda v, d: v if d == 0 else lax.rem(v + d, 4)

    count = [0]

    def rcopy(src, dst, to):
        k = count[0]
        count[0] += 1
        return pltpu.make_async_remote_copy(src_ref=src, dst_ref=dst, send_sem=ss.at[k], recv_sem=rs.at[k],
                                            device_id=to, device_id_type=MESH_ID)

    lcount = [0]

    def lcopy(src, dst):
        k = lcount[0]
        lcount[0] += 1
        return pltpu.make_async_copy(src, dst, ls.at[k])

    def mo(v, m):
        return pl.multiple_of(v, m)

    class Gather4:
        def __init__(self, axis, src, dst):
            i, right, left = rings[axis]
            lft, rgt = off(i, 3), off(i, 1)
            self.d = [rcopy(src(0), dst(i, 0), right), rcopy(src(1), dst(i, 1), right),
                      rcopy(src(0), dst(i, 0), left), rcopy(src(1), dst(i, 1), left),
                      rcopy(dst(lft, 0), dst(lft, 0), right), rcopy(dst(rgt, 1), dst(rgt, 1), left)]

        def start(self):
            for k in (0, 3, 1, 2):
                self.d[k].start()

        def forward(self):
            self.d[0].wait_recv()
            self.d[4].start()
            self.d[3].wait_recv()
            self.d[5].start()

        def finish(self):
            for k in (1, 2, 4, 5):
                self.d[k].wait_recv()

        def drain(self):
            for d in self.d:
                d.wait_send()

    class Gather8:
        def __init__(self, src, dst):
            self.ring = Gather4("x", src, lambda b, h: dst(b, c, h))
            lft, rgt, opp = off(x, PRV), off(x, NXT), off(x, OPP)
            blocks = [(lft, 0), (rgt, 1), (lft, 1), (rgt, 0), (opp, 0), (opp, 1)]
            self.own = [rcopy(src(h), dst(x, c, h), partner) for h in HALVES]
            self.push = [rcopy(dst(b, c, h), dst(b, c, h), partner) for b, h in blocks]

        def start(self):
            self.ring.start()
            for d in self.own:
                d.start()

        def forward(self):
            self.ring.forward()
            self.push[0].start()
            self.push[1].start()

        def sides(self):
            self.ring.d[1].wait_recv()
            self.push[2].start()
            self.ring.d[2].wait_recv()
            self.push[3].start()

        def last(self):
            self.ring.d[4].wait_recv()
            self.push[4].start()
            self.ring.d[5].wait_recv()
            self.push[5].start()

        def wait_own(self):
            for d in self.own:
                d.wait_recv()

        def wait_push(self, ks):
            for k in ks:
                self.push[k].wait_recv()

        def drain(self):
            self.ring.drain()
            for d in self.own + self.push:
                d.wait_send()

    def add_rows(dst, srcs, rows, step):
        def body(r, carry):
            sl = pl.ds(mo(r * step, step), step)
            if len(dst.shape) == 3:
                for q in range(dst.shape[0]):
                    acc = dst[q, sl, :]
                    for s in srcs:
                        acc = acc + s[q, sl, :]
                    dst[q, sl, :] = acc
            else:
                acc = dst[sl, :]
                for s in srcs:
                    acc = acc + s[sl, :]
                dst[sl, :] = acc
            return carry
        loop(rows // step, body, None)

    barrier = pltpu.get_barrier_semaphore()
    group = [(dx, dc) for dx in range(RING) for dc in range(2) if (dx, dc) != (0, 0)]
    peers = [dev(dx=dx, dc=dc) for dx, dc in group] + [rings["z"][1], rings["z"][2], rings["y"][1], rings["y"][2]]
    for p in peers:
        pl.semaphore_signal(barrier, inc=1, device_id=p, device_id_type=MESH_ID)

    load_u = [[lcopy(wu_in.at[l, :, pl.ds(b * (4 * K // 2), 4 * K // 2)],
                     RES.at[G0, pl.ds((l * 4 + b) * UR, UR), :]) for b in range(RING)] for l in HALVES]
    for l in HALVES:
        for cpy in load_u[l]:
            cpy.start()
    load_d = [lcopy(wd_in.at[l], RES.at[X1, pl.ds(l * DR_ROWS, DR_ROWS), :]) for l in HALVES]
    for cpy in load_d:
        cpy.start()
    load_x = lcopy(x_in, RES.at[X0])
    load_g = lcopy(g_in, RES.at[G1])
    load_x.start()
    load_g.start()
    pl.semaphore_wait(barrier, len(peers))

    half = lambda h: pl.ds(h * HB, HB)
    gx0 = Gather8(lambda h: x_in.at[half(h)], lambda b, k, h: xh0.at[b, k, half(h)])
    gg1 = Gather8(lambda h: g_in.at[half(h)], lambda b, k, h: gh1.at[b, k, half(h)])
    gx0.start()

    hr = DR_ROWS // 2
    gd1 = [Gather4("z", (lambda l: lambda h: wd_in.at[l, pl.ds(h * hr, hr)])(l),
                   (lambda l: lambda b, h: wdh.at[l, y, b, pl.ds(h * hr, hr)])(l)) for l in HALVES]
    gd2 = [Gather4("y", (lambda l: lambda h: wdh.at[l, y, pl.ds(2 * h, 2)])(l),
                   (lambda l: lambda b, h: wdh.at[l, b, pl.ds(2 * h, 2)])(l)) for l in HALVES]
    gu1 = [Gather4("y", (lambda l: lambda h: wuh.at[l, pl.ds(2 * h, 2), z, y])(l),
                   (lambda l: lambda b, h: wuh.at[l, pl.ds(2 * h, 2), z, b])(l)) for l in HALVES]
    gu2 = [Gather4("z", (lambda l: lambda h: wuh.at[l, pl.ds(2 * h, 2), z])(l),
                   (lambda l: lambda b, h: wuh.at[l, pl.ds(2 * h, 2), b])(l)) for l in HALVES]
    gd1[0].start()

    lane = lax.broadcasted_iota(jnp.int32, (UR, S2), 1)
    low = lane < DR_ROWS

    def shuffle_up(l):
        for b in range(RING):
            rows = pl.ds((l * 4 + b) * UR, UR)
            for yy in range(RING):
                for m in HALVES:
                    s0 = RES[G0, rows, pl.ds((2 * m * 4 + yy) * S2, S2)].astype(F32)
                    s1 = RES[G0, rows, pl.ds(((2 * m + 1) * 4 + yy) * S2, S2)].astype(F32)
                    cols = pl.ds((yy * 2 + m) * S2, S2)
                    t0 = jnp.where(low, s0, pltpu.roll(s1, DR_ROWS, 1))
                    t1 = jnp.where(low, pltpu.roll(s0, DR_ROWS, 1), s1)
                    AV[l, pl.ds((b * 2 + 0) * UR, UR), cols] = t0.astype(BF16)
                    AV[l, pl.ds((b * 2 + 1) * UR, UR), cols] = t1.astype(BF16)

    a2a = [[], []]
    own_u = []
    for l in HALVES:
        for cpy in load_u[l]:
            cpy.wait()
        shuffle_up(l)
        for dx, dc in group:
            tx, tc = off(x, dx), (c if dc == 0 else cp)
            src = AV.at[l, pl.ds(mo((tx * 2 + tc) * UR, UR), UR), :]
            dst = wuh.at[l, x, z, y, pl.ds(mo(c * UR, UR), UR), :]
            d = rcopy(src, dst, dev(dx=dx, dc=dc))
            d.start()
            a2a[l].append(d)
        cpy = lcopy(AV.at[l, pl.ds(mo((x * 2 + c) * UR, UR), UR), :], wuh.at[l, x, z, y, pl.ds(mo(c * UR, UR), UR), :])
        cpy.start()
        own_u.append(cpy)
    own_d = []
    for l in HALVES:
        load_d[l].wait()
        cpy = lcopy(RES.at[X1, pl.ds(l * DR_ROWS, DR_ROWS), :], wdh.at[l, y, z])
        cpy.start()
        own_d.append(cpy)
    load_x.wait()
    load_g.wait()
    own_x = lcopy(RES.at[X0], xh0.at[x, c])
    own_x.start()
    own_g = lcopy(RES.at[G1], gh1.at[x, c])
    own_g.start()

    for d in a2a[0]:
        d.wait_recv()
    own_u[0].wait()
    gu1[0].start()
    gd1[0].forward()
    gx0.forward()
    gu1[0].forward()
    gd1[0].finish()
    own_d[0].wait()
    gd2[0].start()
    gu1[0].finish()
    gu2[0].start()
    gx0.sides()
    gg1.start()
    gx0.last()
    gx0.wait_own()
    gx0.wait_push(range(6))
    own_x.wait()
    load_xv = lcopy(xh0, XV)
    load_xv.start()
    gu2[0].forward()
    gd2[0].forward()
    gd1[1].start()
    for d in a2a[1]:
        d.wait_recv()
    own_u[1].wait()
    gu1[1].start()
    gg1.forward()
    gg1.sides()
    gg1.last()
    gu2[0].finish()
    load_w0u = lcopy(wuh.at[0], U)
    load_w0u.start()
    gd2[0].finish()
    load_w0d = lcopy(wdh.at[0], W)
    load_w0d.start()
    for l in HALVES:
        for d in a2a[l]:
            d.wait_send()
    load_xv.wait()
    load_w0u.wait()

    T2 = 2 * TB
    ND = D // 4
    NK = K // 4

    def up_tile(t, n):
        cols = pl.ds(mo(n * NK, NK), NK)
        return dot_nn(XV[t].reshape(T2, D), U[:, :, :, :, cols].reshape(D, NK)), cols

    def hidden0(t):
        def body(n, carry):
            pre, cols = up_tile(t, n)
            act, slope = gelu_parts(pre)
            AV[t, :, cols] = act.astype(BF16)
            SV[t, :, cols] = slope
            return carry
        loop(K // NK, body, None)

    def hidden1(t):
        def body(n, carry):
            pre, cols = up_tile(t, n)
            act, slope = gelu_parts(pre)
            AV[t, :, cols] = act.astype(BF16)
            DV[t, :, cols] = (SV[t, :, cols] * slope).astype(BF16)
            return carry
        loop(K // NK, body, None)

    def dact(gv, t, n):
        return dot_nt(gv[t].reshape(T2, D), W[n].reshape(NK, D))

    def dact1(t):
        def body(n, carry):
            SV[t, :, pl.ds(mo(n * NK, NK), NK)] = dact(GV1, t, n)
            return carry
        loop(RING, body, None)

    def dact0(t):
        def body(n, carry):
            cols = pl.ds(mo(n * NK, NK), NK)
            DV[t, :, cols] = (dact(GV0, t, n) * SV[t, :, cols]).astype(BF16)
            return carry
        loop(RING, body, None)

    def down_part(j):
        t = off(x, j)

        def body(n, carry):
            cols = pl.ds(mo(n * ND, ND), ND)
            PP[j, :, :, cols] = dot_nn(AV[t], W[:, :, :, cols].reshape(K, ND)).reshape(2, TB, ND)
            return carry
        loop(RING, body, None)

    def dx_part(j):
        t = off(x, j)

        def body(n, carry):
            cols = pl.ds(mo(n * ND, ND), ND)
            PP[j, :, :, cols] = dot_nt(DV[t], U[n].reshape(ND, K)).reshape(2, TB, ND)
            return carry
        loop(RING, body, None)

    class Reduce8:
        def __init__(self, part, index):
            self.part, self.index = part, index
            _, right, left = rings["x"]
            self.right, self.left = right, left
            self.pair = [rcopy(PP.at[j, cp], DR.at[j], partner) for j in range(RING)]
            self.m = [rcopy(PP.at[OPP, c, half(0)], XR.at[0], right), rcopy(PP.at[OPP, c, half(1)], XR.at[1], left),
                      rcopy(PP.at[NXT, c, half(1)], XR.at[2], right), rcopy(PP.at[PRV, c, half(0)], XR.at[3], left),
                      rcopy(PP.at[NXT, c, half(0)], XR.at[4], right), rcopy(PP.at[PRV, c, half(1)], XR.at[5], left)]

        def credits(self):
            if self.index:
                for k in range(3):
                    pl.semaphore_wait(credit.at[k], 1)

        def compute(self, j):
            self.part(j)
            self.pair[j].start()

        def combine(self, j):
            self.pair[j].wait_recv()
            add_rows(PP.at[j, c], [DR.at[j]], TB, min(TB, 16))

        def opposite(self):
            self.combine(OPP)
            self.m[0].start()
            self.m[1].start()

        def sides(self, j):
            self.combine(j)
            self.m[2 if j == NXT else 3].start()

        def relay(self):
            self.m[0].wait_recv()
            add_rows(PP.at[NXT, c, half(0)], [XR.at[0]], HB, min(HB, 16))
            self.m[4].start()
            self.m[1].wait_recv()
            add_rows(PP.at[PRV, c, half(1)], [XR.at[1]], HB, min(HB, 16))
            self.m[5].start()

        def finish(self, res, outs):
            for k in (2, 3, 4, 5):
                self.m[k].wait_recv()
            step = min(HB, 16)
            for h, (kl, kr) in enumerate(((4, 3), (2, 5))):
                def body(r, carry):
                    lo = pl.ds(mo(r * step, step), step)
                    sl = pl.ds(mo(h * HB + r * step, step), step)
                    tot = PP[OWN, c, sl, :] + (XR[kl, lo, :] + XR[kr, lo, :])
                    val = (res[sl, :].astype(F32) + tot).astype(BF16)
                    for o in outs:
                        o[sl, :] = val
                    return carry
                loop(HB // step, body, None)
            for d in self.pair + self.m:
                d.wait_send()
            if self.index < 3:
                pl.semaphore_signal(credit.at[0], inc=1, device_id=self.right, device_id_type=MESH_ID)
                pl.semaphore_signal(credit.at[1], inc=1, device_id=self.left, device_id_type=MESH_ID)
                pl.semaphore_signal(credit.at[2], inc=1, device_id=partner, device_id_type=MESH_ID)

    def grad_a(j):
        t = off(z, j)
        for h in HALVES:
            lo = [pl.ds(mo((2 * h + q) * XD + t * ZD, ZD), ZD) for q in HALVES]
            lhs = jnp.concatenate([XV[:, :, :, s].reshape(8 * TB, ZD) for s in lo], axis=1)

            def body(n, carry):
                cols = pl.ds(mo(n * NK, NK), NK)
                out = dot_tn(lhs, DV[:, :, cols].reshape(8 * TB, NK))
                GPA[j, h, :, :, cols] = out.reshape(2, ZD, NK)
                return carry
            loop(K // NK, body, None)

    def grad_b(gv, j):
        t = off(y, j)
        cols_l = pl.ds(mo(t * NK, NK), NK)

        def body(n, carry):
            cols = pl.ds(mo(n * ND, ND), ND)
            out = dot_tn(AV[:, :, cols_l].reshape(8 * TB, NK), gv[:, :, :, cols].reshape(8 * TB, ND))
            GPB[j, :, :, cols] = out.reshape(2, NK // 2, ND)
            return carry
        loop(RING, body, None)

    class Reduce4:
        def __init__(self, axis, part, recv, rows, step):
            _, right, left = rings[axis]
            self.part, self.recv, self.rows, self.step = part, recv, rows, step
            self.m = [rcopy(part(OPP, 0), recv(0), right), rcopy(part(OPP, 1), recv(1), left),
                      rcopy(part(NXT, 1), recv(2), right), rcopy(part(PRV, 0), recv(3), left),
                      rcopy(part(NXT, 0), recv(4), right), rcopy(part(PRV, 1), recv(5), left)]

        def opposite(self):
            self.m[0].start()
            self.m[1].start()

        def sides(self, j):
            self.m[2 if j == NXT else 3].start()

        def relay(self, stage):
            loads = [lcopy(self.recv(0), stage(0)), lcopy(self.recv(1), stage(1))]
            for k in range(2):
                self.m[k].wait_send()
                self.m[k].wait_recv()
                loads[k].start()
            loads[0].wait()
            add_rows(self.part(NXT, 0), [stage(0)], self.rows, self.step)
            self.m[4].start()
            loads[1].wait()
            add_rows(self.part(PRV, 1), [stage(1)], self.rows, self.step)
            self.m[5].start()

        def finish(self, stages):
            for k in (2, 3, 4, 5):
                self.m[k].wait_send()
            for h, (kl, kr) in enumerate(((4, 3), (2, 5))):
                st = stages(h)
                loads = [lcopy(self.recv(kl), st[0]), lcopy(self.recv(kr), st[1])]
                self.m[kl].wait_recv()
                loads[0].start()
                self.m[kr].wait_recv()
                loads[1].start()
                loads[0].wait()
                loads[1].wait()
                add_rows(self.part(0, h), st, self.rows, self.step)

    hq = DR_ROWS // 2

    def make_reduce(l):
        a1 = Reduce4("z", lambda j, h: GPA.at[j, h], lambda k: ra1.at[l, k], ZD, min(ZD, 16))
        b1 = Reduce4("y", lambda j, h: GPB.at[j, h], lambda k: rb1.at[l, k], NK // 2, min(NK // 2, 16))

        def part_a2(j, h):
            return GPA.at[OWN, h, :, pl.ds(mo(off(y, j) * 2 * UR, 2 * UR), 2 * UR), :]

        def part_b2(j, h):
            t = off(z, j)
            return GPB.at[OWN, t // 2, pl.ds(mo(lax.rem(t, 2) * DR_ROWS + h * hq, hq), hq), :]
        a2 = Reduce4("y", part_a2, lambda k: ra2.at[l, k], 2 * UR, min(2 * UR, 16))
        b2 = Reduce4("z", part_b2, lambda k: rb2.at[l, k], hq, min(hq, 16))
        return a1, b1, a2, b2

    def grads_phase2_start(a2, b2):
        for r in (a2, b2):
            r.opposite()
            r.sides(NXT)
            r.sides(PRV)

    st_a = lambda k: STA.at[k]
    st_b = lambda k: STB.at[k]

    def grads_out_start(l):
        sends = []
        for dx, dc in group:
            tx, tc = off(x, dx), (c if dc == 0 else cp)
            src = GPA.at[OWN, tx // 2, lax.rem(tx, 2), pl.ds(mo(y * 2 * UR + tc * UR, UR), UR), :]
            d = rcopy(src, uh.at[l, x, pl.ds(mo(c * UR, UR), UR), :], dev(dx=dx, dc=dc))
            d.start()
            sends.append(d)
        own = lcopy(GPA.at[OWN, x // 2, lax.rem(x, 2), pl.ds(mo(y * 2 * UR + c * UR, UR), UR), :],
                    uh.at[l, x, pl.ds(mo(c * UR, UR), UR), :])
        own.start()
        outs = [lcopy(GPB.at[OWN, z // 2, pl.ds(mo(lax.rem(z, 2) * DR_ROWS + h * hq, hq), hq), :],
                      gd_out.at[l, pl.ds(h * hq, hq), :]) for h in HALVES]
        for o in outs:
            o.start()
        return sends, own, outs

    def grads_out_finish(l, state):
        sends, own, outs = state
        for d in sends:
            d.wait_recv()
        own.wait()
        loads = [lcopy(uh.at[l, b], STA.at[b // 2, b % 2]) for b in range(RING)]
        for ld in loads:
            ld.start()
        writes = []
        for b in range(RING):
            loads[b].wait()
            rows = pl.ds((b % 2) * UR, UR)
            for yy in range(RING):
                for m in HALVES:
                    cols = pl.ds((yy * 2 + m) * S2, S2)
                    t0 = STA[b // 2, b % 2, 0:UR, cols]
                    t1 = STA[b // 2, b % 2, UR:2 * UR, cols]
                    STB[b // 2, rows, pl.ds((2 * m * 4 + yy) * S2, S2)] = jnp.where(low, t0, pltpu.roll(t1, DR_ROWS, 1))
                    STB[b // 2, rows, pl.ds(((2 * m + 1) * 4 + yy) * S2, S2)] = jnp.where(low, pltpu.roll(t0, DR_ROWS, 1), t1)
            wr = lcopy(STB.at[b // 2, rows, :], gu_out.at[l, :, pl.ds(b * 16 * S2, 16 * S2)])
            wr.start()
            writes.append(wr)
        for wr in writes + outs:
            wr.wait()
        for d in sends:
            d.wait_send()

    def each_chip(fn):
        def body(t, carry):
            fn(t)
            return carry
        loop(RING, body, None)

    each_chip(hidden0)
    save_s = lcopy(SV, sh0)
    save_s.start()
    save_a0 = lcopy(AV, ah.at[0])
    save_a0.start()
    load_w0d.wait()

    r = Reduce8(down_part, 0)
    r.credits()
    r.compute(OPP)
    r.compute(NXT)
    r.opposite()
    r.compute(PRV)
    r.sides(NXT)
    r.compute(OWN)
    r.sides(PRV)
    gd1[1].forward()
    gu1[1].forward()
    gd1[1].finish()
    own_d[1].wait()
    gd2[1].start()
    gu1[1].finish()
    gu2[1].start()
    r.relay()
    r.combine(OWN)
    gg1.wait_own()
    gg1.wait_push(range(6))
    own_g.wait()
    load_gv = lcopy(gh1, GV1)
    load_gv.start()
    gu2[1].forward()
    gd2[1].forward()
    load_gv.wait()
    gx1 = Gather8(lambda h: RES.at[X1, half(h)], lambda b, k, h: XV.at[b, k, half(h)])
    r.finish(RES.at[X0], [RES.at[X1], XV.at[x, c]])
    gx1.start()
    gu2[1].finish()
    load_w1u = lcopy(wuh.at[1], U)
    load_w1u.start()
    gd2[1].finish()
    load_w1d = lcopy(wdh.at[1], W)
    load_w1d.start()
    gx1.forward()
    save_s.wait()
    load_w1d.wait()
    dact1(off(x, OWN))
    gx1.sides()
    dact1(off(x, NXT))
    dact1(off(x, PRV))
    load_w1u.wait()
    save_a0.wait()
    gx1.wait_own()
    hidden1(off(x, OWN))
    gx1.last()
    dact1(off(x, OPP))
    load_w0d_again = lcopy(wdh.at[0], W)
    load_w0d_again.start()
    gx1.wait_push((0, 2))
    hidden1(off(x, PRV))
    gx1.wait_push((1, 3))
    hidden1(off(x, NXT))
    gx1.wait_push((4, 5))
    hidden1(off(x, OPP))
    load_s0 = lcopy(sh0, SV)
    load_s0.start()
    save_a1 = lcopy(AV, ah.at[1])
    save_a1.start()

    a1, b1, a2, b2 = make_reduce(1)
    r = Reduce8(dx_part, 1)
    r.credits()
    r.compute(OPP)
    r.compute(NXT)
    r.opposite()
    r.compute(PRV)
    r.sides(NXT)
    r.sides(PRV)
    grad_b(GV1, OPP)
    b1.opposite()
    grad_a(OPP)
    a1.opposite()
    r.compute(OWN)
    load_w0u_again = lcopy(wuh.at[0], U)
    load_w0u_again.start()
    grad_b(GV1, NXT)
    b1.sides(NXT)
    grad_b(GV1, PRV)
    b1.sides(PRV)
    grad_a(NXT)
    a1.sides(NXT)
    grad_a(PRV)
    a1.sides(PRV)
    r.relay()
    r.combine(OWN)
    grad_b(GV1, OWN)
    save_a1.wait()
    load_a0 = lcopy(ah.at[0], AV)
    load_a0.start()
    gx1.drain()
    grad_a(OWN)
    load_x0 = lcopy(xh0, XV)
    load_x0.start()
    b1.relay(lambda k: GPB.at[OPP, k])
    a1.relay(lambda k: GPA.at[OPP, k])
    gg0 = Gather8(lambda h: RES.at[G0, half(h)], lambda b, k, h: GV0.at[b, k, half(h)])
    r.finish(RES.at[G1], [RES.at[G0], GV0.at[x, c]])
    gg0.start()
    load_w0d_again.wait()
    load_s0.wait()
    gg0.forward()
    gg0.wait_own()
    dact0(off(x, OWN))
    gg0.sides()
    gg0.last()
    gg0.wait_push((0, 2))
    dact0(off(x, PRV))
    gg0.wait_push((1, 3))
    dact0(off(x, NXT))
    gg0.wait_push((4, 5))
    dact0(off(x, OPP))
    load_w1d_again = lcopy(wdh.at[1], W)
    load_w1d_again.start()

    load_w0u_again.wait()
    r = Reduce8(dx_part, 2)
    r.credits()
    r.compute(OPP)
    r.compute(NXT)
    r.opposite()
    r.compute(PRV)
    r.sides(NXT)
    r.sides(PRV)
    r.compute(OWN)
    b1.finish(lambda h: [GPB.at[NXT, h], GPB.at[PRV, h]])
    a1.finish(lambda h: [GPA.at[NXT, h], GPA.at[PRV, h]])
    grads_phase2_start(a2, b2)
    load_a0.wait()
    a1n, b1n, a2n, b2n = make_reduce(0)
    grad_b(GV0, OPP)
    b1n.opposite()
    load_x0.wait()
    grad_a(OPP)
    a1n.opposite()
    r.relay()
    r.combine(OWN)
    b2.relay(st_b)
    a2.relay(st_a)
    grad_b(GV0, NXT)
    b1n.sides(NXT)
    grad_b(GV0, PRV)
    b1n.sides(PRV)
    grad_a(NXT)
    a1n.sides(NXT)
    grad_a(PRV)
    a1n.sides(PRV)
    b2.finish(lambda h: [STB.at[0], STB.at[1]])
    a2.finish(lambda h: [STA.at[0], STA.at[1]])
    state1 = grads_out_start(1)
    r.finish(RES.at[G0], [RES.at[X0]])
    write_gi = lcopy(RES.at[X0], gi_out)
    write_gi.start()
    grads_out_finish(1, state1)
    grad_b(GV0, OWN)
    load_a1 = lcopy(ah.at[1], AV)
    load_a1.start()
    grad_a(OWN)
    load_a1.wait()
    load_w1d_again.wait()
    r = Reduce8(down_part, 3)
    r.credits()
    r.compute(OPP)
    r.compute(NXT)
    r.opposite()
    r.compute(PRV)
    r.sides(NXT)
    r.compute(OWN)
    r.sides(PRV)
    b1n.relay(lambda k: GPB.at[OPP, k])
    a1n.relay(lambda k: GPA.at[OPP, k])
    r.relay()
    r.combine(OWN)
    r.finish(RES.at[X1], [RES.at[G1]])
    write_y = lcopy(RES.at[G1], y_out)
    write_y.start()
    b1n.finish(lambda h: [GPB.at[NXT, h], GPB.at[PRV, h]])
    a1n.finish(lambda h: [GPA.at[NXT, h], GPA.at[PRV, h]])
    grads_phase2_start(a2n, b2n)
    b2n.relay(st_b)
    a2n.relay(st_a)
    b2n.finish(lambda h: [STB.at[0], STB.at[1]])
    a2n.finish(lambda h: [STA.at[0], STA.at[1]])
    state0 = grads_out_start(0)
    grads_out_finish(0, state0)
    write_gi.wait()
    write_y.wait()
    for g in gd1 + gd2 + gu1 + gu2 + [gx0, gg1, gg0]:
        g.drain()
    assert count[0] <= N_SEM and lcount[0] <= N_LOCAL


def solution(mesh, interpret=None):
    fine = Mesh(np.asarray(mesh.devices).reshape(4, 4, 4, 2), ALL)
    tok_spec = P(ALL, None)
    weight_spec = P(None, ALL, None)

    def device_step(x_loc, up_loc, down_loc, g_loc):
        layers, ur, ff = up_loc.shape
        dr, dm = down_loc.shape[1:]
        tb = x_loc.shape[0]
        k = ff // 8
        zd = dm // 16
        nk = k // 4
        hbm = lambda shape, dt: jax.ShapeDtypeStruct(shape, dt)
        outs = [
            hbm((tb, dm), BF16), hbm((tb, dm), BF16), hbm((layers, ur, ff), F32), hbm((layers, dr, dm), F32),
            hbm((RING, CORES, tb, dm), BF16), hbm((RING, CORES, tb, dm), BF16),
            hbm((layers, RING, RING, RING, 2 * ur, k), BF16),
            hbm((layers, RING, RING, dr, dm), BF16),
            hbm((RING, 2 * tb, k), F32), hbm((layers, 4, 2 * tb, k), BF16),
            hbm((layers, ARRIVALS, CORES, zd, k), F32), hbm((layers, ARRIVALS, nk // 2, dm), F32),
            hbm((layers, ARRIVALS, CORES, 2 * ur, k), F32), hbm((layers, ARRIVALS, dr // 2, dm), F32),
            hbm((layers, 4, 2 * ur, k), F32),
        ]
        vm = pltpu.VMEM
        scratch = [
            vm((RING, RING, RING, 2 * ur, k), BF16), vm((RING, RING, dr, dm), BF16),
            vm((RING, CORES, tb, dm), BF16), vm((RING, CORES, tb, dm), BF16), vm((RING, CORES, tb, dm), BF16),
            vm((RING, 2 * tb, k), F32), vm((RING, 2 * tb, k), BF16), vm((RING, 2 * tb, k), BF16),
            vm((4, 2, 2, zd, k), F32), vm((4, 2, nk // 2, dm), F32),
            vm((RING, CORES, tb, dm), F32), vm((4, tb, dm), F32), vm((6, tb // 2, dm), F32),
            vm((4, tb, dm), BF16), vm((2, 2, 2 * ur, k), F32), vm((2, dr // 2, dm), F32),
            pltpu.SemaphoreType.DMA((N_SEM,)), pltpu.SemaphoreType.DMA((N_SEM,)), pltpu.SemaphoreType.DMA((N_LOCAL,)),
            pltpu.SemaphoreType.REGULAR((3,)),
        ]
        anyspec = pl.BlockSpec(memory_space=pl.ANY)
        call = pl.pallas_call(
            functools.partial(kernel, (dm, k, tb, ur, dr)),
            out_shape=outs,
            in_specs=[anyspec] * 4,
            out_specs=[anyspec] * len(outs),
            scratch_shapes=scratch,
            compiler_params=pltpu.CompilerParams(collective_id=0, has_side_effects=True, vmem_limit_bytes=67043328),
            name="mlp_stack",
            **({"interpret": interpret} if interpret else {}),
        )
        return tuple(call(x_loc, up_loc, down_loc, g_loc)[:4])

    return jax.shard_map(device_step, mesh=fine, in_specs=(tok_spec, weight_spec, weight_spec, tok_spec),
                         out_specs=(tok_spec, tok_spec, weight_spec, weight_spec), check_vma=False)
```

time: 4100 us -> 392 us (0.10)
  waiting for transfers between devices: 3730 us -> 0 us
  Pallas kernels: 0 us -> 384 us
  matrix products: 241 us -> 0 us
  local copies, waits for them, and re-layouts: 96.9 us -> 7.08 us
    reduce_scatter x2 -> x0, waiting for transfers between devices: 1490 us -> none  [device_step(): lax.psum_scatter(grad_down, all_axes, scatter_dimension=0, tiled=True)]
    unnamed x12 -> x0, waiting for transfers between devices: 1280 us -> none
    all_gather x6 -> x0, waiting for transfers between devices: 961 us -> none  [the longest x1 280 us: device_step(): full_down = lax.all_gather(copies[layer][1], 'inner', axis=0, tiled=True)]
    pallas_call x0 -> x1, Pallas kernels: none -> 384 us  [device_step(): return tuple(call(x_loc, up_loc, down_loc, g_loc)[:4])]
    dot_general x11 -> x0, matrix products: 218 us -> none  [contract(): lax.dot_general(left, right, (((left_dim,), (right_dim,)), ((), ())), pre...]
    unnamed x19 -> x6, local copies, waits for them, and re-layouts: 71.7 us -> 7.08 us
  transfers between devices with their start and end apart: 10 -> 0, of which waited for: 10 -> 0; matrix products, arithmetic and copies ran while one was open for 7% -> 0% of each run, Pallas kernels for 0% -> 0%
where the time goes in v1:
time: 392 us; the launch traced here: 391 us
  Pallas kernels  384 us (98%)
  local copies, waits for them, and re-layouts  7.08 us (2%)
    pallas_call x1, Pallas kernels, device_step(): return tuple(call(x_loc, up_loc, down_loc, g_loc)[:4])  384 us

profile of v1, /device:TPU:1, one launch (start us, length us, event | category | flops | bytes accessed | tf_op | source)
XLA Modules:
  0.0 391.5 jit_solution(16066759468445551905)
XLA Ops:
  0.6 383.7 %mlp_stack.1 = (bf16[128,2048]{1,0:T(8,128)(2,1)}, bf16[128,2048]{1,0:T(8,128)(2,1)}, f32[2,16,8192]{2,1,0:T(8,128)}, f32[2,64,2048]{2,1,0:T(8,128)}, bf16[4,2,1...) custom-call(bf16[128,2048]{1,0:T(8,128)(2,1)} %x_in.1, ...), custom_call_target="tpu_custom_call" | custom-call | tf_op jit(solution)/shard_map/mlp_stack/pallas_call | solution.py:799
  384.4 0.0 copy-start
  384.4 2.0 copy.12
  386.3 1.9 copy.13
  388.2 2.3 copy.14
  390.5 0.0 copy-done
  390.5 1.0 copy.15
Async XLA Ops:
  384.4 6.1 %copy-start = (f32[2,64,2048]{2,1,0:T(8,128)S(1)}, f32[2,64,2048]{2,1,0:T(8,128)}, u32[]{:S(2)}) copy-start(f32[2,64,2048]{2,1,0:T(8,128)} %get-tuple-element.19) | copy-start | bytes 3145732

commit v2 on v0

v2 whole, which is shorter than its diff:
```python
import functools

import jax
import jax.numpy as jnp
import numpy as np
from jax import lax
from jax.experimental import pallas as pl
from jax.experimental.pallas import tpu as pltpu
from jax.sharding import Mesh, PartitionSpec as P

MESH_ID = pl.DeviceIdType.MESH
ALL = ("x", "z", "y", "c")
F32, BF16 = jnp.float32, jnp.bfloat16
RING, CORES, ARRIVALS = 4, 2, 6
OWN, NXT, OPP, PRV = range(RING)
X0, X1, G1, G0 = range(RING)
HALVES = (0, 1)
N_SEM = 384
N_LOCAL = 116


def gelu_parts(pre_act):
    norm_cdf = 0.5 * (1.0 + lax.erf(pre_act * (2.0 ** -0.5)))
    norm_pdf = jnp.exp(-0.5 * pre_act * pre_act) * ((2.0 * jnp.pi) ** -0.5)
    return pre_act * norm_cdf, norm_cdf + pre_act * norm_pdf


def loop(n, body, init):
    return lax.fori_loop(0, n, body, init)


def dot_nn(left, right):
    return lax.dot_general(left, right, (((1,), (0,)), ((), ())), preferred_element_type=F32)


def dot_nt(left, right):
    return lax.dot_general(left, right, (((1,), (1,)), ((), ())), preferred_element_type=F32)


def dot_tn(left, right):
    return lax.dot_general(left, right, (((0,), (0,)), ((), ())), preferred_element_type=F32)


def kernel(dims, x_in, wu_in, wd_in, g_in,
           y_out, gi_out, gd_out,
           xh0, wuh, wdh, sh0, ah, ra1, rb1, ra2, rb2, uh,
           U, W, XV, GV1, GV0, SV, AV, DV, GPA, GPB, PP, DR, XR, RES, STA, STB,
           ss, rs, ls, credit):
    D, K, TB, UR, DR_ROWS = dims
    HB = TB // 2
    x, z, y, c = (lax.axis_index(a) for a in ALL)
    cp = 1 - c
    S2 = 2 * DR_ROWS
    XD = D // 4
    ZD = D // 16

    def dev(dx=0, dz=0, dy=0, dc=0):
        wrap = lambda v, d, n: v if d == 0 else lax.rem(v + (d % n), n)
        return (wrap(x, dx, 4), wrap(z, dz, 4), wrap(y, dy, 4), wrap(c, dc, 2))

    partner = dev(dc=1)
    rings = {"x": (x, dev(dx=1), dev(dx=-1)), "z": (z, dev(dz=1), dev(dz=-1)), "y": (y, dev(dy=1), dev(dy=-1))}
    off = lambda v, d: v if d == 0 else lax.rem(v + d, 4)

    count = [0]

    def rcopy(src, dst, to):
        k = count[0]
        count[0] += 1
        return pltpu.make_async_remote_copy(src_ref=src, dst_ref=dst, send_sem=ss.at[k], recv_sem=rs.at[k],
                                            device_id=to, device_id_type=MESH_ID)

    lcount = [0]

    def lcopy(src, dst):
        k = lcount[0]
        lcount[0] += 1
        return pltpu.make_async_copy(src, dst, ls.at[k])

    def mo(v, m):
        return pl.multiple_of(v, m)

    class Gather4:
        def __init__(self, axis, src, dst):
            i, right, left = rings[axis]
            lft, rgt = off(i, 3), off(i, 1)
            self.d = [rcopy(src(0), dst(i, 0), right), rcopy(src(1), dst(i, 1), right),
                      rcopy(src(0), dst(i, 0), left), rcopy(src(1), dst(i, 1), left),
                      rcopy(dst(lft, 0), dst(lft, 0), right), rcopy(dst(rgt, 1), dst(rgt, 1), left)]

        def start(self):
            for k in (0, 3, 1, 2):
                self.d[k].start()

        def forward(self):
            self.d[0].wait_recv()
            self.d[4].start()
            self.d[3].wait_recv()
            self.d[5].start()

        def neighbours(self):
            self.d[1].wait_recv()
            self.d[2].wait_recv()

        def opposite(self):
            self.d[4].wait_recv()
            self.d[5].wait_recv()

        def finish(self):
            self.neighbours()
            self.opposite()

        def drain(self):
            for d in self.d:
                d.wait_send()

    class Gather8:
        def __init__(self, src, dst):
            self.ring = Gather4("x", src, lambda b, h: dst(b, c, h))
            lft, rgt, opp = off(x, PRV), off(x, NXT), off(x, OPP)
            blocks = [(lft, 0), (rgt, 1), (lft, 1), (rgt, 0), (opp, 0), (opp, 1)]
            self.own = [rcopy(src(h), dst(x, c, h), partner) for h in HALVES]
            self.push = [rcopy(dst(b, c, h), dst(b, c, h), partner) for b, h in blocks]

        def start(self):
            self.ring.start()
            for d in self.own:
                d.start()

        def forward(self):
            self.ring.forward()
            self.push[0].start()
            self.push[1].start()

        def sides(self):
            self.ring.d[1].wait_recv()
            self.push[2].start()
            self.ring.d[2].wait_recv()
            self.push[3].start()

        def last(self):
            self.ring.d[4].wait_recv()
            self.push[4].start()
            self.ring.d[5].wait_recv()
            self.push[5].start()

        def wait_own(self):
            for d in self.own:
                d.wait_recv()

        def wait_push(self, ks):
            for k in ks:
                self.push[k].wait_recv()

        def drain(self):
            self.ring.drain()
            for d in self.own + self.push:
                d.wait_send()

    def add_rows(dst, srcs, rows, step):
        def body(r, carry):
            sl = pl.ds(mo(r * step, step), step)
            if len(dst.shape) == 3:
                for q in range(dst.shape[0]):
                    acc = dst[q, sl, :]
                    for s in srcs:
                        acc = acc + s[q, sl, :]
                    dst[q, sl, :] = acc
            else:
                acc = dst[sl, :]
                for s in srcs:
                    acc = acc + s[sl, :]
                dst[sl, :] = acc
            return carry
        loop(rows // step, body, None)

    barrier = pltpu.get_barrier_semaphore()
    group = [(dx, dc) for dx in range(RING) for dc in HALVES if dx or dc]
    peers = [dev(dx=dx, dc=dc) for dx, dc in group] + [rings[a][k] for a in "zy" for k in (1, 2)]
    for p in peers:
        pl.semaphore_signal(barrier, inc=1, device_id=p, device_id_type=MESH_ID)

    load_u = [[lcopy(wu_in.at[l, :, pl.ds(b * D, D)], RES.at[G0, pl.ds((l * RING + b) * UR, UR), :])
               for b in range(RING)] for l in HALVES]
    load_d = [lcopy(wd_in.at[l], RES.at[X1, pl.ds(l * DR_ROWS, DR_ROWS), :]) for l in HALVES]
    load_x = lcopy(x_in, RES.at[X0])
    load_g = lcopy(g_in, RES.at[G1])
    own_x = lcopy(x_in, XV.at[x, c])
    own_g = lcopy(g_in, GV1.at[x, c])
    own_d0 = lcopy(wd_in.at[0], W.at[y, z])
    for cpy in load_u[0] + load_u[1] + load_d + [load_x, own_d0, own_x, load_g, own_g]:
        cpy.start()

    low = lax.broadcasted_iota(jnp.int32, (UR, S2), 1) < DR_ROWS
    swap = lambda v: pltpu.roll(v, DR_ROWS, 1)
    for l in HALVES:
        for cpy in load_u[l]:
            cpy.wait()
        for b in range(RING):
            rows = pl.ds((l * RING + b) * UR, UR)
            for yy in range(RING):
                for m in HALVES:
                    s0 = RES[G0, rows, pl.ds((2 * m * RING + yy) * S2, S2)].astype(F32)
                    s1 = RES[G0, rows, pl.ds(((2 * m + 1) * RING + yy) * S2, S2)].astype(F32)
                    cols = pl.ds((yy * 2 + m) * S2, S2)
                    AV[l, 0, pl.ds(2 * b * UR, UR), cols] = jnp.where(low, s0, swap(s1)).astype(BF16)
                    AV[l, 0, pl.ds((2 * b + 1) * UR, UR), cols] = jnp.where(low, swap(s0), s1).astype(BF16)
    for cpy in load_d + [load_x, own_d0]:
        cpy.wait()
    pl.semaphore_wait(barrier, len(peers))

    half = lambda h: pl.ds(h * HB, HB)
    gx0 = Gather8(lambda h: RES.at[X0, half(h)], lambda b, k, h: XV.at[b, k, half(h)])
    gg1 = Gather8(lambda h: RES.at[G1, half(h)], lambda b, k, h: GV1.at[b, k, half(h)])
    up = [U, wuh.at[1]]
    down = [W, wdh.at[1]]
    hr = DR_ROWS // 4

    def down_gathers(l):
        def rows(q, h):
            return pl.ds((2 * q + h) * hr, hr)

        def src(q):
            return lambda h: RES.at[X1, pl.ds(l * DR_ROWS + (2 * q + h) * hr, hr)]
        to = down[l]
        first = [Gather4("z", src(0), lambda b, h: to.at[y, b, rows(0, h)]),
                 Gather4("y", src(1), lambda b, h: to.at[b, z, rows(1, h)])]
        second = [Gather4("y", lambda h: to.at[y, :, rows(0, h)], lambda b, h: to.at[b, :, rows(0, h)]),
                  Gather4("z", lambda h: to.at[:, z, rows(1, h)], lambda b, h: to.at[:, b, rows(1, h)])]
        return first, second

    def up_first(to):
        return [Gather4("y", lambda h: to.at[h, z, y], lambda b, h: to.at[h, z, b]),
                Gather4("z", lambda h: to.at[2 + h, z, y], lambda b, h: to.at[2 + h, b, y])]

    def up_second(to):
        return [Gather4("z", lambda h: to.at[h, z], lambda b, h: to.at[h, b]),
                Gather4("y", lambda h: to.at[2 + h, :, y], lambda b, h: to.at[2 + h, :, b])]

    def up_unit(to, j):
        yj, zj = off(y, j), off(z, j)
        return [Gather4("z", lambda h: to.at[h, z, yj], lambda b, h: to.at[h, b, yj]),
                Gather4("y", lambda h: to.at[2 + h, zj, y], lambda b, h: to.at[2 + h, zj, b])]

    def do(gathers, step):
        for g in gathers:
            getattr(g, step)()

    mine = pl.ds(mo(c * UR, UR), UR)

    def up_exchange(l):
        sends = []
        for dx, dc in group:
            tx, tc = off(x, dx), (cp if dc else c)
            src = AV.at[l, 0, pl.ds(mo((tx * 2 + tc) * UR, UR), UR), :]
            sends.append(rcopy(src, up[l].at[x, z, y, mine, :], dev(dx=dx, dc=dc)))
        for cpy in sends:
            cpy.start()
        return sends

    (d0a, d0b), (d1a, d1b) = down_gathers(0), down_gathers(1)
    u0a, u1a, u1b = up_first(up[0]), up_first(up[1]), up_second(up[1])
    u0u = [up_unit(up[0], j) for j in (OWN, PRV, NXT, OPP)]
    ex0 = up_exchange(0)
    do(d0a, "start")
    gx0.start()
    ex1 = up_exchange(1)
    my_rows = pl.ds(mo((x * 2 + c) * UR, UR), UR)
    own_u1 = lcopy(AV.at[1, 0, my_rows, :], up[1].at[x, z, y, mine, :])
    own_u1.start()
    own_d1 = lcopy(RES.at[X1, pl.ds(DR_ROWS, DR_ROWS), :], down[1].at[y, z])
    own_d1.start()
    U[x, z, y, mine, :] = AV[0, 0, my_rows, :]
    do(d0a, "forward")
    for cpy in ex0:
        cpy.wait_recv()
    do(u0a, "start")
    do(u0u[0], "start")
    do(d0a, "finish")
    do(u0a, "forward")
    do(u0a, "neighbours")
    do(u0u[1], "start")
    do(u0u[2], "start")
    do(u0u[0], "forward")
    do(u0a, "opposite")
    do(u0u[3], "start")
    do(u0u[1], "forward")
    do(u0u[2], "forward")
    gx0.forward()
    do(u0u[3], "forward")
    do(d0b, "start")
    gx0.sides()
    gx0.last()
    load_g.wait()
    gg1.start()
    gx0.wait_own()
    gx0.wait_push(range(len(gx0.push)))
    own_x.wait()
    save_x = lcopy(XV, xh0)
    save_x.start()
    for cpy in ex0 + ex1:
        cpy.wait_send()
    for unit in u0u:
        do(unit, "finish")
    save_u0 = lcopy(U, wuh.at[0])
    save_u0.start()

    T2 = 2 * TB
    ND = D // 4
    NK = K // 4

    def up_tile(t, n):
        cols = pl.ds(mo(n * NK, NK), NK)
        return dot_nn(XV[t].reshape(T2, D), U[:, :, :, :, cols].reshape(D, NK)), cols

    def hidden0(t):
        def body(n, carry):
            pre, cols = up_tile(t, n)
            act, slope = gelu_parts(pre)
            AV[t, :, :, cols] = act.astype(BF16).reshape(2, TB, NK)
            SV[t, :, :, cols] = slope.reshape(2, TB, NK)
            return carry
        loop(K // NK, body, None)

    def hidden1(t):
        def body(n, carry):
            pre, cols = up_tile(t, n)
            act, slope = gelu_parts(pre)
            AV[t, :, :, cols] = act.astype(BF16).reshape(2, TB, NK)
            DV[t, :, cols] = (SV[t, :, :, cols].reshape(T2, NK) * slope).astype(BF16)
            return carry
        loop(K // NK, body, None)

    def dact(gv, t, n):
        return dot_nt(gv[t].reshape(T2, D), W[n].reshape(NK, D))

    def dact1(t):
        def body(n, carry):
            SV[t, :, :, pl.ds(mo(n * NK, NK), NK)] = dact(GV1, t, n).reshape(2, TB, NK)
            return carry
        loop(RING, body, None)

    def dact0(t):
        def body(n, carry):
            cols = pl.ds(mo(n * NK, NK), NK)
            DV[t, :, cols] = (dact(GV0, t, n) * SV[t, :, :, cols].reshape(T2, NK)).astype(BF16)
            return carry
        loop(RING, body, None)

    def down_part(act, j):
        t = off(x, j)

        def body(n, carry):
            cols = pl.ds(mo(n * ND, ND), ND)
            PP[j, :, :, cols] = dot_nn(act[t, :, :, 0:K].reshape(T2, K), W[:, :, :, cols].reshape(K, ND)).reshape(2, TB, ND)
            return carry
        loop(RING, body, None)

    def dx_part(j):
        t = off(x, j)

        def body(n, carry):
            cols = pl.ds(mo(n * ND, ND), ND)
            PP[j, :, :, cols] = dot_nt(DV[t], U[n].reshape(ND, K)).reshape(2, TB, ND)
            return carry
        loop(RING, body, None)

    class Reduce8:
        def __init__(self, part, index, chunks=1):
            self.part, self.index, self.chunks = part, index, chunks
            _, right, left = rings["x"]
            self.right, self.left = right, left
            self.qb = HB // chunks
            self.pair = [rcopy(PP.at[j, cp], DR.at[j], partner) for j in range(RING)]

            def messages(q):
                src = lambda j, h: PP.at[j, c, self.rows(q, h)]
                dst = lambda k: XR.at[k, pl.ds(q * self.qb, self.qb)]
                return [rcopy(src(OPP, 0), dst(0), right), rcopy(src(OPP, 1), dst(1), left),
                        rcopy(src(NXT, 1), dst(2), right), rcopy(src(PRV, 0), dst(3), left),
                        rcopy(src(NXT, 0), dst(4), right), rcopy(src(PRV, 1), dst(5), left)]
            self.m = [messages(q) for q in range(chunks)]

        def rows(self, q, h):
            return pl.ds((2 * q + h) * self.qb, self.qb)

        def credits(self):
            if self.index:
                for k in range(len((self.right, self.left, partner))):
                    pl.semaphore_wait(credit.at[k], 1)

        def compute(self, j):
            self.part(j)
            self.pair[j].start()

        def combine(self, j):
            self.pair[j].wait_recv()
            add_rows(PP.at[j, c], [DR.at[j]], TB, min(TB, 16))

        def opposite(self, q):
            self.m[q][0].start()
            self.m[q][1].start()

        def sides(self, q):
            self.m[q][2].start()
            self.m[q][3].start()

        def relay(self, q):
            for k, j, h in ((0, NXT, 0), (1, PRV, 1)):
                self.m[q][k].wait_recv()
                add_rows(PP.at[j, c, self.rows(q, h)], [XR.at[k, pl.ds(q * self.qb, self.qb)]], self.qb, min(self.qb, 16))
                self.m[q][4 + k].start()

        def finish(self, q, res, outs):
            for d in self.m[q][2:]:
                d.wait_recv()
            step = min(self.qb, 16)
            for h, (kl, kr) in enumerate(((4, 3), (2, 5))):
                def body(r, carry):
                    lo = pl.ds(mo(q * self.qb + r * step, step), step)
                    sl = pl.ds(mo((2 * q + h) * self.qb + r * step, step), step)
                    tot = PP[OWN, c, sl, :] + (XR[kl, lo, :] + XR[kr, lo, :])
                    val = (res[sl, :].astype(F32) + tot).astype(BF16)
                    for o in outs:
                        o[sl, :] = val
                    return carry
                loop(self.qb // step, body, None)

        def release(self):
            for d in self.pair + sum(self.m, []):
                d.wait_send()
            for k, to in enumerate((self.right, self.left, partner)):
                pl.semaphore_signal(credit.at[k], inc=1, device_id=to, device_id_type=MESH_ID)

        def drain(self):
            for d in self.pair + sum(self.m, []):
                d.wait_send()

        def launch(self):
            self.credits()
            self.compute(OPP)
            self.compute(NXT)
            self.combine(OPP)
            self.opposite(0)
            self.compute(PRV)
            self.combine(NXT)
            self.combine(PRV)
            self.sides(0)

    def grad_a(j, dst):
        t = off(z, j)
        for h in HALVES:
            lo = [pl.ds(mo((2 * h + q) * XD + t * ZD, ZD), ZD) for q in HALVES]
            lhs = jnp.concatenate([XV[:, :, :, s].reshape(8 * TB, ZD) for s in lo], axis=1)

            def body(n, carry):
                cols = pl.ds(mo(n * NK, NK), NK)
                dst[h, :, :, cols] = dot_tn(lhs, DV[:, :, cols].reshape(8 * TB, NK)).reshape(2, ZD, NK)
                return carry
            loop(K // NK, body, None)

    def grad_b(gv, j, dst):
        cols_l = pl.ds(mo(off(y, j) * NK, NK), NK)
        for n in HALVES:
            def body(m, carry):
                cols = pl.ds(mo(n * K + m * ND, ND), ND)
                out = dot_tn(AV[:, :, :, cols_l].reshape(8 * TB, NK), gv[:, :, :, cols].reshape(8 * TB, ND))
                dst[:, n, :, pl.ds(mo(m * ND, ND), ND)] = out.reshape(2, NK // 2, ND)
                return carry
            loop(2, body, None)

    class Reduce4:
        def __init__(self, axis, part, recv, stage):
            _, right, left = rings[axis]
            self.part, self.recv, self.stage = part, recv, stage
            self.m = [rcopy(part(OPP, 0), recv(0), right), rcopy(part(OPP, 1), recv(1), left),
                      rcopy(part(NXT, 1), recv(2), right), rcopy(part(PRV, 0), recv(3), left),
                      rcopy(part(NXT, 0), recv(4), right), rcopy(part(PRV, 1), recv(5), left)]
            self.to = [(NXT, 0), (PRV, 1), (OWN, 1), (OWN, 0), (OWN, 0), (OWN, 1)]
            self.loads = [lcopy(recv(k), stage(k)) for k in range(ARRIVALS)]

        def opposite(self):
            self.m[0].start()
            self.m[1].start()

        def sides(self, j):
            self.m[2 if j == NXT else 3].start()

        def fetch(self, k):
            self.m[k].wait_send()
            self.m[k].wait_recv()
            self.loads[k].start()

        def absorb(self, k):
            self.loads[k].wait()
            dst = self.part(*self.to[k])
            add_rows(dst, [self.stage(k)], dst.shape[1], min(dst.shape[1], 16))

    def arrive(reduces, ks):
        for k in ks:
            for r in reduces:
                r.fetch(k)
        for k in ks:
            for r in reduces:
                r.absorb(k)

    def relay(reduces):
        for k in (0, 1):
            for r in reduces:
                r.fetch(k)
        for k in (0, 1):
            for r in reduces:
                r.absorb(k)
                r.m[4 + k].start()

    EARLY, LATE = (2, 3), (4, 5)
    hq = DR_ROWS // 2
    own_grads = [(SV.at[pl.ds(0, 2)], SV.at[pl.ds(2, 2)]), (GPA.at[OWN], GPB.at[OWN])]

    def make_reduce(l, q, chunks):
        own_a, own_b = own_grads[l]
        ca = pl.ds(q * (K // chunks), K // chunks)
        nb = pl.ds(q, 1) if chunks == 2 else pl.ds(0, 2)
        pick = ((OPP, 0), (OPP, 1), (NXT, 1), (PRV, 0), (NXT, 0), (PRV, 1))

        def part_a(j, h):
            return (own_a.at[h, :, :, ca] if j == OWN else GPA.at[j, h, :, :, ca])

        def part_b(j, h):
            return (own_b.at[h, nb] if j == OWN else GPB.at[j, h, nb])

        def part_a2(j, h):
            return own_a.at[h, :, pl.ds(mo(off(y, j) * 2 * UR, 2 * UR), 2 * UR), ca]

        def part_b2(j, h):
            t = off(z, j)
            return own_b.at[t // 2, nb, pl.ds(mo(lax.rem(t, 2) * DR_ROWS + h * hq, hq), hq), :]
        return (Reduce4("z", part_a, lambda k: ra1.at[l, k, :, :, ca], lambda k: part_a(*pick[k])),
                Reduce4("y", part_b, lambda k: rb1.at[l, k, nb], lambda k: part_b(*pick[k])),
                Reduce4("y", part_a2, lambda k: ra2.at[l, k, :, :, ca], lambda k: STA.at[k % 2, :, :, ca]),
                Reduce4("z", part_b2, lambda k: rb2.at[l, k, nb], lambda k: STB.at[k % 2, nb]))

    def second_start(reduces):
        for r in reduces:
            r.opposite()
            r.sides(NXT)
            r.sides(PRV)

    def grads_out_start(l, q, chunks):
        own_a, own_b = own_grads[l]
        ca = pl.ds(q * (K // chunks), K // chunks)

        def rows_of(tx, tc):
            return own_a.at[tx // 2, lax.rem(tx, 2), pl.ds(mo((2 * y + tc) * UR, UR), UR), ca]
        to = uh.at[l, x, mine, ca]
        sends = [rcopy(rows_of(off(x, dx), cp if dc else c), to, dev(dx=dx, dc=dc)) for dx, dc in group]
        local = [lcopy(rows_of(x, c), to)]
        for n in ((q,) if chunks == 2 else HALVES):
            local.append(lcopy(own_b.at[z // 2, n, pl.ds(mo(lax.rem(z, 2) * DR_ROWS, DR_ROWS), DR_ROWS), :],
                               gd_out.at[l, :, pl.ds(n * K, K)]))
        for cpy in sends + local:
            cpy.start()
        return sends, local

    def grads_out_finish(state):
        for cpy in state[0]:
            cpy.wait_recv()
            cpy.wait_send()
        for cpy in state[1]:
            cpy.wait()

    hidden0(0)
    do(d0b, "forward")
    do(d1a, "start")
    for cpy in ex1:
        cpy.wait_recv()
    own_u1.wait()
    own_d1.wait()
    do(u1a, "start")
    hidden0(1)
    hidden0(2)
    gg1.forward()
    hidden0(3)
    save_s = lcopy(SV, sh0)
    save_s.start()
    save_a0 = lcopy(AV, ah.at[0])
    save_a0.start()
    gg1.sides()
    do(d0b, "finish")
    save_d0 = lcopy(W, wdh.at[0])
    save_d0.start()
    save_x.wait()
    gx0.drain()
    do(d0a, "drain")

    r = Reduce8(functools.partial(down_part, AV), 0, 2)
    r.compute(OPP)
    do(d1a, "forward")
    r.compute(NXT)
    r.combine(OPP)
    r.opposite(0)
    r.compute(PRV)
    r.combine(NXT)
    r.combine(PRV)
    r.sides(0)
    do(u1a, "forward")
    gg1.last()
    do(d1a, "finish")
    do(d1b, "start")
    r.compute(OWN)
    do(u1a, "finish")
    r.relay(0)
    r.opposite(1)
    r.sides(1)
    r.combine(OWN)
    do(d1b, "forward")
    do(u1b, "start")

    def token_gathers(slot, buf):
        rows = lambda q, h: pl.ds((2 * q + h) * r.qb, r.qb)
        make = lambda q: Gather8(lambda h: RES.at[slot, rows(q, h)], lambda b, k, h: buf.at[b, k, rows(q, h)])
        return [make(0), make(1)]

    gx1 = token_gathers(X1, XV)
    r.relay(1)
    do(d1a, "drain")
    r.finish(0, RES.at[X0], [RES.at[X1], XV.at[x, c]])
    gx1[0].start()
    gg1.wait_own()
    gg1.wait_push(range(len(gg1.push)))
    own_g.wait()
    save_d0.wait()
    do(d0b, "drain")
    do(d1b, "finish")
    load_w1d = lcopy(wdh.at[1], W)
    load_w1d.start()
    do(u1b, "forward")
    r.finish(1, RES.at[X0], [RES.at[X1], XV.at[x, c]])
    gx1[1].start()
    save_s.wait()
    load_w1d.wait()
    dact1(off(x, OWN))
    gx1[0].forward()
    dact1(off(x, NXT))
    gx1[0].sides()
    r.release()
    dact1(off(x, PRV))
    gx1[1].forward()
    gx1[0].last()
    dact1(off(x, OPP))
    load_w0d_again = lcopy(wdh.at[0], W)
    load_w0d_again.start()
    gx1[1].sides()
    save_u0.wait()
    do(sum(u0u, u0a), "drain")
    do(u1b, "finish")
    load_w1u = lcopy(wuh.at[1], U)
    load_w1u.start()
    load_w1u.wait()
    save_a0.wait()
    do(gx1, "wait_own")
    hidden1(off(x, OWN))
    gx1[1].last()
    for g in gx1:
        g.wait_push((0, 2))
    hidden1(off(x, PRV))
    for g in gx1:
        g.wait_push((1, 3))
    hidden1(off(x, NXT))
    for g in gx1:
        g.wait_push((4, 5))
    hidden1(off(x, OPP))
    load_s0 = lcopy(sh0, SV)
    load_s0.start()
    save_a1 = lcopy(AV, ah.at[1])
    save_a1.start()

    a1, b1, a2, b2 = make_reduce(1, 0, 1)
    grad_b(GV1, OPP, GPB.at[OPP])
    b1.opposite()
    grad_a(OPP, GPA.at[OPP])
    a1.opposite()
    r = Reduce8(dx_part, 1, 2)
    r.launch()
    grad_b(GV1, NXT, GPB.at[NXT])
    b1.sides(NXT)
    grad_b(GV1, PRV, GPB.at[PRV])
    b1.sides(PRV)
    r.relay(0)
    r.opposite(1)
    r.sides(1)
    r.compute(OWN)
    load_w0u_again = lcopy(wuh.at[0], U)
    load_w0u_again.start()
    grad_a(NXT, GPA.at[NXT])
    a1.sides(NXT)
    grad_a(PRV, GPA.at[PRV])
    a1.sides(PRV)
    r.combine(OWN)
    gg0 = token_gathers(G0, GV0)
    r.relay(1)
    r.finish(0, RES.at[G1], [RES.at[G0], GV0.at[x, c]])
    gg0[0].start()
    grad_b(GV1, OWN, GPB.at[OWN])
    save_a1.wait()
    load_a0 = lcopy(ah.at[0], AV)
    load_a0.start()
    gg1.drain()
    load_a1 = lcopy(ah.at[1], GV1.at[:, :, :, 0:K])
    load_a1.start()
    r.finish(1, RES.at[G1], [RES.at[G0], GV0.at[x, c]])
    gg0[1].start()
    gg0[0].forward()
    grad_a(OWN, GPA.at[OWN])
    do(gx1, "drain")
    load_x0 = lcopy(xh0, XV)
    load_x0.start()
    gg0[0].sides()
    relay((b1, a1))
    r.release()
    gg0[1].forward()
    gg0[0].last()
    load_w0d_again.wait()
    load_s0.wait()
    do(gg0, "wait_own")
    dact0(off(x, OWN))
    gg0[1].sides()
    gg0[1].last()
    for g in gg0:
        g.wait_push((0, 2))
    dact0(off(x, PRV))
    for g in gg0:
        g.wait_push((1, 3))
    dact0(off(x, NXT))
    for g in gg0:
        g.wait_push((4, 5))

    a1n, b1n, a2n, b2n = zip(*[make_reduce(0, q, 2) for q in HALVES])
    load_a0.wait()
    grad_b(GV0, OPP, GPB.at[OPP])
    b1n[0].opposite()
    dact0(off(x, OPP))
    load_w1d_again = lcopy(wdh.at[1], W)
    load_w1d_again.start()
    load_x0.wait()
    grad_a(OPP, GPA.at[OPP])
    a1n[0].opposite()
    load_w0u_again.wait()
    r = Reduce8(dx_part, 2)
    r.launch()
    arrive((b1, a1), EARLY + LATE)
    second_start((a2, b2))
    grad_b(GV0, NXT, GPB.at[NXT])
    b1n[0].sides(NXT)
    grad_b(GV0, PRV, GPB.at[PRV])
    b1n[0].sides(PRV)
    grad_a(NXT, GPA.at[NXT])
    a1n[0].sides(NXT)
    grad_a(PRV, GPA.at[PRV])
    a1n[0].sides(PRV)
    relay((b2, a2))
    r.relay(0)
    relay((b1n[0], a1n[0]))
    for red in (b1n[1], a1n[1]):
        red.opposite()
        red.sides(NXT)
        red.sides(PRV)
    r.compute(OWN)
    r.combine(OWN)
    grad_b(GV0, OWN, own_grads[0][1])
    grad_a(OWN, own_grads[0][0])
    r.finish(0, RES.at[G0], [RES.at[X0]])
    r.release()
    write_gi = lcopy(RES.at[X0], gi_out)
    write_gi.start()
    arrive((b1n[0], a1n[0]), EARLY)
    load_a1.wait()
    load_w1d_again.wait()
    r = Reduce8(functools.partial(down_part, GV1), 3)
    r.launch()
    r.compute(OWN)
    arrive((b2, a2), EARLY)
    arrive((b2, a2), LATE)
    state1 = grads_out_start(1, 0, 1)
    r.combine(OWN)
    arrive((b1n[0], a1n[0]), LATE)
    r.relay(0)
    relay((b1n[1], a1n[1]))
    second_start((a2n[0], b2n[0]))
    arrive((b1n[1], a1n[1]), EARLY)
    relay((b2n[0], a2n[0]))
    arrive((b1n[1], a1n[1]), LATE)
    second_start((a2n[1], b2n[1]))
    arrive((b2n[0], a2n[0]), EARLY)
    arrive((b2n[0], a2n[0]), LATE)
    state0 = [grads_out_start(0, 0, 2)]
    relay((b2n[1], a2n[1]))
    r.finish(0, RES.at[X1], [RES.at[G1]])
    write_y = lcopy(RES.at[G1], y_out)
    write_y.start()
    grads_out_finish(state1)
    arrive((b2n[1], a2n[1]), EARLY)
    arrive((b2n[1], a2n[1]), LATE)
    state0.append(grads_out_start(0, 1, 2))
    r.drain()
    do(d1b + u1a + u1b + gg0, "drain")
    write_gi.wait()
    write_y.wait()
    for state in state0:
        grads_out_finish(state)
    assert count[0] <= N_SEM and lcount[0] <= N_LOCAL


def finish_kernel(y_in, gi_in, gu_in, gd_in, y_out, gi_out, gu_out, gd_out, ybuf, gibuf, gubuf, gdbuf, gushuf, sems):
    layers, ur, ff = gu_out.shape
    s2 = ff // 64
    half = s2 // 2
    loads = [pltpu.make_async_copy(a, b, sems.at[0, k])
             for k, (a, b) in enumerate(((gu_in, gubuf), (gd_in, gdbuf), (y_in, ybuf), (gi_in, gibuf)))]
    stores = [pltpu.make_async_copy(a, b, sems.at[1, k])
              for k, (a, b) in enumerate(((gushuf, gu_out), (gdbuf, gd_out), (ybuf, y_out), (gibuf, gi_out)))]
    for cpy in loads:
        cpy.start()
    low = lax.broadcasted_iota(jnp.int32, (ur, s2), 1) < half
    swap = lambda v: pltpu.roll(v, half, 1)
    for k in (1, 2, 3):
        loads[k].wait()
        stores[k].start()
    loads[0].wait()
    for l in range(layers):
        for b in range(RING):
            for yy in range(RING):
                for m in HALVES:
                    cols = pl.ds((yy * 2 + m) * s2, s2)
                    t0, t1 = (gubuf[l, b, pl.ds(k * ur, ur), cols] for k in HALVES)
                    strip = (b * RING + 2 * m) * RING + yy
                    gushuf[l, :, pl.ds(strip * s2, s2)] = jnp.where(low, t0, swap(t1))
                    gushuf[l, :, pl.ds((strip + RING) * s2, s2)] = jnp.where(low, swap(t0), t1)
    stores[0].start()
    for cpy in stores:
        cpy.wait()


def solution(mesh, interpret=None):
    fine = Mesh(np.asarray(mesh.devices).reshape(4, 4, 4, 2), ALL)
    tok_spec = P(ALL, None)
    weight_spec = P(None, ALL, None)

    def device_step(x_loc, up_loc, down_loc, g_loc):
        layers, ur, ff = up_loc.shape
        dr, dm = down_loc.shape[1:]
        tb = x_loc.shape[0]
        k = ff // 8
        zd = dm // 16
        hbm = lambda shape, dt: jax.ShapeDtypeStruct(shape, dt)
        outs = [
            hbm((tb, dm), BF16), hbm((tb, dm), BF16), hbm((layers, dr, dm), F32),
            hbm((RING, CORES, tb, dm), BF16),
            hbm((layers, RING, RING, RING, 2 * ur, k), BF16),
            hbm((layers, RING, RING, dr, dm), BF16),
            hbm((RING, CORES, tb, k), F32), hbm((layers, RING, CORES, tb, k), BF16),
            *[hbm((layers, ARRIVALS, CORES, n, k), F32) for n in (zd, zd, 2 * ur, 2 * ur)],
            hbm((layers, RING, 2 * ur, k), F32),
        ]
        vm = pltpu.VMEM
        scratch = [
            vm((RING, RING, RING, 2 * ur, k), BF16), vm((RING, RING, dr, dm), BF16),
            vm((RING, CORES, tb, dm), BF16), vm((RING, CORES, tb, dm), BF16), vm((RING, CORES, tb, dm), BF16),
            vm((RING, CORES, tb, k), F32), vm((RING, CORES, tb, k), BF16), vm((RING, 2 * tb, k), BF16),
            vm((RING, CORES, CORES, zd, k), F32), vm((RING, CORES, CORES, zd, k), F32),
            vm((RING, CORES, tb, dm), F32), vm((4, tb, dm), F32), vm((6, tb // 2, dm), F32),
            vm((4, tb, dm), BF16), vm((CORES, CORES, 2 * ur, k), F32), vm((CORES, CORES, 2 * ur, k), F32),
            pltpu.SemaphoreType.DMA((N_SEM,)), pltpu.SemaphoreType.DMA((N_SEM,)), pltpu.SemaphoreType.DMA((N_LOCAL,)),
            pltpu.SemaphoreType.REGULAR((3,)),
        ]
        anyspec = pl.BlockSpec(memory_space=pl.ANY)
        call = pl.pallas_call(
            functools.partial(kernel, (dm, k, tb, ur, dr)),
            out_shape=outs,
            in_specs=[anyspec] * 4,
            out_specs=[anyspec] * len(outs),
            scratch_shapes=scratch,
            compiler_params=pltpu.CompilerParams(collective_id=0, has_side_effects=True, vmem_limit_bytes=67043328),
            name="mlp_stack",
            **({"interpret": interpret} if interpret else {}),
        )
        y_raw, gi_raw, gd_raw, *_, gu_raw = call(x_loc, up_loc, down_loc, g_loc)
        raws = (y_raw, gi_raw, gu_raw, gd_raw)
        outs = [hbm((tb, dm), BF16), hbm((tb, dm), BF16), hbm((layers, ur, ff), F32), hbm((layers, dr, dm), F32)]
        return tuple(pl.pallas_call(
            finish_kernel, out_shape=outs, in_specs=[anyspec] * len(outs), out_specs=[anyspec] * len(outs),
            scratch_shapes=[vm(v.shape, v.dtype) for v in raws] + [vm(outs[2].shape, F32), pltpu.SemaphoreType.DMA((2, len(outs)))],
            name="write_out")(*raws))

    return jax.shard_map(device_step, mesh=fine, in_specs=(tok_spec, weight_spec, weight_spec, tok_spec),
                         out_specs=(tok_spec, tok_spec, weight_spec, weight_spec), check_vma=False)
```

time: 4100 us -> 324 us (0.08)
  waiting for transfers between devices: 3730 us -> 0 us
  Pallas kernels: 0 us -> 322 us
  matrix products: 241 us -> 0 us
  local copies, waits for them, and re-layouts: 96.9 us -> 0 us
    reduce_scatter x2 -> x0, waiting for transfers between devices: 1490 us -> none  [device_step(): lax.psum_scatter(grad_down, all_axes, scatter_dimension=0, tiled=True)]
    unnamed x12 -> x0, waiting for transfers between devices: 1280 us -> none
    all_gather x6 -> x0, waiting for transfers between devices: 961 us -> none  [the longest x1 280 us: device_step(): full_down = lax.all_gather(copies[layer][1], 'inner', axis=0, tiled=True)]
    pallas_call x0 -> x2, Pallas kernels: none -> 322 us  [the longest x1 319 us: device_step(): y_raw, gi_raw, gd_raw, *_, gu_raw = call(x_loc, up_loc, down_loc, g_loc)]
    dot_general x11 -> x0, matrix products: 218 us -> none  [contract(): lax.dot_general(left, right, (((left_dim,), (right_dim,)), ((), ())), pre...]
    unnamed x19 -> x0, local copies, waits for them, and re-layouts: 71.7 us -> none
  transfers between devices with their start and end apart: 10 -> 0, of which waited for: 10 -> 0; matrix products, arithmetic and copies ran while one was open for 7% -> 0% of each run, Pallas kernels for 0% -> 0%
where the time goes in v2:
time: 324 us; the launch traced here: 323 us
  Pallas kernels  322 us (99%)
    pallas_call x1, Pallas kernels, device_step(): y_raw, gi_raw, gd_raw, *_, gu_raw = call(x_loc, up_loc, down_loc, g_loc)  319 us

profile of v2, /device:TPU:1, one launch (start us, length us, event | category | flops | bytes accessed | tf_op | source)
XLA Modules:
  0.0 322.9 jit_solution(5294281319162219978)
XLA Ops:
  0.6 318.8 %mlp_stack.1 = (bf16[128,2048]{1,0:T(8,128)(2,1)}, bf16[128,2048]{1,0:T(8,128)(2,1)}, f32[2,64,2048]{2,1,0:T(8,128)}, bf16[4,2,128,2048]{3,2,1,0:T(8,128)(2,1)},...) custom-call(bf16[128,2048]{1,0:T(8,128)(2,1)} %x_in.1, ...), custom_call_target="tpu_custom_call" | custom-call | tf_op jit(solution)/shard_map/mlp_stack/pallas_call | solution.py:887
  319.5 3.3 %write_out.1 = (bf16[128,2048]{1,0:T(8,128)(2,1)}, bf16[128,2048]{1,0:T(8,128)(2,1)}, f32[2,16,8192]{2,1,0:T(8,128)}, f32[2,64,2048]{2,1,0:T(8,128)}) custom-call(bf16[128,2048]{1,0:T(8,128)(2,1)} %get-tuple-element.8.y_in, bf16[128,2048]{1,0:T(8,128)(2,1)} %get-tuple-element.9.gi_in, f32[2,4,32,1024]{3,2,1,0:T(8,128)} %get-tuple-element.10.gu_in, ...), custom_call_target="tpu_custom_call" | custom-call | tf_op jit(solution)/shard_map/write_out/pallas_call | solution.py:890

commit v3 on v2

--- a/solution.py
+++ b/solution.py
@@ -15,8 +15,9 @@
 OWN, NXT, OPP, PRV = range(RING)
 X0, X1, G1, G0 = range(RING)
 HALVES = (0, 1)
-N_SEM = 384
-N_LOCAL = 116
+WHOLE, SPLIT2, SPLIT3 = (4,), (2, 2), (1, 1, 2)
+N_SEM = 440
+N_LOCAL = 120
 
 
 def gelu_parts(pre_act):
@@ -210,32 +211,40 @@
     pl.semaphore_wait(barrier, len(peers))
 
     half = lambda h: pl.ds(h * HB, HB)
+
+    def tile_cols(split, q):
+        return pl.ds(sum(split[:q]) * (D // RING), split[q] * (D // RING))
+
     gx0 = Gather8(lambda h: RES.at[X0, half(h)], lambda b, k, h: XV.at[b, k, half(h)])
     gg1 = Gather8(lambda h: RES.at[G1, half(h)], lambda b, k, h: GV1.at[b, k, half(h)])
     up = [U, wuh.at[1]]
     down = [W, wdh.at[1]]
     hr = DR_ROWS // 4
 
-    def down_gathers(l):
+    def down_gathers(l, split):
         def rows(q, h):
             return pl.ds((2 * q + h) * hr, hr)
 
         def src(q):
             return lambda h: RES.at[X1, pl.ds(l * DR_ROWS + (2 * q + h) * hr, hr)]
         to = down[l]
+
+        def second(n):
+            cs = tile_cols(split, n)
+            return [Gather4("y", lambda h: to.at[y, :, rows(0, h), cs], lambda b, h: to.at[b, :, rows(0, h), cs]),
+                    Gather4("z", lambda h: to.at[:, z, rows(1, h), cs], lambda b, h: to.at[:, b, rows(1, h), cs])]
         first = [Gather4("z", src(0), lambda b, h: to.at[y, b, rows(0, h)]),
                  Gather4("y", src(1), lambda b, h: to.at[b, z, rows(1, h)])]
-        second = [Gather4("y", lambda h: to.at[y, :, rows(0, h)], lambda b, h: to.at[b, :, rows(0, h)]),
-                  Gather4("z", lambda h: to.at[:, z, rows(1, h)], lambda b, h: to.at[:, b, rows(1, h)])]
-        return first, second
+        return [first] + [second(n) for n in range(len(split))]
 
     def up_first(to):
         return [Gather4("y", lambda h: to.at[h, z, y], lambda b, h: to.at[h, z, b]),
                 Gather4("z", lambda h: to.at[2 + h, z, y], lambda b, h: to.at[2 + h, b, y])]
 
-    def up_second(to):
-        return [Gather4("z", lambda h: to.at[h, z], lambda b, h: to.at[h, b]),
-                Gather4("y", lambda h: to.at[2 + h, :, y], lambda b, h: to.at[2 + h, :, b])]
+    def up_second(to, n):
+        cs = pl.ds(n * (K // 2), K // 2)
+        return [Gather4("z", lambda h: to.at[h, z, :, :, cs], lambda b, h: to.at[h, b, :, :, cs]),
+                Gather4("y", lambda h: to.at[2 + h, :, y, :, cs], lambda b, h: to.at[2 + h, :, b, :, cs])]
 
     def up_unit(to, j):
         yj, zj = off(y, j), off(z, j)
@@ -258,8 +267,9 @@
             cpy.start()
         return sends
 
-    (d0a, d0b), (d1a, d1b) = down_gathers(0), down_gathers(1)
-    u0a, u1a, u1b = up_first(up[0]), up_first(up[1]), up_second(up[1])
+    (d0a, d0b, d0c, d0d), (d1a, d1b) = down_gathers(0, SPLIT3), down_gathers(1, WHOLE)
+    u0a, u1a = up_first(up[0]), up_first(up[1])
+    u1b, u1c = up_second(up[1], 0), up_second(up[1], 1)
     u0u = [up_unit(up[0], j) for j in (OWN, PRV, NXT, OPP)]
     ex0 = up_exchange(0)
     do(d0a, "start")
@@ -276,7 +286,6 @@
         cpy.wait_recv()
     do(u0a, "start")
     do(u0u[0], "start")
-    do(d0a, "finish")
     do(u0a, "forward")
     do(u0a, "neighbours")
     do(u0u[1], "start")
@@ -284,15 +293,16 @@
     do(u0u[0], "forward")
     do(u0a, "opposite")
     do(u0u[3], "start")
+    gx0.forward()
+    load_g.wait()
+    gg1.start()
     do(u0u[1], "forward")
     do(u0u[2], "forward")
-    gx0.forward()
+    gx0.sides()
+    do(d0a, "finish")
     do(u0u[3], "forward")
     do(d0b, "start")
-    gx0.sides()
     gx0.last()
-    load_g.wait()
-    gg1.start()
     gx0.wait_own()
     gx0.wait_push(range(len(gx0.push)))
     own_x.wait()
@@ -300,6 +310,8 @@
     save_x.start()
     for cpy in ex0 + ex1:
         cpy.wait_send()
+    own_u1.wait()
+    gg1.forward()
     for unit in u0u:
         do(unit, "finish")
     save_u0 = lcopy(U, wuh.at[0])
@@ -314,22 +326,18 @@
         return dot_nn(XV[t].reshape(T2, D), U[:, :, :, :, cols].reshape(D, NK)), cols
 
     def hidden0(t):
-        def body(n, carry):
+        for n in range(RING):
             pre, cols = up_tile(t, n)
             act, slope = gelu_parts(pre)
             AV[t, :, :, cols] = act.astype(BF16).reshape(2, TB, NK)
             SV[t, :, :, cols] = slope.reshape(2, TB, NK)
-            return carry
-        loop(K // NK, body, None)
-
-    def hidden1(t):
-        def body(n, carry):
+
+    def hidden1(t, part):
+        for n in (2 * part, 2 * part + 1):
             pre, cols = up_tile(t, n)
             act, slope = gelu_parts(pre)
             AV[t, :, :, cols] = act.astype(BF16).reshape(2, TB, NK)
             DV[t, :, cols] = (SV[t, :, :, cols].reshape(T2, NK) * slope).astype(BF16)
-            return carry
-        loop(K // NK, body, None)
 
     def dact(gv, t, n):
         return dot_nt(gv[t].reshape(T2, D), W[n].reshape(NK, D))
@@ -347,127 +355,136 @@
             return carry
         loop(RING, body, None)
 
-    def down_part(act, j):
-        t = off(x, j)
+    def down_part(act, j, lo, tiles):
+        t = lax.rem(x + j, RING)
 
         def body(n, carry):
-            cols = pl.ds(mo(n * ND, ND), ND)
+            cols = pl.ds(mo((lo + n) * ND, ND), ND)
             PP[j, :, :, cols] = dot_nn(act[t, :, :, 0:K].reshape(T2, K), W[:, :, :, cols].reshape(K, ND)).reshape(2, TB, ND)
             return carry
-        loop(RING, body, None)
-
-    def dx_part(j):
-        t = off(x, j)
+        loop(tiles, body, None)
+
+    def dx_part(j, lo, tiles):
+        t = lax.rem(x + j, RING)
 
         def body(n, carry):
-            cols = pl.ds(mo(n * ND, ND), ND)
-            PP[j, :, :, cols] = dot_nt(DV[t], U[n].reshape(ND, K)).reshape(2, TB, ND)
+            cols = pl.ds(mo((lo + n) * ND, ND), ND)
+            PP[j, :, :, cols] = dot_nt(DV[t], U[lo + n].reshape(ND, K)).reshape(2, TB, ND)
             return carry
-        loop(RING, body, None)
+        loop(tiles, body, None)
 
     class Reduce8:
-        def __init__(self, part, index, chunks=1):
-            self.part, self.index, self.chunks = part, index, chunks
+        def __init__(self, part, index, split):
+            self.part, self.index, self.split = part, index, split
             _, right, left = rings["x"]
             self.right, self.left = right, left
-            self.qb = HB // chunks
-            self.pair = [rcopy(PP.at[j, cp], DR.at[j], partner) for j in range(RING)]
-
-            def messages(q):
-                src = lambda j, h: PP.at[j, c, self.rows(q, h)]
-                dst = lambda k: XR.at[k, pl.ds(q * self.qb, self.qb)]
-                return [rcopy(src(OPP, 0), dst(0), right), rcopy(src(OPP, 1), dst(1), left),
-                        rcopy(src(NXT, 1), dst(2), right), rcopy(src(PRV, 0), dst(3), left),
-                        rcopy(src(NXT, 0), dst(4), right), rcopy(src(PRV, 1), dst(5), left)]
-            self.m = [messages(q) for q in range(chunks)]
-
-        def rows(self, q, h):
-            return pl.ds((2 * q + h) * self.qb, self.qb)
-
-        def credits(self):
-            if self.index:
-                for k in range(len((self.right, self.left, partner))):
-                    pl.semaphore_wait(credit.at[k], 1)
-
-        def compute(self, j):
-            self.part(j)
-            self.pair[j].start()
-
-        def combine(self, j):
-            self.pair[j].wait_recv()
-            add_rows(PP.at[j, c], [DR.at[j]], TB, min(TB, 16))
+            self.pair, self.m = [], []
+            for q in range(len(split)):
+                cq = self.cols(q)
+                self.pair.append((count[0], [rcopy(PP.at[j, cp, :, cq], DR.at[j, :, cq], partner) for j in range(RING)]))
+                src = lambda j, h: PP.at[j, c, half(h), cq]
+                self.m.append([rcopy(src(OPP, 0), XR.at[0, :, cq], right), rcopy(src(OPP, 1), XR.at[1, :, cq], left),
+                               rcopy(src(NXT, 1), XR.at[2, :, cq], right), rcopy(src(PRV, 0), XR.at[3, :, cq], left),
+                               rcopy(src(NXT, 0), XR.at[4, :, cq], right), rcopy(src(PRV, 1), XR.at[5, :, cq], left)])
+
+        def cols(self, q):
+            return tile_cols(self.split, q)
+
+        def compute(self, j, q):
+            self.part(j, sum(self.split[:q]), self.split[q])
+            self.pair[q][1][j].start()
+
+        def compute_all(self, q):
+            first, cq = self.pair[q][0], self.cols(q)
+
+            def body(i, carry):
+                j = lax.rem(i + 1, RING)
+                self.part(j, sum(self.split[:q]), self.split[q])
+                pltpu.make_async_remote_copy(src_ref=PP.at[j, cp, :, cq], dst_ref=DR.at[j, :, cq],
+                                             send_sem=ss.at[first + j], recv_sem=rs.at[first + j],
+                                             device_id=partner, device_id_type=MESH_ID).start()
+                return carry
+            loop(RING, body, None)
+
+        def combine(self, j, q):
+            self.pair[q][1][j].wait_recv()
+            add_rows(PP.at[j, c, :, self.cols(q)], [DR.at[j, :, self.cols(q)]], TB, min(TB, 16))
 
         def opposite(self, q):
             self.m[q][0].start()
             self.m[q][1].start()
 
-        def sides(self, q):
-            self.m[q][2].start()
-            self.m[q][3].start()
+        def side(self, j, q):
+            self.combine(j, q)
+            self.m[q][2 if j == NXT else 3].start()
+
+        def send(self, q):
+            self.combine(OPP, q)
+            self.opposite(q)
+            self.side(NXT, q)
+            self.side(PRV, q)
 
         def relay(self, q):
             for k, j, h in ((0, NXT, 0), (1, PRV, 1)):
                 self.m[q][k].wait_recv()
-                add_rows(PP.at[j, c, self.rows(q, h)], [XR.at[k, pl.ds(q * self.qb, self.qb)]], self.qb, min(self.qb, 16))
+                add_rows(PP.at[j, c, half(h), self.cols(q)], [XR.at[k, :, self.cols(q)]], HB, min(HB, 16))
                 self.m[q][4 + k].start()
 
         def finish(self, q, res, outs):
             for d in self.m[q][2:]:
                 d.wait_recv()
-            step = min(self.qb, 16)
+            step, cq = min(HB, 16), self.cols(q)
             for h, (kl, kr) in enumerate(((4, 3), (2, 5))):
                 def body(r, carry):
-                    lo = pl.ds(mo(q * self.qb + r * step, step), step)
-                    sl = pl.ds(mo((2 * q + h) * self.qb + r * step, step), step)
-                    tot = PP[OWN, c, sl, :] + (XR[kl, lo, :] + XR[kr, lo, :])
-                    val = (res[sl, :].astype(F32) + tot).astype(BF16)
+                    lo = pl.ds(mo(r * step, step), step)
+                    sl = pl.ds(mo(h * HB + r * step, step), step)
+                    tot = PP[OWN, c, sl, cq] + (XR[kl, lo, cq] + XR[kr, lo, cq])
+                    val = (res[sl, cq].astype(F32) + tot).astype(BF16)
                     for o in outs:
-                        o[sl, :] = val
+                        o[sl, cq] = val
                     return carry
-                loop(self.qb // step, body, None)
+                loop(HB // step, body, None)
+
+        def drain(self):
+            for d in sum([p[1] for p in self.pair] + self.m, []):
+                d.wait_send()
 
         def release(self):
-            for d in self.pair + sum(self.m, []):
-                d.wait_send()
+            self.drain()
             for k, to in enumerate((self.right, self.left, partner)):
                 pl.semaphore_signal(credit.at[k], inc=1, device_id=to, device_id_type=MESH_ID)
 
-        def drain(self):
-            for d in self.pair + sum(self.m, []):
-                d.wait_send()
-
-        def launch(self):
-            self.credits()
-            self.compute(OPP)
-            self.compute(NXT)
-            self.combine(OPP)
-            self.opposite(0)
-            self.compute(PRV)
-            self.combine(NXT)
-            self.combine(PRV)
-            self.sides(0)
-
-    def grad_a(j, dst):
+        def acquire(self):
+            for k in range(len((self.right, self.left, partner))):
+                pl.semaphore_wait(credit.at[k], 1)
+
+    def grad_a(j, dst, halves=None):
         t = off(z, j)
-        for h in HALVES:
+
+        def rows(h, carry):
             lo = [pl.ds(mo((2 * h + q) * XD + t * ZD, ZD), ZD) for q in HALVES]
             lhs = jnp.concatenate([XV[:, :, :, s].reshape(8 * TB, ZD) for s in lo], axis=1)
 
             def body(n, carry):
-                cols = pl.ds(mo(n * NK, NK), NK)
-                dst[h, :, :, cols] = dot_tn(lhs, DV[:, :, cols].reshape(8 * TB, NK)).reshape(2, ZD, NK)
+                cols = pl.ds(mo(n * ND, ND), ND)
+                dst[h, :, :, cols] = dot_tn(lhs, DV[:, :, cols].reshape(8 * TB, ND)).reshape(2, ZD, ND)
                 return carry
-            loop(K // NK, body, None)
+            return loop(K // ND, body, carry)
+        if halves is None:
+            loop(2, rows, None)
+        else:
+            for h in halves:
+                rows(h, None)
 
     def grad_b(gv, j, dst):
         cols_l = pl.ds(mo(off(y, j) * NK, NK), NK)
-        for n in HALVES:
-            def body(m, carry):
-                cols = pl.ds(mo(n * K + m * ND, ND), ND)
-                out = dot_tn(AV[:, :, :, cols_l].reshape(8 * TB, NK), gv[:, :, :, cols].reshape(8 * TB, ND))
-                dst[:, n, :, pl.ds(mo(m * ND, ND), ND)] = out.reshape(2, NK // 2, ND)
-                return carry
-            loop(2, body, None)
+
+        def body(m, carry):
+            cols = pl.ds(mo(m * ND, ND), ND)
+            out = dot_tn(AV[:, :, :, cols_l].reshape(8 * TB, NK), gv[:, :, :, cols].reshape(8 * TB, ND))
+            dst[:, m // 2, :, pl.ds(mo(lax.rem(m, 2) * ND, ND), ND)] = out.reshape(2, NK // 2, ND)
+            return carry
+        loop(RING, body, None)
 
     class Reduce4:
         def __init__(self, axis, part, recv, stage):
@@ -569,107 +586,127 @@
         for cpy in state[1]:
             cpy.wait()
 
-    hidden0(0)
     do(d0b, "forward")
-    do(d1a, "start")
-    for cpy in ex1:
-        cpy.wait_recv()
-    own_u1.wait()
-    own_d1.wait()
-    do(u1a, "start")
-    hidden0(1)
-    hidden0(2)
-    gg1.forward()
-    hidden0(3)
+    do(d0c, "start")
+    gx0.drain()
+    do(d0a, "drain")
+    save_x.wait()
+    r = Reduce8(functools.partial(down_part, AV), 0, SPLIT3)
+    hidden0(off(x, OPP))
+    do(d0b, "finish")
+    r.compute(OPP, 0)
+    hidden0(off(x, NXT))
+    do(d0c, "forward")
+    do(d0d, "start")
+    r.compute(NXT, 0)
+    r.combine(OPP, 0)
+    r.opposite(0)
+    hidden0(off(x, PRV))
+    r.compute(PRV, 0)
+    r.side(NXT, 0)
+    gg1.sides()
+    hidden0(off(x, OWN))
+    r.side(PRV, 0)
     save_s = lcopy(SV, sh0)
     save_s.start()
     save_a0 = lcopy(AV, ah.at[0])
     save_a0.start()
-    gg1.sides()
-    do(d0b, "finish")
+    do(d0d, "forward")
+    do(d1a, "start")
+    do(d0c, "finish")
+    r.compute_all(1)
+    r.relay(0)
+    r.send(1)
+    for cpy in ex1:
+        cpy.wait_recv()
+    own_d1.wait()
+    do(u1a, "start")
+    gg1.last()
+    do(d0d, "finish")
     save_d0 = lcopy(W, wdh.at[0])
     save_d0.start()
-    save_x.wait()
-    gx0.drain()
-    do(d0a, "drain")
-
-    r = Reduce8(functools.partial(down_part, AV), 0, 2)
-    r.compute(OPP)
+    r.compute_all(2)
     do(d1a, "forward")
-    r.compute(NXT)
-    r.combine(OPP)
-    r.opposite(0)
-    r.compute(PRV)
-    r.combine(NXT)
-    r.combine(PRV)
-    r.sides(0)
+    r.relay(1)
+    r.send(2)
     do(u1a, "forward")
-    gg1.last()
+    r.compute(OWN, 0)
     do(d1a, "finish")
     do(d1b, "start")
-    r.compute(OWN)
+    for q in range(len(SPLIT3)):
+        r.combine(OWN, q)
     do(u1a, "finish")
-    r.relay(0)
-    r.opposite(1)
-    r.sides(1)
-    r.combine(OWN)
-    do(d1b, "forward")
-    do(u1b, "start")
 
     def token_gathers(slot, buf):
-        rows = lambda q, h: pl.ds((2 * q + h) * r.qb, r.qb)
-        make = lambda q: Gather8(lambda h: RES.at[slot, rows(q, h)], lambda b, k, h: buf.at[b, k, rows(q, h)])
+        def make(q):
+            cq = tile_cols(SPLIT2, q)
+            return Gather8(lambda h: RES.at[slot, half(h), cq], lambda b, k, h: buf.at[b, k, half(h), cq])
         return [make(0), make(1)]
 
     gx1 = token_gathers(X1, XV)
-    r.relay(1)
     do(d1a, "drain")
-    r.finish(0, RES.at[X0], [RES.at[X1], XV.at[x, c]])
-    gx1[0].start()
+    for q in HALVES:
+        r.finish(q, RES.at[X0], [RES.at[X1], XV.at[x, c]])
     gg1.wait_own()
     gg1.wait_push(range(len(gg1.push)))
     own_g.wait()
+    do(d1b, "forward")
+    do(u1b, "start")
+    r.relay(2)
+    gx1[0].start()
     save_d0.wait()
-    do(d0b, "drain")
+    do(d0b + d0c + d0d, "drain")
     do(d1b, "finish")
     load_w1d = lcopy(wdh.at[1], W)
     load_w1d.start()
-    do(u1b, "forward")
-    r.finish(1, RES.at[X0], [RES.at[X1], XV.at[x, c]])
+    r.finish(2, RES.at[X0], [RES.at[X1], XV.at[x, c]])
     gx1[1].start()
     save_s.wait()
+    do(u1b, "forward")
+    do(u1c, "start")
+    gx1[0].forward()
     load_w1d.wait()
     dact1(off(x, OWN))
-    gx1[0].forward()
+    r.release()
     dact1(off(x, NXT))
     gx1[0].sides()
-    r.release()
     dact1(off(x, PRV))
+    save_u0.wait()
+    do(sum(u0u, u0a), "drain")
+    do(u1b, "finish")
+
+    def load_up(n):
+        cs = pl.ds(n * (K // 2), K // 2)
+        return lcopy(wuh.at[1, :, :, :, :, cs], U.at[:, :, :, :, cs])
+    load_w1u = [load_up(n) for n in HALVES]
+    load_w1u[0].start()
+    do(u1c, "forward")
     gx1[1].forward()
-    gx1[0].last()
     dact1(off(x, OPP))
     load_w0d_again = lcopy(wdh.at[0], W)
     load_w0d_again.start()
-    gx1[1].sides()
-    save_u0.wait()
-    do(sum(u0u, u0a), "drain")
-    do(u1b, "finish")
-    load_w1u = lcopy(wuh.at[1], U)
-    load_w1u.start()
-    load_w1u.wait()
     save_a0.wait()
     do(gx1, "wait_own")
-    hidden1(off(x, OWN))
+    load_w1u[0].wait()
+    hidden1(off(x, OWN), 0)
+    gx1[1].sides()
+    gx1[0].last()
+    do(u1c, "finish")
+    load_w1u[1].start()
+    for g in gx1:
+        g.wait_push((0, 2))
+    hidden1(off(x, PRV), 0)
     gx1[1].last()
     for g in gx1:
-        g.wait_push((0, 2))
-    hidden1(off(x, PRV))
-    for g in gx1:
         g.wait_push((1, 3))
-    hidden1(off(x, NXT))
+    hidden1(off(x, NXT), 0)
+    load_w1u[1].wait()
+    for j in (OWN, PRV, NXT):
+        hidden1(off(x, j), 1)
     for g in gx1:
         g.wait_push((4, 5))
-    hidden1(off(x, OPP))
+    for n in HALVES:
+        hidden1(off(x, OPP), n)
     load_s0 = lcopy(sh0, SV)
     load_s0.start()
     save_a1 = lcopy(AV, ah.at[1])
@@ -678,29 +715,39 @@
     a1, b1, a2, b2 = make_reduce(1, 0, 1)
     grad_b(GV1, OPP, GPB.at[OPP])
     b1.opposite()
-    grad_a(OPP, GPA.at[OPP])
-    a1.opposite()
-    r = Reduce8(dx_part, 1, 2)
-    r.launch()
+    for h in HALVES:
+        grad_a(OPP, GPA.at[OPP], (h,))
+        a1.m[h].start()
+    r = Reduce8(dx_part, 1, SPLIT2)
+    r.acquire()
+    r.compute(OPP, 0)
+    r.compute(NXT, 0)
+    r.combine(OPP, 0)
+    r.opposite(0)
+    r.compute(PRV, 0)
+    r.side(NXT, 0)
+    r.side(PRV, 0)
+    r.compute_all(1)
+    load_w0u_again = lcopy(wuh.at[0], U)
+    r.compute(OWN, 0)
+    load_w0u_again.start()
     grad_b(GV1, NXT, GPB.at[NXT])
     b1.sides(NXT)
     grad_b(GV1, PRV, GPB.at[PRV])
     b1.sides(PRV)
     r.relay(0)
-    r.opposite(1)
-    r.sides(1)
-    r.compute(OWN)
-    load_w0u_again = lcopy(wuh.at[0], U)
-    load_w0u_again.start()
+    r.send(1)
     grad_a(NXT, GPA.at[NXT])
     a1.sides(NXT)
     grad_a(PRV, GPA.at[PRV])
     a1.sides(PRV)
-    r.combine(OWN)
+    r.combine(OWN, 0)
+    r.combine(OWN, 1)
     gg0 = token_gathers(G0, GV0)
     r.relay(1)
     r.finish(0, RES.at[G1], [RES.at[G0], GV0.at[x, c]])
     gg0[0].start()
+    relay((b1, a1))
     grad_b(GV1, OWN, GPB.at[OWN])
     save_a1.wait()
     load_a0 = lcopy(ah.at[0], AV)
@@ -716,7 +763,6 @@
     load_x0 = lcopy(xh0, XV)
     load_x0.start()
     gg0[0].sides()
-    relay((b1, a1))
     r.release()
     gg0[1].forward()
     gg0[0].last()
@@ -743,13 +789,16 @@
     load_w1d_again = lcopy(wdh.at[1], W)
     load_w1d_again.start()
     load_x0.wait()
-    grad_a(OPP, GPA.at[OPP])
-    a1n[0].opposite()
-    load_w0u_again.wait()
-    r = Reduce8(dx_part, 2)
-    r.launch()
+    for h in HALVES:
+        grad_a(OPP, GPA.at[OPP], (h,))
+        a1n[0].m[h].start()
     arrive((b1, a1), EARLY + LATE)
     second_start((a2, b2))
+    load_w0u_again.wait()
+    r = Reduce8(dx_part, 2, WHOLE)
+    r.acquire()
+    r.compute_all(0)
+    r.send(0)
     grad_b(GV0, NXT, GPB.at[NXT])
     b1n[0].sides(NXT)
     grad_b(GV0, PRV, GPB.at[PRV])
@@ -765,8 +814,7 @@
         red.opposite()
         red.sides(NXT)
         red.sides(PRV)
-    r.compute(OWN)
-    r.combine(OWN)
+    r.combine(OWN, 0)
     grad_b(GV0, OWN, own_grads[0][1])
     grad_a(OWN, own_grads[0][0])
     r.finish(0, RES.at[G0], [RES.at[X0]])
@@ -776,25 +824,26 @@
     arrive((b1n[0], a1n[0]), EARLY)
     load_a1.wait()
     load_w1d_again.wait()
-    r = Reduce8(functools.partial(down_part, GV1), 3)
-    r.launch()
-    r.compute(OWN)
+    r = Reduce8(functools.partial(down_part, GV1), 3, WHOLE)
+    r.acquire()
+    r.compute_all(0)
+    r.send(0)
     arrive((b2, a2), EARLY)
     arrive((b2, a2), LATE)
     state1 = grads_out_start(1, 0, 1)
-    r.combine(OWN)
+    r.combine(OWN, 0)
     arrive((b1n[0], a1n[0]), LATE)
-    r.relay(0)
     relay((b1n[1], a1n[1]))
     second_start((a2n[0], b2n[0]))
+    r.relay(0)
     arrive((b1n[1], a1n[1]), EARLY)
-    relay((b2n[0], a2n[0]))
     arrive((b1n[1], a1n[1]), LATE)
     second_start((a2n[1], b2n[1]))
+    relay((b2n[0], a2n[0]))
     arrive((b2n[0], a2n[0]), EARLY)
+    relay((b2n[1], a2n[1]))
     arrive((b2n[0], a2n[0]), LATE)
     state0 = [grads_out_start(0, 0, 2)]
-    relay((b2n[1], a2n[1]))
     r.finish(0, RES.at[X1], [RES.at[G1]])
     write_y = lcopy(RES.at[G1], y_out)
     write_y.start()
@@ -803,7 +852,7 @@
     arrive((b2n[1], a2n[1]), LATE)
     state0.append(grads_out_start(0, 1, 2))
     r.drain()
-    do(d1b + u1a + u1b + gg0, "drain")
+    do(d1b + u1a + u1b + u1c + gg0, "drain")
     write_gi.wait()
     write_y.wait()
     for state in state0:

time: 324 us -> 302 us (0.932)
  Pallas kernels: 322 us -> 300 us
    pallas_call x1, Pallas kernels: 319 us -> 297 us  [device_step(): y_raw, gi_raw, gd_raw, *_, gu_raw = call(x_loc, up_loc, down_loc, g_loc)]
where the time goes in v3:
time: 302 us; the launch traced here: 301 us
  Pallas kernels  300 us (99%)
    pallas_call x1, Pallas kernels, device_step(): y_raw, gi_raw, gd_raw, *_, gu_raw = call(x_loc, up_loc, down_loc, g_loc)  297 us

profile of v3, /device:TPU:1, one launch (start us, length us, event | category | flops | bytes accessed | tf_op | source)
XLA Modules:
  0.0 300.9 jit_solution(17987062917216077239)
XLA Ops:
  0.6 296.8 %mlp_stack.1 = (bf16[128,2048]{1,0:T(8,128)(2,1)}, bf16[128,2048]{1,0:T(8,128)(2,1)}, f32[2,64,2048]{2,1,0:T(8,128)}, bf16[4,2,128,2048]{3,2,1,0:T(8,128)(2,1)},...) custom-call(bf16[128,2048]{1,0:T(8,128)(2,1)} %x_in.1, ...), custom_call_target="tpu_custom_call" | custom-call | tf_op jit(solution)/shard_map/mlp_stack/pallas_call | solution.py:936
  297.4 3.3 %write_out.1 = (bf16[128,2048]{1,0:T(8,128)(2,1)}, bf16[128,2048]{1,0:T(8,128)(2,1)}, f32[2,16,8192]{2,1,0:T(8,128)}, f32[2,64,2048]{2,1,0:T(8,128)}) custom-call(bf16[128,2048]{1,0:T(8,128)(2,1)} %get-tuple-element.8.y_in, bf16[128,2048]{1,0:T(8,128)(2,1)} %get-tuple-element.9.gi_in, f32[2,4,32,1024]{3,2,1,0:T(8,128)} %get-tuple-element.10.gu_in, ...), custom_call_target="tpu_custom_call" | custom-call | tf_op jit(solution)/shard_map/write_out/pallas_call | solution.py:939

commit v4 on v3

--- a/solution.py
+++ b/solution.py
@@ -16,8 +16,7 @@
 X0, X1, G1, G0 = range(RING)
 HALVES = (0, 1)
 WHOLE, SPLIT2, SPLIT3 = (4,), (2, 2), (1, 1, 2)
-N_SEM = 440
-N_LOCAL = 120
+N_RECV, N_SEND, N_LOCAL = 182, 110, 15
 
 
 def gelu_parts(pre_act):
@@ -46,7 +45,7 @@
            y_out, gi_out, gd_out,
            xh0, wuh, wdh, sh0, ah, ra1, rb1, ra2, rb2, uh,
            U, W, XV, GV1, GV0, SV, AV, DV, GPA, GPB, PP, DR, XR, RES, STA, STB,
-           ss, rs, ls, credit):
+           ss, rs, ls, ps, credit):
     D, K, TB, UR, DR_ROWS = dims
     HB = TB // 2
     x, z, y, c = (lax.axis_index(a) for a in ALL)
@@ -63,20 +62,52 @@
     rings = {"x": (x, dev(dx=1), dev(dx=-1)), "z": (z, dev(dz=1), dev(dz=-1)), "y": (y, dev(dy=1), dev(dy=-1))}
     off = lambda v, d: v if d == 0 else lax.rem(v + d, 4)
 
-    count = [0]
-
-    def rcopy(src, dst, to):
-        k = count[0]
-        count[0] += 1
-        return pltpu.make_async_remote_copy(src_ref=src, dst_ref=dst, send_sem=ss.at[k], recv_sem=rs.at[k],
+    used = {"recv": 0, "send": 0, "local": 0}
+    free = {"send": [], "local": []}
+    keys = []
+
+    def fresh(kind):
+        if kind == "recv" and keys:
+            return keys.pop()
+        used[kind] += 1
+        return used[kind] - 1
+
+    def take(kind):
+        return free[kind].pop() if free[kind] else fresh(kind)
+
+    def remote(src, dst, send, recv, to):
+        return pltpu.make_async_remote_copy(src_ref=src, dst_ref=dst, send_sem=send, recv_sem=recv,
                                             device_id=to, device_id_type=MESH_ID)
 
-    lcount = [0]
-
-    def lcopy(src, dst):
-        k = lcount[0]
-        lcount[0] += 1
-        return pltpu.make_async_copy(src, dst, ls.at[k])
+    class rcopy:
+        def __init__(self, src, dst, to, key=None):
+            self.args, self.key = (src, dst, to), fresh("recv") if key is None else key
+
+        def start(self):
+            src, dst, to = self.args
+            self.sem = take("send")
+            self.d = remote(src, dst, ss.at[self.sem], rs.at[self.key], to)
+            self.d.start()
+
+        def wait_recv(self):
+            self.d.wait_recv()
+
+        def wait_send(self):
+            self.d.wait_send()
+            free["send"].append(self.sem)
+
+    class lcopy:
+        def __init__(self, src, dst):
+            self.args = src, dst
+
+        def start(self):
+            self.sem = take("local")
+            self.d = pltpu.make_async_copy(*self.args, ls.at[self.sem])
+            self.d.start()
+
+        def wait(self):
+            self.d.wait()
+            free["local"].append(self.sem)
 
     def mo(v, m):
         return pl.multiple_of(v, m)
@@ -89,15 +120,22 @@
                       rcopy(src(0), dst(i, 0), left), rcopy(src(1), dst(i, 1), left),
                       rcopy(dst(lft, 0), dst(lft, 0), right), rcopy(dst(rgt, 1), dst(rgt, 1), left)]
 
+        def start_first(self):
+            self.d[0].start()
+            self.d[3].start()
+
+        def start_rest(self):
+            self.d[1].start()
+            self.d[2].start()
+
         def start(self):
-            for k in (0, 3, 1, 2):
-                self.d[k].start()
+            self.start_first()
+            self.start_rest()
 
         def forward(self):
-            self.d[0].wait_recv()
-            self.d[4].start()
-            self.d[3].wait_recv()
-            self.d[5].start()
+            for k in HALVES:
+                self.d[3 * k].wait_recv()
+                self.d[4 + k].start()
 
         def neighbours(self):
             self.d[1].wait_recv()
@@ -221,28 +259,29 @@
     down = [W, wdh.at[1]]
     hr = DR_ROWS // 4
 
-    def down_gathers(l, split):
-        def rows(q, h):
-            return pl.ds((2 * q + h) * hr, hr)
-
-        def src(q):
-            return lambda h: RES.at[X1, pl.ds(l * DR_ROWS + (2 * q + h) * hr, hr)]
+    def quarter(q, h):
+        return pl.ds((2 * q + h) * hr, hr)
+
+    def down_first(l):
         to = down[l]
-
-        def second(n):
-            cs = tile_cols(split, n)
-            return [Gather4("y", lambda h: to.at[y, :, rows(0, h), cs], lambda b, h: to.at[b, :, rows(0, h), cs]),
-                    Gather4("z", lambda h: to.at[:, z, rows(1, h), cs], lambda b, h: to.at[:, b, rows(1, h), cs])]
-        first = [Gather4("z", src(0), lambda b, h: to.at[y, b, rows(0, h)]),
-                 Gather4("y", src(1), lambda b, h: to.at[b, z, rows(1, h)])]
-        return [first] + [second(n) for n in range(len(split))]
+        src = lambda q: lambda h: RES.at[X1, pl.ds(l * DR_ROWS + (2 * q + h) * hr, hr)]
+        return [Gather4("z", src(0), lambda b, h: to.at[y, b, quarter(0, h)]),
+                Gather4("y", src(1), lambda b, h: to.at[b, z, quarter(1, h)])]
+
+    def down_second(l, split, n):
+        to, cs = down[l], tile_cols(split, n)
+        return [Gather4("y", lambda h: to.at[y, :, quarter(0, h), cs], lambda b, h: to.at[b, :, quarter(0, h), cs]),
+                Gather4("z", lambda h: to.at[:, z, quarter(1, h), cs], lambda b, h: to.at[:, b, quarter(1, h), cs])]
 
     def up_first(to):
         return [Gather4("y", lambda h: to.at[h, z, y], lambda b, h: to.at[h, z, b]),
                 Gather4("z", lambda h: to.at[2 + h, z, y], lambda b, h: to.at[2 + h, b, y])]
 
+    def hidden_cols(n):
+        return pl.ds(sum(SPLIT2[:n]) * (K // RING), SPLIT2[n] * (K // RING))
+
     def up_second(to, n):
-        cs = pl.ds(n * (K // 2), K // 2)
+        cs = hidden_cols(n)
         return [Gather4("z", lambda h: to.at[h, z, :, :, cs], lambda b, h: to.at[h, b, :, :, cs]),
                 Gather4("y", lambda h: to.at[2 + h, :, y, :, cs], lambda b, h: to.at[2 + h, :, b, :, cs])]
 
@@ -267,10 +306,18 @@
             cpy.start()
         return sends
 
-    (d0a, d0b, d0c, d0d), (d1a, d1b) = down_gathers(0, SPLIT3), down_gathers(1, WHOLE)
-    u0a, u1a = up_first(up[0]), up_first(up[1])
+    def keys_of(gathers):
+        return [d.key for g in gathers for d in g.d]
+
+    d0a, d0b, d0c = down_first(0), down_second(0, SPLIT3, 0), down_second(0, SPLIT3, 1)
+    u0a, u0u = up_first(up[0]), [up_unit(up[0], j) for j in (OWN, PRV, NXT, OPP)]
+    keys.extend(keys_of(u0a))
+    d0d = down_second(0, SPLIT3, 2)
+    keys.extend(keys_of(d0a))
+    d1a = down_first(1)
+    keys.extend(keys_of(sum(u0u, [])))
+    d1b, u1a = down_second(1, WHOLE, 0), up_first(up[1])
     u1b, u1c = up_second(up[1], 0), up_second(up[1], 1)
-    u0u = [up_unit(up[0], j) for j in (OWN, PRV, NXT, OPP)]
     ex0 = up_exchange(0)
     do(d0a, "start")
     gx0.start()
@@ -287,31 +334,38 @@
     do(u0a, "start")
     do(u0u[0], "start")
     do(u0a, "forward")
+    gx0.forward()
+    load_g.wait()
+    gg1.start()
     do(u0a, "neighbours")
     do(u0u[1], "start")
     do(u0u[2], "start")
     do(u0u[0], "forward")
     do(u0a, "opposite")
     do(u0u[3], "start")
-    gx0.forward()
-    load_g.wait()
-    gg1.start()
+    do(d0a, "finish")
     do(u0u[1], "forward")
     do(u0u[2], "forward")
+    do(d0b, "start_first")
     gx0.sides()
-    do(d0a, "finish")
+    for cpy in ex0 + ex1:
+        cpy.wait_send()
+    own_u1.wait()
     do(u0u[3], "forward")
-    do(d0b, "start")
+    do(u0a + d0a, "drain")
+    do(d0b, "start_rest")
+    do(d0c, "start_first")
+    gg1.forward()
+    do(d0b, "forward")
+    do(d0c, "start_rest")
+    do(d1a, "start")
     gx0.last()
     gx0.wait_own()
     gx0.wait_push(range(len(gx0.push)))
     own_x.wait()
     save_x = lcopy(XV, xh0)
     save_x.start()
-    for cpy in ex0 + ex1:
-        cpy.wait_send()
-    own_u1.wait()
-    gg1.forward()
+    gx0.drain()
     for unit in u0u:
         do(unit, "finish")
     save_u0 = lcopy(U, wuh.at[0])
@@ -333,7 +387,7 @@
             SV[t, :, :, cols] = slope.reshape(2, TB, NK)
 
     def hidden1(t, part):
-        for n in (2 * part, 2 * part + 1):
+        for n in range(sum(SPLIT2[:part]), sum(SPLIT2[:part + 1])):
             pre, cols = up_tile(t, n)
             act, slope = gelu_parts(pre)
             AV[t, :, :, cols] = act.astype(BF16).reshape(2, TB, NK)
@@ -374,40 +428,44 @@
         loop(tiles, body, None)
 
     class Reduce8:
-        def __init__(self, part, index, split):
+        def __init__(self, part, index, split, old=()):
             self.part, self.index, self.split = part, index, split
+            keys.extend(old)
             _, right, left = rings["x"]
             self.right, self.left = right, left
-            self.pair, self.m = [], []
+            self.pair, self.m, self.first = [], [], []
             for q in range(len(split)):
                 cq = self.cols(q)
-                self.pair.append((count[0], [rcopy(PP.at[j, cp, :, cq], DR.at[j, :, cq], partner) for j in range(RING)]))
+                first = sorted(fresh("recv") for j in range(RING))
+                self.pair.append([self.swap(j, q, first[0]) for j in range(RING)])
+                self.first.append(first[0])
                 src = lambda j, h: PP.at[j, c, half(h), cq]
                 self.m.append([rcopy(src(OPP, 0), XR.at[0, :, cq], right), rcopy(src(OPP, 1), XR.at[1, :, cq], left),
                                rcopy(src(NXT, 1), XR.at[2, :, cq], right), rcopy(src(PRV, 0), XR.at[3, :, cq], left),
                                rcopy(src(NXT, 0), XR.at[4, :, cq], right), rcopy(src(PRV, 1), XR.at[5, :, cq], left)])
+            keys.clear()
 
         def cols(self, q):
             return tile_cols(self.split, q)
 
+        def swap(self, j, q, first):
+            cq = self.cols(q)
+            return remote(PP.at[j, cp, :, cq], DR.at[j, :, cq], ps.at[q * RING + j], rs.at[first + j], partner)
+
         def compute(self, j, q):
             self.part(j, sum(self.split[:q]), self.split[q])
-            self.pair[q][1][j].start()
+            self.pair[q][j].start()
 
         def compute_all(self, q):
-            first, cq = self.pair[q][0], self.cols(q)
-
             def body(i, carry):
                 j = lax.rem(i + 1, RING)
                 self.part(j, sum(self.split[:q]), self.split[q])
-                pltpu.make_async_remote_copy(src_ref=PP.at[j, cp, :, cq], dst_ref=DR.at[j, :, cq],
-                                             send_sem=ss.at[first + j], recv_sem=rs.at[first + j],
-                                             device_id=partner, device_id_type=MESH_ID).start()
+                self.swap(j, q, self.first[q]).start()
                 return carry
             loop(RING, body, None)
 
         def combine(self, j, q):
-            self.pair[q][1][j].wait_recv()
+            self.pair[q][j].wait_recv()
             add_rows(PP.at[j, c, :, self.cols(q)], [DR.at[j, :, self.cols(q)]], TB, min(TB, 16))
 
         def opposite(self, q):
@@ -446,7 +504,7 @@
                 loop(HB // step, body, None)
 
         def drain(self):
-            for d in sum([p[1] for p in self.pair] + self.m, []):
+            for d in sum(self.pair + self.m, []):
                 d.wait_send()
 
         def release(self):
@@ -486,15 +544,17 @@
             return carry
         loop(RING, body, None)
 
+    grad_keys = [keys_of(sum(u0u, u0a) + d0a), [d.key for d in ex0 + ex1] + keys_of(d0b + d0c)]
+
     class Reduce4:
-        def __init__(self, axis, part, recv, stage):
+        def __init__(self, l, axis, part, recv, stage):
             _, right, left = rings[axis]
             self.part, self.recv, self.stage = part, recv, stage
-            self.m = [rcopy(part(OPP, 0), recv(0), right), rcopy(part(OPP, 1), recv(1), left),
-                      rcopy(part(NXT, 1), recv(2), right), rcopy(part(PRV, 0), recv(3), left),
-                      rcopy(part(NXT, 0), recv(4), right), rcopy(part(PRV, 1), recv(5), left)]
+            which = ((OPP, 0), (OPP, 1), (NXT, 1), (PRV, 0), (NXT, 0), (PRV, 1))
+            self.m = [rcopy(part(*which[k]), recv(k), left if k % 2 else right, grad_keys[l].pop())
+                      for k in range(ARRIVALS)]
             self.to = [(NXT, 0), (PRV, 1), (OWN, 1), (OWN, 0), (OWN, 0), (OWN, 1)]
-            self.loads = [lcopy(recv(k), stage(k)) for k in range(ARRIVALS)]
+            self.loads = [lcopy(recv(k), stage(k)) for k in range(ARRIVALS)] if stage else None
 
         def opposite(self):
             self.m[0].start()
@@ -506,12 +566,14 @@
         def fetch(self, k):
             self.m[k].wait_send()
             self.m[k].wait_recv()
-            self.loads[k].start()
+            if self.loads:
+                self.loads[k].start()
 
         def absorb(self, k):
-            self.loads[k].wait()
+            if self.loads:
+                self.loads[k].wait()
             dst = self.part(*self.to[k])
-            add_rows(dst, [self.stage(k)], dst.shape[1], min(dst.shape[1], 16))
+            add_rows(dst, [(self.stage or self.recv)(k)], dst.shape[1], min(dst.shape[1], 16))
 
     def arrive(reduces, ks):
         for k in ks:
@@ -552,10 +614,15 @@
         def part_b2(j, h):
             t = off(z, j)
             return own_b.at[t // 2, nb, pl.ds(mo(lax.rem(t, 2) * DR_ROWS + h * hq, hq), hq), :]
-        return (Reduce4("z", part_a, lambda k: ra1.at[l, k, :, :, ca], lambda k: part_a(*pick[k])),
-                Reduce4("y", part_b, lambda k: rb1.at[l, k, nb], lambda k: part_b(*pick[k])),
-                Reduce4("y", part_a2, lambda k: ra2.at[l, k, :, :, ca], lambda k: STA.at[k % 2, :, :, ca]),
-                Reduce4("z", part_b2, lambda k: rb2.at[l, k, nb], lambda k: STB.at[k % 2, nb]))
+        first = (Reduce4(l, "z", part_a, lambda k: ra1.at[l, k, :, :, ca], lambda k: part_a(*pick[k])),
+                 Reduce4(l, "y", part_b, lambda k: rb1.at[l, k, nb], lambda k: part_b(*pick[k])))
+        if q:
+            def third(k, rows):
+                return pl.ds((k // 2) * rows, rows)
+            return first + (Reduce4(l, "y", part_a2, lambda k: GPA.at[OWN, k % 2, :, third(k, 2 * UR), ca], None),
+                            Reduce4(l, "z", part_b2, lambda k: GPB.at[OWN, k % 2, nb, third(k, hq), :], None))
+        return first + (Reduce4(l, "y", part_a2, lambda k: ra2.at[l, k, :, :, ca], lambda k: STA.at[k % 2, :, :, ca]),
+                        Reduce4(l, "z", part_b2, lambda k: rb2.at[l, k, nb], lambda k: STB.at[k % 2, nb]))
 
     def second_start(reduces):
         for r in reduces:
@@ -570,7 +637,7 @@
         def rows_of(tx, tc):
             return own_a.at[tx // 2, lax.rem(tx, 2), pl.ds(mo((2 * y + tc) * UR, UR), UR), ca]
         to = uh.at[l, x, mine, ca]
-        sends = [rcopy(rows_of(off(x, dx), cp if dc else c), to, dev(dx=dx, dc=dc)) for dx, dc in group]
+        sends = [rcopy(rows_of(off(x, dx), cp if dc else c), to, dev(dx=dx, dc=dc), grad_keys[l].pop()) for dx, dc in group]
         local = [lcopy(rows_of(x, c), to)]
         for n in ((q,) if chunks == 2 else HALVES):
             local.append(lcopy(own_b.at[z // 2, n, pl.ds(mo(lax.rem(z, 2) * DR_ROWS, DR_ROWS), DR_ROWS), :],
@@ -586,56 +653,61 @@
         for cpy in state[1]:
             cpy.wait()
 
-    do(d0b, "forward")
-    do(d0c, "start")
-    gx0.drain()
-    do(d0a, "drain")
-    save_x.wait()
     r = Reduce8(functools.partial(down_part, AV), 0, SPLIT3)
+    r_keys = sorted([d.key for m in r.m for d in m] + [f + j for f in r.first for j in range(RING)])
     hidden0(off(x, OPP))
+    hidden0(off(x, NXT))
     do(d0b, "finish")
     r.compute(OPP, 0)
-    hidden0(off(x, NXT))
+    r.compute(NXT, 0)
     do(d0c, "forward")
     do(d0d, "start")
-    r.compute(NXT, 0)
     r.combine(OPP, 0)
     r.opposite(0)
+    do(sum(u0u, []), "drain")
     hidden0(off(x, PRV))
     r.compute(PRV, 0)
     r.side(NXT, 0)
-    gg1.sides()
+    do(d1a, "forward")
     hidden0(off(x, OWN))
     r.side(PRV, 0)
     save_s = lcopy(SV, sh0)
     save_s.start()
     save_a0 = lcopy(AV, ah.at[0])
     save_a0.start()
-    do(d0d, "forward")
-    do(d1a, "start")
+    gg1.sides()
     do(d0c, "finish")
     r.compute_all(1)
     r.relay(0)
-    r.send(1)
+    do(d0d, "forward")
     for cpy in ex1:
         cpy.wait_recv()
     own_d1.wait()
     do(u1a, "start")
+    r.send(1)
+    do(d1a, "finish")
+    do(d1b, "start")
     gg1.last()
+    save_x.wait()
     do(d0d, "finish")
     save_d0 = lcopy(W, wdh.at[0])
     save_d0.start()
-    r.compute_all(2)
-    do(d1a, "forward")
+    r.compute(OPP, 2)
     r.relay(1)
-    r.send(2)
     do(u1a, "forward")
+    r.compute(NXT, 2)
+    r.combine(OPP, 2)
+    r.opposite(2)
+    r.compute(PRV, 2)
+    r.side(NXT, 2)
+    r.compute(OWN, 2)
+    r.side(PRV, 2)
     r.compute(OWN, 0)
-    do(d1a, "finish")
-    do(d1b, "start")
     for q in range(len(SPLIT3)):
         r.combine(OWN, q)
-    do(u1a, "finish")
+
+    def gather_keys(gathers):
+        return [d.key for g in gathers for d in g.ring.d + g.own + g.push]
 
     def token_gathers(slot, buf):
         def make(q):
@@ -643,19 +715,23 @@
             return Gather8(lambda h: RES.at[slot, half(h), cq], lambda b, k, h: buf.at[b, k, half(h), cq])
         return [make(0), make(1)]
 
+    keys.extend(gather_keys((gx0,)))
     gx1 = token_gathers(X1, XV)
     do(d1a, "drain")
+    do(d1b, "forward")
     for q in HALVES:
         r.finish(q, RES.at[X0], [RES.at[X1], XV.at[x, c]])
+    r.relay(2)
+    gx1[0].start()
+    do(u1a, "finish")
+    do(u1b, "start")
+    do(u1c, "start_first")
     gg1.wait_own()
     gg1.wait_push(range(len(gg1.push)))
     own_g.wait()
-    do(d1b, "forward")
-    do(u1b, "start")
-    r.relay(2)
-    gx1[0].start()
     save_d0.wait()
     do(d0b + d0c + d0d, "drain")
+    gg1.drain()
     do(d1b, "finish")
     load_w1d = lcopy(wdh.at[1], W)
     load_w1d.start()
@@ -663,25 +739,23 @@
     gx1[1].start()
     save_s.wait()
     do(u1b, "forward")
-    do(u1c, "start")
-    gx1[0].forward()
+    do(u1c, "start_rest")
     load_w1d.wait()
     dact1(off(x, OWN))
+    gx1[0].forward()
     r.release()
     dact1(off(x, NXT))
     gx1[0].sides()
     dact1(off(x, PRV))
+    do(u1c, "forward")
     save_u0.wait()
-    do(sum(u0u, u0a), "drain")
     do(u1b, "finish")
 
     def load_up(n):
-        cs = pl.ds(n * (K // 2), K // 2)
+        cs = hidden_cols(n)
         return lcopy(wuh.at[1, :, :, :, :, cs], U.at[:, :, :, :, cs])
     load_w1u = [load_up(n) for n in HALVES]
     load_w1u[0].start()
-    do(u1c, "forward")
-    gx1[1].forward()
     dact1(off(x, OPP))
     load_w0d_again = lcopy(wdh.at[0], W)
     load_w0d_again.start()
@@ -689,20 +763,22 @@
     do(gx1, "wait_own")
     load_w1u[0].wait()
     hidden1(off(x, OWN), 0)
+    gx1[1].forward()
+    gx1[0].last()
     gx1[1].sides()
-    gx1[0].last()
     do(u1c, "finish")
     load_w1u[1].start()
     for g in gx1:
         g.wait_push((0, 2))
     hidden1(off(x, PRV), 0)
-    gx1[1].last()
     for g in gx1:
         g.wait_push((1, 3))
     hidden1(off(x, NXT), 0)
     load_w1u[1].wait()
-    for j in (OWN, PRV, NXT):
-        hidden1(off(x, j), 1)
+    hidden1(off(x, OWN), 1)
+    gx1[1].last()
+    hidden1(off(x, PRV), 1)
+    hidden1(off(x, NXT), 1)
     for g in gx1:
         g.wait_push((4, 5))
     for n in HALVES:
@@ -718,7 +794,7 @@
     for h in HALVES:
         grad_a(OPP, GPA.at[OPP], (h,))
         a1.m[h].start()
-    r = Reduce8(dx_part, 1, SPLIT2)
+    r = Reduce8(dx_part, 1, SPLIT2, r_keys)
     r.acquire()
     r.compute(OPP, 0)
     r.compute(NXT, 0)
@@ -743,6 +819,7 @@
     a1.sides(PRV)
     r.combine(OWN, 0)
     r.combine(OWN, 1)
+    keys.extend(gather_keys(gx1))
     gg0 = token_gathers(G0, GV0)
     r.relay(1)
     r.finish(0, RES.at[G1], [RES.at[G0], GV0.at[x, c]])
@@ -752,7 +829,7 @@
     save_a1.wait()
     load_a0 = lcopy(ah.at[0], AV)
     load_a0.start()
-    gg1.drain()
+    do(d1b + u1a + u1b + u1c, "drain")
     load_a1 = lcopy(ah.at[1], GV1.at[:, :, :, 0:K])
     load_a1.start()
     r.finish(1, RES.at[G1], [RES.at[G0], GV0.at[x, c]])
@@ -795,7 +872,7 @@
     arrive((b1, a1), EARLY + LATE)
     second_start((a2, b2))
     load_w0u_again.wait()
-    r = Reduce8(dx_part, 2, WHOLE)
+    r = Reduce8(dx_part, 2, WHOLE, r_keys)
     r.acquire()
     r.compute_all(0)
     r.send(0)
@@ -824,7 +901,7 @@
     arrive((b1n[0], a1n[0]), EARLY)
     load_a1.wait()
     load_w1d_again.wait()
-    r = Reduce8(functools.partial(down_part, GV1), 3, WHOLE)
+    r = Reduce8(functools.partial(down_part, GV1), 3, WHOLE, r_keys)
     r.acquire()
     r.compute_all(0)
     r.send(0)
@@ -833,6 +910,7 @@
     state1 = grads_out_start(1, 0, 1)
     r.combine(OWN, 0)
     arrive((b1n[0], a1n[0]), LATE)
+    grads_out_finish(state1)
     relay((b1n[1], a1n[1]))
     second_start((a2n[0], b2n[0]))
     r.relay(0)
@@ -842,22 +920,21 @@
     relay((b2n[0], a2n[0]))
     arrive((b2n[0], a2n[0]), EARLY)
     relay((b2n[1], a2n[1]))
+    arrive((b2n[1], a2n[1]), EARLY)
     arrive((b2n[0], a2n[0]), LATE)
     state0 = [grads_out_start(0, 0, 2)]
     r.finish(0, RES.at[X1], [RES.at[G1]])
     write_y = lcopy(RES.at[G1], y_out)
     write_y.start()
-    grads_out_finish(state1)
-    arrive((b2n[1], a2n[1]), EARLY)
     arrive((b2n[1], a2n[1]), LATE)
     state0.append(grads_out_start(0, 1, 2))
     r.drain()
-    do(d1b + u1a + u1b + u1c + gg0, "drain")
+    do(gg0, "drain")
     write_gi.wait()
     write_y.wait()
     for state in state0:
         grads_out_finish(state)
-    assert count[0] <= N_SEM and lcount[0] <= N_LOCAL
+    assert used["recv"] <= N_RECV and used["send"] <= N_SEND and used["local"] <= N_LOCAL
 
 
 def finish_kernel(y_in, gi_in, gu_in, gd_in, y_out, gi_out, gu_out, gd_out, ybuf, gibuf, gubuf, gdbuf, gushuf, sems):
@@ -872,9 +949,6 @@
         cpy.start()
     low = lax.broadcasted_iota(jnp.int32, (ur, s2), 1) < half
     swap = lambda v: pltpu.roll(v, half, 1)
-    for k in (1, 2, 3):
-        loads[k].wait()
-        stores[k].start()
     loads[0].wait()
     for l in range(layers):
         for b in range(RING):
@@ -886,6 +960,9 @@
                     gushuf[l, :, pl.ds(strip * s2, s2)] = jnp.where(low, t0, swap(t1))
                     gushuf[l, :, pl.ds((strip + RING) * s2, s2)] = jnp.where(low, swap(t0), t1)
     stores[0].start()
+    for k in (1, 2, 3):
+        loads[k].wait()
+        stores[k].start()
     for cpy in stores:
         cpy.wait()
 
@@ -919,7 +996,7 @@
             vm((RING, CORES, CORES, zd, k), F32), vm((RING, CORES, CORES, zd, k), F32),
             vm((RING, CORES, tb, dm), F32), vm((4, tb, dm), F32), vm((6, tb // 2, dm), F32),
             vm((4, tb, dm), BF16), vm((CORES, CORES, 2 * ur, k), F32), vm((CORES, CORES, 2 * ur, k), F32),
-            pltpu.SemaphoreType.DMA((N_SEM,)), pltpu.SemaphoreType.DMA((N_SEM,)), pltpu.SemaphoreType.DMA((N_LOCAL,)),
+            *[pltpu.SemaphoreType.DMA((n,)) for n in (N_SEND, N_RECV, N_LOCAL, len(SPLIT3) * RING)],
             pltpu.SemaphoreType.REGULAR((3,)),
         ]
         anyspec = pl.BlockSpec(memory_space=pl.ANY)

time: 302 us -> 310 us (1.026)
  Pallas kernels: 300 us -> 309 us
    pallas_call x1, Pallas kernels: 297 us -> 306 us  [device_step(): y_raw, gi_raw, gd_raw, *_, gu_raw = call(x_loc, up_loc, down_loc, g_loc)]
where the time goes in v4:
time: 310 us
  Pallas kernels  309 us (100%)
    pallas_call x1, Pallas kernels, device_step(): y_raw, gi_raw, gd_raw, *_, gu_raw = call(x_loc, up_loc, down_loc, g_loc)  306 us

profile of v4, /device:TPU:1, one launch (start us, length us, event | category | flops | bytes accessed | tf_op | source)
XLA Modules:
  0.0 309.8 jit_solution(10609236149194828423)
XLA Ops:
  0.6 305.7 %mlp_stack.1 = (bf16[128,2048]{1,0:T(8,128)(2,1)}, bf16[128,2048]{1,0:T(8,128)(2,1)}, f32[2,64,2048]{2,1,0:T(8,128)}, bf16[4,2,128,2048]{3,2,1,0:T(8,128)(2,1)},...) custom-call(bf16[128,2048]{1,0:T(8,128)(2,1)} %x_in.1, ...), custom_call_target="tpu_custom_call" | custom-call | tf_op jit(solution)/shard_map/mlp_stack/pallas_call | solution.py:1013
  306.3 3.3 %write_out.1 = (bf16[128,2048]{1,0:T(8,128)(2,1)}, bf16[128,2048]{1,0:T(8,128)(2,1)}, f32[2,16,8192]{2,1,0:T(8,128)}, f32[2,64,2048]{2,1,0:T(8,128)}) custom-call(bf16[128,2048]{1,0:T(8,128)(2,1)} %get-tuple-element.8.y_in, bf16[128,2048]{1,0:T(8,128)(2,1)} %get-tuple-element.9.gi_in, f32[2,4,32,1024]{3,2,1,0:T(8,128)} %get-tuple-element.10.gu_in, ...), custom_call_target="tpu_custom_call" | custom-call | tf_op jit(solution)/shard_map/write_out/pallas_call | solution.py:1016

commit v5 on v4

--- a/solution.py
+++ b/solution.py
@@ -899,15 +899,15 @@
     write_gi = lcopy(RES.at[X0], gi_out)
     write_gi.start()
     arrive((b1n[0], a1n[0]), EARLY)
+    arrive((b2, a2), EARLY)
+    arrive((b2, a2), LATE)
+    state1 = grads_out_start(1, 0, 1)
     load_a1.wait()
     load_w1d_again.wait()
     r = Reduce8(functools.partial(down_part, GV1), 3, WHOLE, r_keys)
     r.acquire()
     r.compute_all(0)
     r.send(0)
-    arrive((b2, a2), EARLY)
-    arrive((b2, a2), LATE)
-    state1 = grads_out_start(1, 0, 1)
     r.combine(OWN, 0)
     arrive((b1n[0], a1n[0]), LATE)
     grads_out_finish(state1)

time: 310 us -> 293 us (0.945)
  Pallas kernels: 309 us -> 292 us
    pallas_call x1, Pallas kernels: 306 us -> 289 us  [device_step(): y_raw, gi_raw, gd_raw, *_, gu_raw = call(x_loc, up_loc, down_loc, g_loc)]
where the time goes in v5:
time: 293 us
  Pallas kernels  292 us (100%)
    pallas_call x1, Pallas kernels, device_step(): y_raw, gi_raw, gd_raw, *_, gu_raw = call(x_loc, up_loc, down_loc, g_loc)  289 us

profile of v5, /device:TPU:1, one launch (start us, length us, event | category | flops | bytes accessed | tf_op | source)
XLA Modules:
  0.0 292.7 jit_solution(1035279259474684896)
XLA Ops:
  0.6 288.6 %mlp_stack.1 = (bf16[128,2048]{1,0:T(8,128)(2,1)}, bf16[128,2048]{1,0:T(8,128)(2,1)}, f32[2,64,2048]{2,1,0:T(8,128)}, bf16[4,2,128,2048]{3,2,1,0:T(8,128)(2,1)},...) custom-call(bf16[128,2048]{1,0:T(8,128)(2,1)} %x_in.1, ...), custom_call_target="tpu_custom_call" | custom-call | tf_op jit(solution)/shard_map/mlp_stack/pallas_call | solution.py:1013
  289.2 3.3 %write_out.1 = (bf16[128,2048]{1,0:T(8,128)(2,1)}, bf16[128,2048]{1,0:T(8,128)(2,1)}, f32[2,16,8192]{2,1,0:T(8,128)}, f32[2,64,2048]{2,1,0:T(8,128)}) custom-call(bf16[128,2048]{1,0:T(8,128)(2,1)} %get-tuple-element.8.y_in, bf16[128,2048]{1,0:T(8,128)(2,1)} %get-tuple-element.9.gi_in, f32[2,4,32,1024]{3,2,1,0:T(8,128)} %get-tuple-element.10.gu_in, ...), custom_call_target="tpu_custom_call" | custom-call | tf_op jit(solution)/shard_map/write_out/pallas_call | solution.py:1016

commit v6 on v5

--- a/solution.py
+++ b/solution.py
@@ -16,7 +16,11 @@
 X0, X1, G1, G0 = range(RING)
 HALVES = (0, 1)
 WHOLE, SPLIT2, SPLIT3 = (4,), (2, 2), (1, 1, 2)
-N_RECV, N_SEND, N_LOCAL = 182, 110, 15
+PIECES = ((OPP, 0), (OPP, 1), (NXT, 1), (PRV, 0), (NXT, 0), (PRV, 1))
+TARGETS = ((NXT, 0), (PRV, 1), (OWN, 1), (OWN, 0), (OWN, 0), (OWN, 1))
+EARLY, LATE = (2, 3), (4, 5)
+PUSHES = {PRV: (0, 2), NXT: (1, 3), OPP: (4, 5)}
+N_RECV, N_SEND, N_LOCAL = 187, 110, 15
 
 
 def gelu_parts(pre_act):
@@ -214,7 +218,7 @@
         loop(rows // step, body, None)
 
     barrier = pltpu.get_barrier_semaphore()
-    group = [(dx, dc) for dx in range(RING) for dc in HALVES if dx or dc]
+    group = [(dx, dc) for dx in (OPP, NXT, PRV, OWN) for dc in HALVES if dx or dc]
     peers = [dev(dx=dx, dc=dc) for dx, dc in group] + [rings[a][k] for a in "zy" for k in (1, 2)]
     for p in peers:
         pl.semaphore_signal(barrier, inc=1, device_id=p, device_id_type=MESH_ID)
@@ -440,9 +444,7 @@
                 self.pair.append([self.swap(j, q, first[0]) for j in range(RING)])
                 self.first.append(first[0])
                 src = lambda j, h: PP.at[j, c, half(h), cq]
-                self.m.append([rcopy(src(OPP, 0), XR.at[0, :, cq], right), rcopy(src(OPP, 1), XR.at[1, :, cq], left),
-                               rcopy(src(NXT, 1), XR.at[2, :, cq], right), rcopy(src(PRV, 0), XR.at[3, :, cq], left),
-                               rcopy(src(NXT, 0), XR.at[4, :, cq], right), rcopy(src(PRV, 1), XR.at[5, :, cq], left)])
+                self.m.append([rcopy(src(*PIECES[k]), XR.at[k, :, cq], left if k % 2 else right) for k in range(ARRIVALS)])
             keys.clear()
 
         def cols(self, q):
@@ -534,26 +536,28 @@
             for h in halves:
                 rows(h, None)
 
-    def grad_b(gv, j, dst):
+    def grad_b(gv, j, dst, lo=0, tiles=RING):
         cols_l = pl.ds(mo(off(y, j) * NK, NK), NK)
 
-        def body(m, carry):
+        def body(i, carry):
+            m = lo + i
             cols = pl.ds(mo(m * ND, ND), ND)
             out = dot_tn(AV[:, :, :, cols_l].reshape(8 * TB, NK), gv[:, :, :, cols].reshape(8 * TB, ND))
             dst[:, m // 2, :, pl.ds(mo(lax.rem(m, 2) * ND, ND), ND)] = out.reshape(2, NK // 2, ND)
             return carry
-        loop(RING, body, None)
+        loop(tiles, body, None)
 
     grad_keys = [keys_of(sum(u0u, u0a) + d0a), [d.key for d in ex0 + ex1] + keys_of(d0b + d0c)]
+
+    def grad_key(l):
+        return grad_keys[l].pop() if grad_keys[l] else fresh("recv")
 
     class Reduce4:
         def __init__(self, l, axis, part, recv, stage):
             _, right, left = rings[axis]
             self.part, self.recv, self.stage = part, recv, stage
-            which = ((OPP, 0), (OPP, 1), (NXT, 1), (PRV, 0), (NXT, 0), (PRV, 1))
-            self.m = [rcopy(part(*which[k]), recv(k), left if k % 2 else right, grad_keys[l].pop())
+            self.m = [rcopy(part(*PIECES[k]), recv(k), left if k % 2 else right, grad_key(l))
                       for k in range(ARRIVALS)]
-            self.to = [(NXT, 0), (PRV, 1), (OWN, 1), (OWN, 0), (OWN, 0), (OWN, 1)]
             self.loads = [lcopy(recv(k), stage(k)) for k in range(ARRIVALS)] if stage else None
 
         def opposite(self):
@@ -572,7 +576,7 @@
         def absorb(self, k):
             if self.loads:
                 self.loads[k].wait()
-            dst = self.part(*self.to[k])
+            dst = self.part(*TARGETS[k])
             add_rows(dst, [(self.stage or self.recv)(k)], dst.shape[1], min(dst.shape[1], 16))
 
     def arrive(reduces, ks):
@@ -592,37 +596,47 @@
                 r.absorb(k)
                 r.m[4 + k].start()
 
-    EARLY, LATE = (2, 3), (4, 5)
     hq = DR_ROWS // 2
     own_grads = [(SV.at[pl.ds(0, 2)], SV.at[pl.ds(2, 2)]), (GPA.at[OWN], GPB.at[OWN])]
 
-    def make_reduce(l, q, chunks):
-        own_a, own_b = own_grads[l]
+    def third(k, rows):
+        return pl.ds((k // 2) * rows, rows)
+
+    def reduce_a(l, q, chunks):
+        own = own_grads[l][0]
         ca = pl.ds(q * (K // chunks), K // chunks)
-        nb = pl.ds(q, 1) if chunks == 2 else pl.ds(0, 2)
-        pick = ((OPP, 0), (OPP, 1), (NXT, 1), (PRV, 0), (NXT, 0), (PRV, 1))
-
-        def part_a(j, h):
-            return (own_a.at[h, :, :, ca] if j == OWN else GPA.at[j, h, :, :, ca])
-
-        def part_b(j, h):
-            return (own_b.at[h, nb] if j == OWN else GPB.at[j, h, nb])
-
-        def part_a2(j, h):
-            return own_a.at[h, :, pl.ds(mo(off(y, j) * 2 * UR, 2 * UR), 2 * UR), ca]
-
-        def part_b2(j, h):
+
+        def part(j, h):
+            return (own if j == OWN else GPA.at[j]).at[h, :, :, ca]
+
+        def part2(j, h):
+            return own.at[h, :, pl.ds(mo(off(y, j) * 2 * UR, 2 * UR), 2 * UR), ca]
+        if l < q:
+            second = lambda k: GPA.at[OWN, k % 2, :, third(k, 2 * UR), ca], None
+        else:
+            second = lambda k: ra2.at[l, k, :, :, ca], lambda k: STA.at[k % 2, :, :, ca]
+        return (Reduce4(l, "z", part, lambda k: ra1.at[l, k, :, :, ca], lambda k: part(*PIECES[k])),
+                Reduce4(l, "y", part2, *second))
+
+    def reduce_b(l, q):
+        own, nb = own_grads[l][1], pl.ds(q, 1)
+
+        def part(j, h):
+            return (own if j == OWN else GPB.at[j]).at[h, nb]
+
+        def part2(j, h):
             t = off(z, j)
-            return own_b.at[t // 2, nb, pl.ds(mo(lax.rem(t, 2) * DR_ROWS + h * hq, hq), hq), :]
-        first = (Reduce4(l, "z", part_a, lambda k: ra1.at[l, k, :, :, ca], lambda k: part_a(*pick[k])),
-                 Reduce4(l, "y", part_b, lambda k: rb1.at[l, k, nb], lambda k: part_b(*pick[k])))
-        if q:
-            def third(k, rows):
-                return pl.ds((k // 2) * rows, rows)
-            return first + (Reduce4(l, "y", part_a2, lambda k: GPA.at[OWN, k % 2, :, third(k, 2 * UR), ca], None),
-                            Reduce4(l, "z", part_b2, lambda k: GPB.at[OWN, k % 2, nb, third(k, hq), :], None))
-        return first + (Reduce4(l, "y", part_a2, lambda k: ra2.at[l, k, :, :, ca], lambda k: STA.at[k % 2, :, :, ca]),
-                        Reduce4(l, "z", part_b2, lambda k: rb2.at[l, k, nb], lambda k: STB.at[k % 2, nb]))
+            return own.at[t // 2, nb, pl.ds(mo(lax.rem(t, 2) * DR_ROWS + h * hq, hq), hq), :]
+        if l < q:
+            second = lambda k: GPB.at[OWN, k % 2, nb, third(k, hq), :], None
+        else:
+            second = lambda k: rb2.at[l, k, nb], lambda k: STB.at[k % 2, nb]
+        return (Reduce4(l, "y", part, lambda k: rb1.at[l, k, nb], lambda k: part(*PIECES[k])),
+                Reduce4(l, "z", part2, *second))
+
+    def sides(reduces, j):
+        for r in reduces:
+            r.sides(j)
 
     def second_start(reduces):
         for r in reduces:
@@ -630,21 +644,24 @@
             r.sides(NXT)
             r.sides(PRV)
 
-    def grads_out_start(l, q, chunks):
-        own_a, own_b = own_grads[l]
+    def up_out(l, q, chunks):
+        own = own_grads[l][0]
         ca = pl.ds(q * (K // chunks), K // chunks)
 
         def rows_of(tx, tc):
-            return own_a.at[tx // 2, lax.rem(tx, 2), pl.ds(mo((2 * y + tc) * UR, UR), UR), ca]
+            return own.at[tx // 2, lax.rem(tx, 2), pl.ds(mo((2 * y + tc) * UR, UR), UR), ca]
         to = uh.at[l, x, mine, ca]
-        sends = [rcopy(rows_of(off(x, dx), cp if dc else c), to, dev(dx=dx, dc=dc), grad_keys[l].pop()) for dx, dc in group]
+        sends = [rcopy(rows_of(off(x, dx), cp if dc else c), to, dev(dx=dx, dc=dc), grad_key(l)) for dx, dc in group]
         local = [lcopy(rows_of(x, c), to)]
-        for n in ((q,) if chunks == 2 else HALVES):
-            local.append(lcopy(own_b.at[z // 2, n, pl.ds(mo(lax.rem(z, 2) * DR_ROWS, DR_ROWS), DR_ROWS), :],
-                               gd_out.at[l, :, pl.ds(n * K, K)]))
         for cpy in sends + local:
             cpy.start()
         return sends, local
+
+    def down_out(l, n):
+        cpy = lcopy(own_grads[l][1].at[z // 2, n, pl.ds(mo(lax.rem(z, 2) * DR_ROWS, DR_ROWS), DR_ROWS), :],
+                    gd_out.at[l, :, pl.ds(n * K, K)])
+        cpy.start()
+        return [], [cpy]
 
     def grads_out_finish(state):
         for cpy in state[0]:
@@ -763,24 +780,22 @@
     do(gx1, "wait_own")
     load_w1u[0].wait()
     hidden1(off(x, OWN), 0)
-    gx1[1].forward()
+    do(gx1[1:], "forward")
+    do(gx1[1:], "sides")
+    for j in (PRV, NXT):
+        for g in gx1:
+            g.wait_push(PUSHES[j])
+        hidden1(off(x, j), 0)
     gx1[0].last()
-    gx1[1].sides()
     do(u1c, "finish")
     load_w1u[1].start()
-    for g in gx1:
-        g.wait_push((0, 2))
-    hidden1(off(x, PRV), 0)
-    for g in gx1:
-        g.wait_push((1, 3))
-    hidden1(off(x, NXT), 0)
     load_w1u[1].wait()
     hidden1(off(x, OWN), 1)
     gx1[1].last()
     hidden1(off(x, PRV), 1)
     hidden1(off(x, NXT), 1)
     for g in gx1:
-        g.wait_push((4, 5))
+        g.wait_push(PUSHES[OPP])
     for n in HALVES:
         hidden1(off(x, OPP), n)
     load_s0 = lcopy(sh0, SV)
@@ -788,12 +803,15 @@
     save_a1 = lcopy(AV, ah.at[1])
     save_a1.start()
 
-    a1, b1, a2, b2 = make_reduce(1, 0, 1)
-    grad_b(GV1, OPP, GPB.at[OPP])
-    b1.opposite()
+    (a1, a2), (b1, b2) = reduce_a(1, 0, 1), zip(*[reduce_b(1, q) for q in HALVES])
+    first1, second1 = (*b1, a1), (*b2, a2)
+    grad_b(GV1, OPP, GPB.at[OPP], 0, 2)
+    b1[0].opposite()
     for h in HALVES:
         grad_a(OPP, GPA.at[OPP], (h,))
         a1.m[h].start()
+    grad_b(GV1, OPP, GPB.at[OPP], 2, 2)
+    b1[1].opposite()
     r = Reduce8(dx_part, 1, SPLIT2, r_keys)
     r.acquire()
     r.compute(OPP, 0)
@@ -808,9 +826,9 @@
     r.compute(OWN, 0)
     load_w0u_again.start()
     grad_b(GV1, NXT, GPB.at[NXT])
-    b1.sides(NXT)
+    sides(b1, NXT)
     grad_b(GV1, PRV, GPB.at[PRV])
-    b1.sides(PRV)
+    sides(b1, PRV)
     r.relay(0)
     r.send(1)
     grad_a(NXT, GPA.at[NXT])
@@ -824,7 +842,7 @@
     r.relay(1)
     r.finish(0, RES.at[G1], [RES.at[G0], GV0.at[x, c]])
     gg0[0].start()
-    relay((b1, a1))
+    relay(first1)
     grad_b(GV1, OWN, GPB.at[OWN])
     save_a1.wait()
     load_a0 = lcopy(ah.at[0], AV)
@@ -850,15 +868,15 @@
     gg0[1].sides()
     gg0[1].last()
     for g in gg0:
-        g.wait_push((0, 2))
+        g.wait_push(PUSHES[PRV])
     dact0(off(x, PRV))
     for g in gg0:
-        g.wait_push((1, 3))
+        g.wait_push(PUSHES[NXT])
     dact0(off(x, NXT))
     for g in gg0:
-        g.wait_push((4, 5))
-
-    a1n, b1n, a2n, b2n = zip(*[make_reduce(0, q, 2) for q in HALVES])
+        g.wait_push(PUSHES[OPP])
+
+    (a1n, a2n), (b1n, b2n) = zip(*[reduce_a(0, q, 2) for q in HALVES]), zip(*[reduce_b(0, q) for q in HALVES])
     load_a0.wait()
     grad_b(GV0, OPP, GPB.at[OPP])
     b1n[0].opposite()
@@ -869,8 +887,8 @@
     for h in HALVES:
         grad_a(OPP, GPA.at[OPP], (h,))
         a1n[0].m[h].start()
-    arrive((b1, a1), EARLY + LATE)
-    second_start((a2, b2))
+    arrive(first1, EARLY + LATE)
+    second_start(second1)
     load_w0u_again.wait()
     r = Reduce8(dx_part, 2, WHOLE, r_keys)
     r.acquire()
@@ -884,7 +902,7 @@
     a1n[0].sides(NXT)
     grad_a(PRV, GPA.at[PRV])
     a1n[0].sides(PRV)
-    relay((b2, a2))
+    relay(second1)
     r.relay(0)
     relay((b1n[0], a1n[0]))
     for red in (b1n[1], a1n[1]):
@@ -899,9 +917,9 @@
     write_gi = lcopy(RES.at[X0], gi_out)
     write_gi.start()
     arrive((b1n[0], a1n[0]), EARLY)
-    arrive((b2, a2), EARLY)
-    arrive((b2, a2), LATE)
-    state1 = grads_out_start(1, 0, 1)
+    arrive(second1, EARLY)
+    arrive(second1, LATE)
+    state1 = [up_out(1, 0, 1)] + [down_out(1, n) for n in HALVES]
     load_a1.wait()
     load_w1d_again.wait()
     r = Reduce8(functools.partial(down_part, GV1), 3, WHOLE, r_keys)
@@ -910,24 +928,33 @@
     r.send(0)
     r.combine(OWN, 0)
     arrive((b1n[0], a1n[0]), LATE)
-    grads_out_finish(state1)
+    for state in state1:
+        grads_out_finish(state)
     relay((b1n[1], a1n[1]))
     second_start((a2n[0], b2n[0]))
     r.relay(0)
     arrive((b1n[1], a1n[1]), EARLY)
     arrive((b1n[1], a1n[1]), LATE)
-    second_start((a2n[1], b2n[1]))
+    last = (a2n[1], b2n[1])
+    for red in last:
+        red.opposite()
     relay((b2n[0], a2n[0]))
+    sides(last, NXT)
+    sides(last, PRV)
     arrive((b2n[0], a2n[0]), EARLY)
     relay((b2n[1], a2n[1]))
-    arrive((b2n[1], a2n[1]), EARLY)
-    arrive((b2n[0], a2n[0]), LATE)
-    state0 = [grads_out_start(0, 0, 2)]
+    arrive((a2n[0],), LATE)
+    state0 = [up_out(0, 0, 2)]
+    arrive((b2n[0],), LATE)
+    state0.append(down_out(0, 0))
+    arrive((a2n[1], b2n[1]), EARLY)
     r.finish(0, RES.at[X1], [RES.at[G1]])
     write_y = lcopy(RES.at[G1], y_out)
     write_y.start()
-    arrive((b2n[1], a2n[1]), LATE)
-    state0.append(grads_out_start(0, 1, 2))
+    arrive((a2n[1],), LATE)
+    state0.append(up_out(0, 1, 2))
+    arrive((b2n[1],), LATE)
+    state0.append(down_out(0, 1))
     r.drain()
     do(gg0, "drain")
     write_gi.wait()
@@ -960,7 +987,7 @@
                     gushuf[l, :, pl.ds(strip * s2, s2)] = jnp.where(low, t0, swap(t1))
                     gushuf[l, :, pl.ds((strip + RING) * s2, s2)] = jnp.where(low, swap(t0), t1)
     stores[0].start()
-    for k in (1, 2, 3):
+    for k in range(1, len(loads)):
         loads[k].wait()
         stores[k].start()
     for cpy in stores:

time: 293 us -> 289 us (0.986)
  Pallas kernels: 292 us -> 288 us
    pallas_call x1, Pallas kernels: 289 us -> 284 us  [device_step(): y_raw, gi_raw, gd_raw, *_, gu_raw = call(x_loc, up_loc, down_loc, g_loc)]
where the time goes in v6:
time: 289 us; the launch traced here: 288 us
  Pallas kernels  288 us (100%)
    pallas_call x1, Pallas kernels, device_step(): y_raw, gi_raw, gd_raw, *_, gu_raw = call(x_loc, up_loc, down_loc, g_loc)  284 us

profile of v6, /device:TPU:1, one launch (start us, length us, event | category | flops | bytes accessed | tf_op | source)
XLA Modules:
  0.0 288.3 jit_solution(9280110997819816450)
XLA Ops:
  0.6 284.2 %mlp_stack.1 = (bf16[128,2048]{1,0:T(8,128)(2,1)}, bf16[128,2048]{1,0:T(8,128)(2,1)}, f32[2,64,2048]{2,1,0:T(8,128)}, bf16[4,2,128,2048]{3,2,1,0:T(8,128)(2,1)},...) custom-call(bf16[128,2048]{1,0:T(8,128)(2,1)} %x_in.1, ...), custom_call_target="tpu_custom_call" | custom-call | tf_op jit(solution)/shard_map/mlp_stack/pallas_call | solution.py:1040
  284.9 3.3 %write_out.1 = (bf16[128,2048]{1,0:T(8,128)(2,1)}, bf16[128,2048]{1,0:T(8,128)(2,1)}, f32[2,16,8192]{2,1,0:T(8,128)}, f32[2,64,2048]{2,1,0:T(8,128)}) custom-call(bf16[128,2048]{1,0:T(8,128)(2,1)} %get-tuple-element.8.y_in, bf16[128,2048]{1,0:T(8,128)(2,1)} %get-tuple-element.9.gi_in, f32[2,4,32,1024]{3,2,1,0:T(8,128)} %get-tuple-element.10.gu_in, ...), custom_call_target="tpu_custom_call" | custom-call | tf_op jit(solution)/shard_map/write_out/pallas_call | solution.py:1043

commit v7 on v6

--- a/solution.py
+++ b/solution.py
@@ -20,7 +20,7 @@
 TARGETS = ((NXT, 0), (PRV, 1), (OWN, 1), (OWN, 0), (OWN, 0), (OWN, 1))
 EARLY, LATE = (2, 3), (4, 5)
 PUSHES = {PRV: (0, 2), NXT: (1, 3), OPP: (4, 5)}
-N_RECV, N_SEND, N_LOCAL = 187, 110, 15
+N_RECV, N_SEND, N_LOCAL = 206, 110, 19
 
 
 def gelu_parts(pre_act):
@@ -284,10 +284,10 @@
     def hidden_cols(n):
         return pl.ds(sum(SPLIT2[:n]) * (K // RING), SPLIT2[n] * (K // RING))
 
-    def up_second(to, n):
-        cs = hidden_cols(n)
-        return [Gather4("z", lambda h: to.at[h, z, :, :, cs], lambda b, h: to.at[h, b, :, :, cs]),
-                Gather4("y", lambda h: to.at[2 + h, :, y, :, cs], lambda b, h: to.at[2 + h, :, b, :, cs])]
+    def up_second(n):
+        cs, src = hidden_cols(n), up[1]
+        return [Gather4("z", lambda h: src.at[h, z, :, :, cs], lambda b, h: U.at[h, b, :, :, cs]),
+                Gather4("y", lambda h: src.at[2 + h, :, y, :, cs], lambda b, h: U.at[2 + h, :, b, :, cs])]
 
     def up_unit(to, j):
         yj, zj = off(y, j), off(z, j)
@@ -321,7 +321,7 @@
     d1a = down_first(1)
     keys.extend(keys_of(sum(u0u, [])))
     d1b, u1a = down_second(1, WHOLE, 0), up_first(up[1])
-    u1b, u1c = up_second(up[1], 0), up_second(up[1], 1)
+    u1b, u1c = up_second(0), up_second(1)
     ex0 = up_exchange(0)
     do(d0a, "start")
     gx0.start()
@@ -390,12 +390,15 @@
             AV[t, :, :, cols] = act.astype(BF16).reshape(2, TB, NK)
             SV[t, :, :, cols] = slope.reshape(2, TB, NK)
 
+    def hidden1_tile(t, n):
+        pre, cols = up_tile(t, n)
+        act, slope = gelu_parts(pre)
+        AV[t, :, :, cols] = act.astype(BF16).reshape(2, TB, NK)
+        DV[t, :, cols] = (SV[t, :, :, cols].reshape(T2, NK) * slope).astype(BF16)
+
     def hidden1(t, part):
         for n in range(sum(SPLIT2[:part]), sum(SPLIT2[:part + 1])):
-            pre, cols = up_tile(t, n)
-            act, slope = gelu_parts(pre)
-            AV[t, :, :, cols] = act.astype(BF16).reshape(2, TB, NK)
-            DV[t, :, cols] = (SV[t, :, :, cols].reshape(T2, NK) * slope).astype(BF16)
+            hidden1_tile(t, n)
 
     def dact(gv, t, n):
         return dot_nt(gv[t].reshape(T2, D), W[n].reshape(NK, D))
@@ -518,7 +521,7 @@
             for k in range(len((self.right, self.left, partner))):
                 pl.semaphore_wait(credit.at[k], 1)
 
-    def grad_a(j, dst, halves=None):
+    def grad_a(j, dst, halves=None, q=None):
         t = off(z, j)
 
         def rows(h, carry):
@@ -529,7 +532,7 @@
                 cols = pl.ds(mo(n * ND, ND), ND)
                 dst[h, :, :, cols] = dot_tn(lhs, DV[:, :, cols].reshape(8 * TB, ND)).reshape(2, ZD, ND)
                 return carry
-            return loop(K // ND, body, carry)
+            return loop(K // ND, body, carry) if q is None else body(q, carry)
         if halves is None:
             loop(2, rows, None)
         else:
@@ -711,6 +714,7 @@
     save_d0.start()
     r.compute(OPP, 2)
     r.relay(1)
+    save_u0.wait()
     do(u1a, "forward")
     r.compute(NXT, 2)
     r.combine(OPP, 2)
@@ -743,6 +747,10 @@
     do(u1a, "finish")
     do(u1b, "start")
     do(u1c, "start_first")
+    pair, rest = pl.ds(0, 2), pl.ds(2, 2)
+    own_up = [lcopy(up[1].at[pair, z], U.at[pair, z]), lcopy(up[1].at[rest, :, y], U.at[rest, :, y])]
+    for cpy in own_up:
+        cpy.start()
     gg1.wait_own()
     gg1.wait_push(range(len(gg1.push)))
     own_g.wait()
@@ -765,20 +773,14 @@
     gx1[0].sides()
     dact1(off(x, PRV))
     do(u1c, "forward")
-    save_u0.wait()
     do(u1b, "finish")
-
-    def load_up(n):
-        cs = hidden_cols(n)
-        return lcopy(wuh.at[1, :, :, :, :, cs], U.at[:, :, :, :, cs])
-    load_w1u = [load_up(n) for n in HALVES]
-    load_w1u[0].start()
     dact1(off(x, OPP))
     load_w0d_again = lcopy(wdh.at[0], W)
     load_w0d_again.start()
     save_a0.wait()
     do(gx1, "wait_own")
-    load_w1u[0].wait()
+    for cpy in own_up:
+        cpy.wait()
     hidden1(off(x, OWN), 0)
     do(gx1[1:], "forward")
     do(gx1[1:], "sides")
@@ -788,28 +790,28 @@
         hidden1(off(x, j), 0)
     gx1[0].last()
     do(u1c, "finish")
-    load_w1u[1].start()
-    load_w1u[1].wait()
     hidden1(off(x, OWN), 1)
+    hidden1(off(x, PRV), 1)
     gx1[1].last()
-    hidden1(off(x, PRV), 1)
     hidden1(off(x, NXT), 1)
     for g in gx1:
         g.wait_push(PUSHES[OPP])
-    for n in HALVES:
-        hidden1(off(x, OPP), n)
+    hidden1_tile(off(x, OPP), off(y, OPP))
+
+    (a1, a2), (b1, b2) = zip(*[reduce_a(1, q, 2) for q in HALVES]), zip(*[reduce_b(1, q) for q in HALVES])
+    first1, second1 = b1 + a1, b2 + a2
+    grad_b(GV1, OPP, GPB.at[OPP], 0, 2)
+    b1[0].opposite()
+    for n in (PRV, OWN, NXT):
+        hidden1_tile(off(x, OPP), off(y, n))
+    for q in HALVES:
+        for h in HALVES:
+            grad_a(OPP, GPA.at[OPP], (h,), q)
+            a1[q].m[h].start()
     load_s0 = lcopy(sh0, SV)
     load_s0.start()
     save_a1 = lcopy(AV, ah.at[1])
     save_a1.start()
-
-    (a1, a2), (b1, b2) = reduce_a(1, 0, 1), zip(*[reduce_b(1, q) for q in HALVES])
-    first1, second1 = (*b1, a1), (*b2, a2)
-    grad_b(GV1, OPP, GPB.at[OPP], 0, 2)
-    b1[0].opposite()
-    for h in HALVES:
-        grad_a(OPP, GPA.at[OPP], (h,))
-        a1.m[h].start()
     grad_b(GV1, OPP, GPB.at[OPP], 2, 2)
     b1[1].opposite()
     r = Reduce8(dx_part, 1, SPLIT2, r_keys)
@@ -824,6 +826,7 @@
     r.compute_all(1)
     load_w0u_again = lcopy(wuh.at[0], U)
     r.compute(OWN, 0)
+    do(u1b + u1c, "drain")
     load_w0u_again.start()
     grad_b(GV1, NXT, GPB.at[NXT])
     sides(b1, NXT)
@@ -832,9 +835,9 @@
     r.relay(0)
     r.send(1)
     grad_a(NXT, GPA.at[NXT])
-    a1.sides(NXT)
+    sides(a1, NXT)
     grad_a(PRV, GPA.at[PRV])
-    a1.sides(PRV)
+    sides(a1, PRV)
     r.combine(OWN, 0)
     r.combine(OWN, 1)
     keys.extend(gather_keys(gx1))
@@ -847,7 +850,7 @@
     save_a1.wait()
     load_a0 = lcopy(ah.at[0], AV)
     load_a0.start()
-    do(d1b + u1a + u1b + u1c, "drain")
+    do(d1b + u1a, "drain")
     load_a1 = lcopy(ah.at[1], GV1.at[:, :, :, 0:K])
     load_a1.start()
     r.finish(1, RES.at[G1], [RES.at[G0], GV0.at[x, c]])
@@ -919,7 +922,7 @@
     arrive((b1n[0], a1n[0]), EARLY)
     arrive(second1, EARLY)
     arrive(second1, LATE)
-    state1 = [up_out(1, 0, 1)] + [down_out(1, n) for n in HALVES]
+    state1 = [up_out(1, q, 2) for q in HALVES] + [down_out(1, n) for n in HALVES]
     load_a1.wait()
     load_w1d_again.wait()
     r = Reduce8(functools.partial(down_part, GV1), 3, WHOLE, r_keys)
@@ -945,16 +948,15 @@
     relay((b2n[1], a2n[1]))
     arrive((a2n[0],), LATE)
     state0 = [up_out(0, 0, 2)]
-    arrive((b2n[0],), LATE)
-    state0.append(down_out(0, 0))
     arrive((a2n[1], b2n[1]), EARLY)
+    arrive((a2n[1],), LATE)
+    state0.append(up_out(0, 1, 2))
+    for q in HALVES:
+        arrive((b2n[q],), LATE)
+        state0.append(down_out(0, q))
     r.finish(0, RES.at[X1], [RES.at[G1]])
     write_y = lcopy(RES.at[G1], y_out)
     write_y.start()
-    arrive((a2n[1],), LATE)
-    state0.append(up_out(0, 1, 2))
-    arrive((b2n[1],), LATE)
-    state0.append(down_out(0, 1))
     r.drain()
     do(gg0, "drain")
     write_gi.wait()

time: 289 us -> 288 us (level)
  no operation moved by 1% of the time
where the time goes in v7:
time: 288 us; the launch traced here: 287 us
  Pallas kernels  287 us (100%)
    pallas_call x1, Pallas kernels, device_step(): y_raw, gi_raw, gd_raw, *_, gu_raw = call(x_loc, up_loc, down_loc, g_loc)  283 us

profile of v7, /device:TPU:1, one launch (start us, length us, event | category | flops | bytes accessed | tf_op | source)
XLA Modules:
  0.0 287.5 jit_solution(3359102165666984036)
XLA Ops:
  0.6 283.3 %mlp_stack.1 = (bf16[128,2048]{1,0:T(8,128)(2,1)}, bf16[128,2048]{1,0:T(8,128)(2,1)}, f32[2,64,2048]{2,1,0:T(8,128)}, bf16[4,2,128,2048]{3,2,1,0:T(8,128)(2,1)},...) custom-call(bf16[128,2048]{1,0:T(8,128)(2,1)} %x_in.1, ...), custom_call_target="tpu_custom_call" | custom-call | tf_op jit(solution)/shard_map/mlp_stack/pallas_call | solution.py:1042
  284.0 3.3 %write_out.1 = (bf16[128,2048]{1,0:T(8,128)(2,1)}, bf16[128,2048]{1,0:T(8,128)(2,1)}, f32[2,16,8192]{2,1,0:T(8,128)}, f32[2,64,2048]{2,1,0:T(8,128)}) custom-call(bf16[128,2048]{1,0:T(8,128)(2,1)} %get-tuple-element.8.y_in, bf16[128,2048]{1,0:T(8,128)(2,1)} %get-tuple-element.9.gi_in, f32[2,4,32,1024]{3,2,1,0:T(8,128)} %get-tuple-element.10.gu_in, ...), custom_call_target="tpu_custom_call" | custom-call | tf_op jit(solution)/shard_map/write_out/pallas_call | solution.py:1045

commit v8 on v7

--- a/solution.py
+++ b/solution.py
@@ -937,20 +937,27 @@
     second_start((a2n[0], b2n[0]))
     r.relay(0)
     arrive((b1n[1], a1n[1]), EARLY)
-    arrive((b1n[1], a1n[1]), LATE)
-    last = (a2n[1], b2n[1])
-    for red in last:
+
+    def start(red):
         red.opposite()
-    relay((b2n[0], a2n[0]))
-    sides(last, NXT)
-    sides(last, PRV)
-    arrive((b2n[0], a2n[0]), EARLY)
-    relay((b2n[1], a2n[1]))
+        sides((red,), NXT)
+        sides((red,), PRV)
+    arrive((b1n[1],), LATE)
+    relay((a2n[0],))
+    arrive((a1n[1],), LATE)
+    start(a2n[1])
+    start(b2n[1])
+    arrive((a2n[0],), EARLY)
+    relay((b2n[0],))
     arrive((a2n[0],), LATE)
     state0 = [up_out(0, 0, 2)]
-    arrive((a2n[1], b2n[1]), EARLY)
+    relay((a2n[1],))
+    arrive((b2n[0],), EARLY)
+    relay((b2n[1],))
+    arrive((a2n[1],), EARLY)
     arrive((a2n[1],), LATE)
     state0.append(up_out(0, 1, 2))
+    arrive((b2n[1],), EARLY)
     for q in HALVES:
         arrive((b2n[q],), LATE)
         state0.append(down_out(0, q))

time: 288 us -> 287 us (level)
  no operation moved by 1% of the time
where the time goes in v8:
time: 287 us; the launch traced here: 286 us
  Pallas kernels  285 us (99%)
    pallas_call x1, Pallas kernels, device_step(): y_raw, gi_raw, gd_raw, *_, gu_raw = call(x_loc, up_loc, down_loc, g_loc)  282 us

profile of v8, /device:TPU:1, one launch (start us, length us, event | category | flops | bytes accessed | tf_op | source)
XLA Modules:
  0.0 286.2 jit_solution(11606155980327937997)
XLA Ops:
  0.6 282.1 %mlp_stack.1 = (bf16[128,2048]{1,0:T(8,128)(2,1)}, bf16[128,2048]{1,0:T(8,128)(2,1)}, f32[2,64,2048]{2,1,0:T(8,128)}, bf16[4,2,128,2048]{3,2,1,0:T(8,128)(2,1)},...) custom-call(bf16[128,2048]{1,0:T(8,128)(2,1)} %x_in.1, ...), custom_call_target="tpu_custom_call" | custom-call | tf_op jit(solution)/shard_map/mlp_stack/pallas_call | solution.py:1049
  282.8 3.3 %write_out.1 = (bf16[128,2048]{1,0:T(8,128)(2,1)}, bf16[128,2048]{1,0:T(8,128)(2,1)}, f32[2,16,8192]{2,1,0:T(8,128)}, f32[2,64,2048]{2,1,0:T(8,128)}) custom-call(bf16[128,2048]{1,0:T(8,128)(2,1)} %get-tuple-element.8.y_in, bf16[128,2048]{1,0:T(8,128)(2,1)} %get-tuple-element.9.gi_in, f32[2,4,32,1024]{3,2,1,0:T(8,128)} %get-tuple-element.10.gu_in, ...), custom_call_target="tpu_custom_call" | custom-call | tf_op jit(solution)/shard_map/write_out/pallas_call | solution.py:1052

commit v9 on v8

--- a/solution.py
+++ b/solution.py
@@ -20,7 +20,7 @@
 TARGETS = ((NXT, 0), (PRV, 1), (OWN, 1), (OWN, 0), (OWN, 0), (OWN, 1))
 EARLY, LATE = (2, 3), (4, 5)
 PUSHES = {PRV: (0, 2), NXT: (1, 3), OPP: (4, 5)}
-N_RECV, N_SEND, N_LOCAL = 206, 110, 19
+N_RECV, N_SEND, N_LOCAL = 192, 90, 19
 
 
 def gelu_parts(pre_act):
@@ -348,6 +348,7 @@
     do(u0a, "opposite")
     do(u0u[3], "start")
     do(d0a, "finish")
+    do(d0a + u0a, "drain")
     do(u0u[1], "forward")
     do(u0u[2], "forward")
     do(d0b, "start_first")
@@ -356,7 +357,7 @@
         cpy.wait_send()
     own_u1.wait()
     do(u0u[3], "forward")
-    do(u0a + d0a, "drain")
+    do(u0u[0] + u0u[1], "drain")
     do(d0b, "start_rest")
     do(d0c, "start_first")
     gg1.forward()
@@ -528,29 +529,28 @@
             lo = [pl.ds(mo((2 * h + q) * XD + t * ZD, ZD), ZD) for q in HALVES]
             lhs = jnp.concatenate([XV[:, :, :, s].reshape(8 * TB, ZD) for s in lo], axis=1)
 
-            def body(n, carry):
-                cols = pl.ds(mo(n * ND, ND), ND)
-                dst[h, :, :, cols] = dot_tn(lhs, DV[:, :, cols].reshape(8 * TB, ND)).reshape(2, ZD, ND)
-                return carry
-            return loop(K // ND, body, carry) if q is None else body(q, carry)
+            cols, width = (pl.ds(0, K), K) if q is None else (pl.ds(q * ND, ND), ND)
+            dst[h, :, :, cols] = dot_tn(lhs, DV[:, :, cols].reshape(8 * TB, width)).reshape(2, ZD, width)
+            return carry
         if halves is None:
             loop(2, rows, None)
         else:
             for h in halves:
                 rows(h, None)
 
-    def grad_b(gv, j, dst, lo=0, tiles=RING):
+    def grad_b(gv, j, dst, n=None):
         cols_l = pl.ds(mo(off(y, j) * NK, NK), NK)
 
-        def body(i, carry):
-            m = lo + i
-            cols = pl.ds(mo(m * ND, ND), ND)
-            out = dot_tn(AV[:, :, :, cols_l].reshape(8 * TB, NK), gv[:, :, :, cols].reshape(8 * TB, ND))
-            dst[:, m // 2, :, pl.ds(mo(lax.rem(m, 2) * ND, ND), ND)] = out.reshape(2, NK // 2, ND)
+        def body(n, carry):
+            out = dot_tn(AV[:, :, :, cols_l].reshape(8 * TB, NK), gv[:, :, :, pl.ds(mo(n * K, K), K)].reshape(8 * TB, K))
+            dst[:, n] = out.reshape(2, NK // 2, K)
             return carry
-        loop(tiles, body, None)
-
-    grad_keys = [keys_of(sum(u0u, u0a) + d0a), [d.key for d in ex0 + ex1] + keys_of(d0b + d0c)]
+        if n is None:
+            loop(2, body, None)
+        else:
+            body(n, None)
+
+    grad_keys = [keys_of(sum(u0u, u0a) + d0a), [d.key for d in ex0 + ex1 + gg1.own + gg1.push] + keys_of(d0b + d0c + [gg1.ring])]
 
     def grad_key(l):
         return grad_keys[l].pop() if grad_keys[l] else fresh("recv")
@@ -684,7 +684,7 @@
     do(d0d, "start")
     r.combine(OPP, 0)
     r.opposite(0)
-    do(sum(u0u, []), "drain")
+    do(u0u[2] + u0u[3], "drain")
     hidden0(off(x, PRV))
     r.compute(PRV, 0)
     r.side(NXT, 0)
@@ -710,6 +710,7 @@
     gg1.last()
     save_x.wait()
     do(d0d, "finish")
+    do(d0b + d0c, "drain")
     save_d0 = lcopy(W, wdh.at[0])
     save_d0.start()
     r.compute(OPP, 2)
@@ -755,7 +756,7 @@
     gg1.wait_push(range(len(gg1.push)))
     own_g.wait()
     save_d0.wait()
-    do(d0b + d0c + d0d, "drain")
+    do(d0d + u1a, "drain")
     gg1.drain()
     do(d1b, "finish")
     load_w1d = lcopy(wdh.at[1], W)
@@ -800,7 +801,7 @@
 
     (a1, a2), (b1, b2) = zip(*[reduce_a(1, q, 2) for q in HALVES]), zip(*[reduce_b(1, q) for q in HALVES])
     first1, second1 = b1 + a1, b2 + a2
-    grad_b(GV1, OPP, GPB.at[OPP], 0, 2)
+    grad_b(GV1, OPP, GPB.at[OPP], 0)
     b1[0].opposite()
     for n in (PRV, OWN, NXT):
         hidden1_tile(off(x, OPP), off(y, n))
@@ -812,7 +813,7 @@
     load_s0.start()
     save_a1 = lcopy(AV, ah.at[1])
     save_a1.start()
-    grad_b(GV1, OPP, GPB.at[OPP], 2, 2)
+    grad_b(GV1, OPP, GPB.at[OPP], 1)
     b1[1].opposite()
     r = Reduce8(dx_part, 1, SPLIT2, r_keys)
     r.acquire()
@@ -850,7 +851,7 @@
     save_a1.wait()
     load_a0 = lcopy(ah.at[0], AV)
     load_a0.start()
-    do(d1b + u1a, "drain")
+    do(d1b, "drain")
     load_a1 = lcopy(ah.at[1], GV1.at[:, :, :, 0:K])
     load_a1.start()
     r.finish(1, RES.at[G1], [RES.at[G0], GV0.at[x, c]])
@@ -977,17 +978,17 @@
     layers, ur, ff = gu_out.shape
     s2 = ff // 64
     half = s2 // 2
-    loads = [pltpu.make_async_copy(a, b, sems.at[0, k])
-             for k, (a, b) in enumerate(((gu_in, gubuf), (gd_in, gdbuf), (y_in, ybuf), (gi_in, gibuf)))]
-    stores = [pltpu.make_async_copy(a, b, sems.at[1, k])
-              for k, (a, b) in enumerate(((gushuf, gu_out), (gdbuf, gd_out), (ybuf, y_out), (gibuf, gi_out)))]
+    pairs = [((gu_in.at[l], gubuf.at[l]), (gushuf.at[l], gu_out.at[l])) for l in range(layers)]
+    pairs += [((a, b), (b, o)) for a, b, o in ((gd_in, gdbuf, gd_out), (y_in, ybuf, y_out), (gi_in, gibuf, gi_out))]
+    loads = [pltpu.make_async_copy(*p, sems.at[0, k]) for k, (p, _) in enumerate(pairs)]
+    stores = [pltpu.make_async_copy(*p, sems.at[1, k]) for k, (_, p) in enumerate(pairs)]
     for cpy in loads:
         cpy.start()
     low = lax.broadcasted_iota(jnp.int32, (ur, s2), 1) < half
     swap = lambda v: pltpu.roll(v, half, 1)
-    loads[0].wait()
-    for l in range(layers):
-        for b in range(RING):
+    for l, (load, store) in enumerate(zip(loads, stores)):
+        load.wait()
+        for b in range(RING if l < layers else 0):
             for yy in range(RING):
                 for m in HALVES:
                     cols = pl.ds((yy * 2 + m) * s2, s2)
@@ -995,10 +996,7 @@
                     strip = (b * RING + 2 * m) * RING + yy
                     gushuf[l, :, pl.ds(strip * s2, s2)] = jnp.where(low, t0, swap(t1))
                     gushuf[l, :, pl.ds((strip + RING) * s2, s2)] = jnp.where(low, swap(t0), t1)
-    stores[0].start()
-    for k in range(1, len(loads)):
-        loads[k].wait()
-        stores[k].start()
+        store.start()
     for cpy in stores:
         cpy.wait()
 
@@ -1051,7 +1049,7 @@
         outs = [hbm((tb, dm), BF16), hbm((tb, dm), BF16), hbm((layers, ur, ff), F32), hbm((layers, dr, dm), F32)]
         return tuple(pl.pallas_call(
             finish_kernel, out_shape=outs, in_specs=[anyspec] * len(outs), out_specs=[anyspec] * len(outs),
-            scratch_shapes=[vm(v.shape, v.dtype) for v in raws] + [vm(outs[2].shape, F32), pltpu.SemaphoreType.DMA((2, len(outs)))],
+            scratch_shapes=[vm(v.shape, v.dtype) for v in raws] + [vm(outs[2].shape, F32), pltpu.SemaphoreType.DMA((2, layers + len(outs)))],
             name="write_out")(*raws))
 
     return jax.shard_map(device_step, mesh=fine, in_specs=(tok_spec, weight_spec, weight_spec, tok_spec),

time: 287 us -> 286 us (level)
  no operation moved by 1% of the time
where the time goes in v9:
time: 286 us; the launch traced here: 285 us
  Pallas kernels  285 us (100%)
    pallas_call x1, Pallas kernels, device_step(): y_raw, gi_raw, gd_raw, *_, gu_raw = call(x_loc, up_loc, down_loc, g_loc)  281 us

profile of v9, /device:TPU:1, one launch (start us, length us, event | category | flops | bytes accessed | tf_op | source)
XLA Modules:
  0.0 285.3 jit_solution(14927412040610585958)
XLA Ops:
  0.6 281.5 %mlp_stack.1 = (bf16[128,2048]{1,0:T(8,128)(2,1)}, bf16[128,2048]{1,0:T(8,128)(2,1)}, f32[2,64,2048]{2,1,0:T(8,128)}, bf16[4,2,128,2048]{3,2,1,0:T(8,128)(2,1)},...) custom-call(bf16[128,2048]{1,0:T(8,128)(2,1)} %x_in.1, ...), custom_call_target="tpu_custom_call" | custom-call | tf_op jit(solution)/shard_map/mlp_stack/pallas_call | solution.py:1047
  282.1 3.0 %write_out.1 = (bf16[128,2048]{1,0:T(8,128)(2,1)}, bf16[128,2048]{1,0:T(8,128)(2,1)}, f32[2,16,8192]{2,1,0:T(8,128)}, f32[2,64,2048]{2,1,0:T(8,128)}) custom-call(bf16[128,2048]{1,0:T(8,128)(2,1)} %get-tuple-element.8.y_in, bf16[128,2048]{1,0:T(8,128)(2,1)} %get-tuple-element.9.gi_in, f32[2,4,32,1024]{3,2,1,0:T(8,128)} %get-tuple-element.10.gu_in, ...), custom_call_target="tpu_custom_call" | custom-call | tf_op jit(solution)/shard_map/write_out/pallas_call | solution.py:1050

commit v10 on v9

--- a/solution.py
+++ b/solution.py
@@ -538,6 +538,14 @@
             for h in halves:
                 rows(h, None)
 
+    def grad_b_first(chips, add):
+        cols_l, cols = pl.ds(mo(off(y, OPP) * NK, NK), NK), pl.ds(0, K)
+        dst = GPB.at[OPP]
+        for t in chips:
+            out = dot_tn(AV[t, :, :, cols_l].reshape(T2, NK), GV1[t, :, :, cols].reshape(T2, K)).reshape(2, NK // 2, K)
+            dst[:, 0] = dst[:, 0] + out if add else out
+            add = True
+
     def grad_b(gv, j, dst, n=None):
         cols_l = pl.ds(mo(off(y, j) * NK, NK), NK)
 
@@ -795,13 +803,14 @@
     hidden1(off(x, PRV), 1)
     gx1[1].last()
     hidden1(off(x, NXT), 1)
+    grad_b_first([off(x, j) for j in (OWN, PRV, NXT)], False)
     for g in gx1:
         g.wait_push(PUSHES[OPP])
     hidden1_tile(off(x, OPP), off(y, OPP))
 
     (a1, a2), (b1, b2) = zip(*[reduce_a(1, q, 2) for q in HALVES]), zip(*[reduce_b(1, q) for q in HALVES])
     first1, second1 = b1 + a1, b2 + a2
-    grad_b(GV1, OPP, GPB.at[OPP], 0)
+    grad_b_first([off(x, OPP)], True)
     b1[0].opposite()
     for n in (PRV, OWN, NXT):
         hidden1_tile(off(x, OPP), off(y, n))

time: 286 us -> 286 us (level)
  no operation moved by 1% of the time
where the time goes in v10:
time: 286 us; the launch traced here: 285 us
  Pallas kernels  284 us (99%)
    pallas_call x1, Pallas kernels, device_step(): y_raw, gi_raw, gd_raw, *_, gu_raw = call(x_loc, up_loc, down_loc, g_loc)  281 us

profile of v10, /device:TPU:1, one launch (start us, length us, event | category | flops | bytes accessed | tf_op | source)
XLA Modules:
  0.0 285.2 jit_solution(4050687430337841789)
XLA Ops:
  0.6 281.3 %mlp_stack.1 = (bf16[128,2048]{1,0:T(8,128)(2,1)}, bf16[128,2048]{1,0:T(8,128)(2,1)}, f32[2,64,2048]{2,1,0:T(8,128)}, bf16[4,2,128,2048]{3,2,1,0:T(8,128)(2,1)},...) custom-call(bf16[128,2048]{1,0:T(8,128)(2,1)} %x_in.1, ...), custom_call_target="tpu_custom_call" | custom-call | tf_op jit(solution)/shard_map/mlp_stack/pallas_call | solution.py:1056
  282.0 3.0 %write_out.1 = (bf16[128,2048]{1,0:T(8,128)(2,1)}, bf16[128,2048]{1,0:T(8,128)(2,1)}, f32[2,16,8192]{2,1,0:T(8,128)}, f32[2,64,2048]{2,1,0:T(8,128)}) custom-call(bf16[128,2048]{1,0:T(8,128)(2,1)} %get-tuple-element.8.y_in, bf16[128,2048]{1,0:T(8,128)(2,1)} %get-tuple-element.9.gi_in, f32[2,4,32,1024]{3,2,1,0:T(8,128)} %get-tuple-element.10.gu_in, ...), custom_call_target="tpu_custom_call" | custom-call | tf_op jit(solution)/shard_map/write_out/pallas_call | solution.py:1059

commit v11 on v10

--- a/solution.py
+++ b/solution.py
@@ -20,7 +20,7 @@
 TARGETS = ((NXT, 0), (PRV, 1), (OWN, 1), (OWN, 0), (OWN, 0), (OWN, 1))
 EARLY, LATE = (2, 3), (4, 5)
 PUSHES = {PRV: (0, 2), NXT: (1, 3), OPP: (4, 5)}
-N_RECV, N_SEND, N_LOCAL = 192, 90, 19
+N_RECV, N_SEND, N_LOCAL = 192, 102, 19
 
 
 def gelu_parts(pre_act):
@@ -360,17 +360,16 @@
     do(u0u[0] + u0u[1], "drain")
     do(d0b, "start_rest")
     do(d0c, "start_first")
-    gg1.forward()
     do(d0b, "forward")
     do(d0c, "start_rest")
     do(d1a, "start")
+    gg1.forward()
     gx0.last()
     gx0.wait_own()
     gx0.wait_push(range(len(gx0.push)))
     own_x.wait()
     save_x = lcopy(XV, xh0)
     save_x.start()
-    gx0.drain()
     for unit in u0u:
         do(unit, "finish")
     save_u0 = lcopy(U, wuh.at[0])
@@ -717,6 +716,7 @@
     do(d1b, "start")
     gg1.last()
     save_x.wait()
+    gx0.drain()
     do(d0d, "finish")
     do(d0b + d0c, "drain")
     save_d0 = lcopy(W, wdh.at[0])
@@ -812,9 +812,8 @@
     first1, second1 = b1 + a1, b2 + a2
     grad_b_first([off(x, OPP)], True)
     b1[0].opposite()
-    for n in (PRV, OWN, NXT):
-        hidden1_tile(off(x, OPP), off(y, n))
     for q in HALVES:
+        hidden1(off(x, OPP), q)
         for h in HALVES:
             grad_a(OPP, GPA.at[OPP], (h,), q)
             a1[q].m[h].start()

time: 286 us -> 285 us (level)
  no operation moved by 1% of the time
where the time goes in v11:
time: 285 us
  Pallas kernels  284 us (100%)
    pallas_call x1, Pallas kernels, device_step(): y_raw, gi_raw, gd_raw, *_, gu_raw = call(x_loc, up_loc, down_loc, g_loc)  281 us

profile of v11, /device:TPU:1, one launch (start us, length us, event | category | flops | bytes accessed | tf_op | source)
XLA Modules:
  0.0 284.8 jit_solution(12805729177149190876)
XLA Ops:
  0.6 281.0 %mlp_stack.1 = (bf16[128,2048]{1,0:T(8,128)(2,1)}, bf16[128,2048]{1,0:T(8,128)(2,1)}, f32[2,64,2048]{2,1,0:T(8,128)}, bf16[4,2,128,2048]{3,2,1,0:T(8,128)(2,1)},...) custom-call(bf16[128,2048]{1,0:T(8,128)(2,1)} %x_in.1, ...), custom_call_target="tpu_custom_call" | custom-call | tf_op jit(solution)/shard_map/mlp_stack/pallas_call | solution.py:1055
  281.6 3.0 %write_out.1 = (bf16[128,2048]{1,0:T(8,128)(2,1)}, bf16[128,2048]{1,0:T(8,128)(2,1)}, f32[2,16,8192]{2,1,0:T(8,128)}, f32[2,64,2048]{2,1,0:T(8,128)}) custom-call(bf16[128,2048]{1,0:T(8,128)(2,1)} %get-tuple-element.8.y_in, bf16[128,2048]{1,0:T(8,128)(2,1)} %get-tuple-element.9.gi_in, f32[2,4,32,1024]{3,2,1,0:T(8,128)} %get-tuple-element.10.gu_in, ...), custom_call_target="tpu_custom_call" | custom-call | tf_op jit(solution)/shard_map/write_out/pallas_call | solution.py:1058

commit v12 on v11

--- a/solution.py
+++ b/solution.py
@@ -20,7 +20,7 @@
 TARGETS = ((NXT, 0), (PRV, 1), (OWN, 1), (OWN, 0), (OWN, 0), (OWN, 1))
 EARLY, LATE = (2, 3), (4, 5)
 PUSHES = {PRV: (0, 2), NXT: (1, 3), OPP: (4, 5)}
-N_RECV, N_SEND, N_LOCAL = 192, 102, 19
+N_RECV, N_SEND, N_LOCAL = 192, 90, 19
 
 
 def gelu_parts(pre_act):
@@ -698,6 +698,7 @@
     do(d1a, "forward")
     hidden0(off(x, OWN))
     r.side(PRV, 0)
+    gx0.drain()
     save_s = lcopy(SV, sh0)
     save_s.start()
     save_a0 = lcopy(AV, ah.at[0])
@@ -716,7 +717,6 @@
     do(d1b, "start")
     gg1.last()
     save_x.wait()
-    gx0.drain()
     do(d0d, "finish")
     do(d0b + d0c, "drain")
     save_d0 = lcopy(W, wdh.at[0])

time: 285 us -> 285 us (level)
  no operation moved by 1% of the time
where the time goes in v12:
time: 285 us
  Pallas kernels  284 us (100%)
    pallas_call x1, Pallas kernels, device_step(): y_raw, gi_raw, gd_raw, *_, gu_raw = call(x_loc, up_loc, down_loc, g_loc)  281 us

profile of v12, /device:TPU:1, one launch (start us, length us, event | category | flops | bytes accessed | tf_op | source)
XLA Modules:
  0.0 284.7 jit_solution(15037102838104064796)
XLA Ops:
  0.6 280.9 %mlp_stack.1 = (bf16[128,2048]{1,0:T(8,128)(2,1)}, bf16[128,2048]{1,0:T(8,128)(2,1)}, f32[2,64,2048]{2,1,0:T(8,128)}, bf16[4,2,128,2048]{3,2,1,0:T(8,128)(2,1)},...) custom-call(bf16[128,2048]{1,0:T(8,128)(2,1)} %x_in.1, ...), custom_call_target="tpu_custom_call" | custom-call | tf_op jit(solution)/shard_map/mlp_stack/pallas_call | solution.py:1055
  281.5 3.0 %write_out.1 = (bf16[128,2048]{1,0:T(8,128)(2,1)}, bf16[128,2048]{1,0:T(8,128)(2,1)}, f32[2,16,8192]{2,1,0:T(8,128)}, f32[2,64,2048]{2,1,0:T(8,128)}) custom-call(bf16[128,2048]{1,0:T(8,128)(2,1)} %get-tuple-element.8.y_in, bf16[128,2048]{1,0:T(8,128)(2,1)} %get-tuple-element.9.gi_in, f32[2,4,32,1024]{3,2,1,0:T(8,128)} %get-tuple-element.10.gu_in, ...), custom_call_target="tpu_custom_call" | custom-call | tf_op jit(solution)/shard_map/write_out/pallas_call | solution.py:1058
